TPU v7x, 128 devices: a whole 4x4x4 slice. The times are simulated.
128 devices in a mesh: gx: 4 (over y), gy: 8 (over x, core), gz: 4 (over z).
Axes of the slice: x: 4, y: 4, z: 4, core: 2. Of those that a mesh axis runs over, the one named last changes fastest.
Arguments:
- rhs: float32 [8, 64, 256, 512], P(None, 'gx', 'gy', 'gz'), may hold values from -8 to 8
- stencil: float32 [14, 64, 256, 512], P(None, 'gx', 'gy', 'gz'), may hold values from 0.02 to 1
Outputs:
- solution: float32 [8, 64, 256, 512], P(None, 'gx', 'gy', 'gz')
- residual: float32 [8, 64, 256, 512], P(None, 'gx', 'gy', 'gz')
All inputs are finite; a program needn't handle non-finite values.
Results may differ from a plain program's by a relative error of at most 0.00029.
Values sent between devices are 32-bit elements; how exact they have to be, the bound alone decides.
No kernel may reach another device: no remote copies, remote signals or barrier semaphores. Data moves between devices by JAX's collectives and lax.ppermute only.
A program may use at most 128 MiB of HBM per device.

v0:
```python
import jax
import jax.numpy as jnp
from jax import lax
from jax.sharding import Mesh
from jax.sharding import PartitionSpec as P

ITERS = 2
GX_GY_GZ = ("gx", "gy_0", "gy_1", "gz")
GY = ("gy_0", "gy_1")


FORWARD = [
    (a, b, c) for a in (-1, 0, 1) for b in (-1, 0, 1) for c in (-1, 0, 1) if (a, b, c) > (0, 0, 0)
]


def over_axes(x, axes):
    for axis in axes:
        x = lax.psum(x, axis)
    return x


def with_halo(cells, sides, width):
    for axis, dim in sides:
        count = lax.axis_size(axis)
        ends = count - 1
        head = lax.slice_in_dim(cells, 0, width, axis=dim)
        tail = lax.slice_in_dim(cells, cells.shape[dim] - width, cells.shape[dim], axis=dim)
        cells = jnp.concatenate(
            [
                lax.ppermute(tail, axis, [(i, (i + 1) % count) for i in range(ends)]),
                cells,
                lax.ppermute(head, axis, [((i + 1) % count, i) for i in range(ends)]),
            ],
            axis=dim,
        )
    return cells


def window(array, margin, depth, offset):
    result = array
    for place in range(3):
        dim = array.ndim - 3 + place
        inner = array.shape[dim] - 2 * margin
        begin = margin - depth + offset[place]
        result = lax.slice_in_dim(result, begin, begin + inner + 2 * depth, axis=dim)
    return result


def diagonal_field(padded, margin, depth):
    total = window(padded[0], margin, depth, (0, 0, 0))
    total = total + jnp.sum(window(padded[1:], margin, depth, (0, 0, 0)), axis=0)
    for index, offset in enumerate(FORWARD):
        back = (-offset[0], -offset[1], -offset[2])
        total = total + window(padded[index + 1], margin, depth, back)
    return total


def operate(field, fmargin, padded, smargin, diag, depth):
    result = diag[None] * window(field, fmargin, depth, (0, 0, 0))
    for index, offset in enumerate(FORWARD):
        back = (-offset[0], -offset[1], -offset[2])
        ahead_w = window(padded[index + 1], smargin, depth, (0, 0, 0))
        behind_w = window(padded[index + 1], smargin, depth, back)
        result = result - ahead_w[None] * window(field, fmargin, depth, offset)
        result = result - behind_w[None] * window(field, fmargin, depth, back)
    return result


def gram(left, right):
    flat_l = left.reshape(left.shape[0], -1)
    flat_r = right.reshape(right.shape[0], -1)
    return lax.dot_general(
        flat_l,
        flat_r,
        (((1,), (1,)), ((), ())),
        precision=lax.Precision.HIGHEST,
        preferred_element_type=jnp.float32,
    )


def combine(coef, field):
    return jnp.einsum("ij,ixyz->jxyz", coef, field, precision=lax.Precision.HIGHEST)


def small_dot(left, right):
    return jnp.dot(left, right, precision=lax.Precision.HIGHEST)


def solve_spd(matrix, right):
    factor = jnp.linalg.cholesky(matrix)
    return jax.scipy.linalg.cho_solve((factor, True), right)


def joint_sum(residual, direction, image):
    parts = (
        gram(residual, residual),
        gram(direction, image),
        gram(image, residual),
        gram(image, image),
    )
    return (
        over_axes(parts[0], GX_GY_GZ),
        over_axes(parts[1], GX_GY_GZ),
        over_axes(parts[2], GX_GY_GZ),
        over_axes(parts[3], GX_GY_GZ),
    )


def shards(rhs, stencil):
    padded = with_halo(stencil, (("gx", 1), (GY, 2), ("gz", 3)), 1)
    smargin = 1
    diag_full = diagonal_field(padded, 1, 0)
    direction = rhs
    dmargin = 0
    residual = direction
    rmargin = dmargin
    solution = jnp.zeros_like(rhs)
    norm_now = None
    for step in range(ITERS):
        field = with_halo(direction, (("gx", 1), (GY, 2), ("gz", 3)), 1)
        fmargin = 1
        depth = 0
        image = operate(field, fmargin, padded, smargin, diag_full, depth)
        dir_here = window(field, fmargin, depth, (0, 0, 0))
        res_here = window(residual, rmargin, depth, (0, 0, 0))
        dir_core = window(dir_here, depth, 0, (0, 0, 0))
        res_core = window(res_here, depth, 0, (0, 0, 0))
        img_core = window(image, depth, 0, (0, 0, 0))
        norm_now, curve, cross, square = joint_sum(res_core, dir_core, img_core)
        alpha = solve_spd(curve, norm_now)
        solution = solution + combine(alpha, dir_core)
        res_here = res_here - combine(alpha, image)
        if step + 1 < ITERS:
            norm_next = (
                norm_now
                - small_dot(alpha.T, cross)
                - small_dot(cross.T, alpha)
                + small_dot(alpha.T, small_dot(square, alpha))
            )
            beta = solve_spd(norm_now, norm_next)
            direction = res_here + combine(beta, dir_here)
            norm_now = norm_next
        residual = res_here
        rmargin = depth
    return (solution, window(residual, rmargin, 0, (0, 0, 0)))


def solution(mesh):
    split = Mesh(
        mesh.devices.reshape(mesh.shape["gx"], 4, 2, mesh.shape["gz"]), ("gx", "gy_0", "gy_1", "gz")
    )
    placed = (P(None, "gx", GY, "gz"), P(None, "gx", GY, "gz"))
    return jax.shard_map(
        shards,
        mesh=split,
        in_specs=placed,
        out_specs=(P(None, "gx", GY, "gz"), P(None, "gx", GY, "gz")),
        check_vma=False,
    )
```

profile of v0, /device:TPU:0, one launch (start us, length us, event | category | flops | bytes accessed | tf_op | source)
XLA Modules:
  0.0 389.5 jit_solution(6726327322583336218)
XLA Ops:
  17.3 6.5 %collective-permute-done.7 = f32[8,1,32,128]{3,0,2,1:T(8,128)S(1)} collective-permute-done((f32[8,1,32,128]{3,0,2,1:T(8,128)S(1)}, f32[8,1,32,128]{3,0,2,1:T(8,128)S(1)}, u32[]{:S(2)}, u32[]{:S(2)}) %collective-permute-start.7) | collective-permute-done | bytes 131104 | tf_op jit(solution)/shard_map/ppermute | solution.py:33
  40.0 4.5 %collective-permute-start.11 = (f32[8,18,34,1]{2,0,3,1:T(8,128)S(1)}, f32[8,18,34,1]{2,0,3,1:T(8,128)S(1)}, u32[]{:S(2)}, u32[]{:S(2)}) collective-permute-start(f32[8,18,34,1]{2,0,3,1:T(8,128)S(1)} %copy.176), channel_id=1, source_target_pairs={{0,1},{1,2},{2,3},{4,5},{5,6},{6,7},{8,9},{9,10},{10,11},{12,13},{... | collective-permute-start | bytes 58760 | tf_op jit(solution)/shard_map/ppermute | solution.py:31
  49.3 4.5 %collective-permute-start.2 = (f32[14,18,1,128]{3,0,2,1:T(8,128)S(1)}, f32[14,18,1,128]{3,0,2,1:T(8,128)S(1)}, u32[]{:S(2)}, u32[]{:S(2)}) collective-permute-start(f32[14,18,1,128]{3,0,2,1:T(8,128)S(1)} %copy.160), channel_id=1, source_target_pairs={{0,4},{4,8},{8,12},{12,16},{16,20},{20,24},{24,28},{1,5},{5,9},{9,... | collective-permute-start | bytes 387080 | tf_op jit(solution)/shard_map/ppermute | solution.py:31
  55.5 5.5 %convolution_bitcast_fusion.5 = f32[8,8]{0,1:T(8,128)} fusion(f32[8,16,32,128]{3,2,1,0:T(8,128)S(1)} %copy-done), kind=kOutput, calls=%fused_computation.145 | convolution fusion | flops 50331648 | bytes 2097408 | tf_op jit(solution)/shard_map/dot_general | solution.py:73
  69.3 5.6 %fusion.103 = (f32[14,18,34,1]{3,2,1,0:T(8,128)}, f32[14,18,34,1]{3,2,1,0:T(8,128)}) fusion(f32[14,18,34,128]{3,2,1,0:T(8,128)S(1)} %pad_maximum_fusion.1), kind=kLoop, calls=%fused_computation.230 | loop fusion | bytes 137088 | tf_op jit(solution)/shard_map/slice | solution.py:28
  88.4 7.9 %pad_maximum_fusion.2 = (f32[8,18,34,129]{3,0,2,1:T(8,128)}, f32[8,18,34,129]{3,0,2,1:T(8,128)}) fusion(f32[8,18,34,1]{3,0,2,1:T(8,128)} %copy.175, f32[8,18,1,128]{3,0,2,1:T(8,128)S(1)} %collective-permute-done.9, f32[8,18,32,128]{3,0,2,1:T(8,128)} %copy-done.4, f32[8,18,1,128]{3,0,2,1:T(8,128)S(1)} %collective-permute-done.8, f32[8,18,34,1]{3,0,2,1:T(8,128)} %copy.177), kind=kLoop, calls=%fused_computation.2 | loop fusion | flops 3789504 | bytes 7598592 | tf_op jit(solution)/shard_map/concatenate | solution.py:29
  103.4 13.4 %pad_maximum_fusion = f32[14,18,34,130]{3,2,1,0:T(8,128)} fusion(f32[14,18,34,1]{3,2,1,0:T(8,128)} %copy.167, f32[14,18,1,128]{3,2,1,0:T(1,128)S(1)} %copy.163, f32[14,18,32,128]{3,2,1,0:T(8,128)} %copy-done.5, f32[14,18,1,128]{3,2,1,0:T(1,128)S(1)} %copy.162, f32[14,18,34,1]{3,2,1,0:T(8,128)} %copy.166), kind=kLoop, calls=%fused_computation | loop fusion | flops 4455360 | bytes 8910720 | tf_op jit(solution)/shard_map/concatenate | solution.py:29
  116.8 8.0 %slice_bitcast_fusion.13 = (f32[16,34,130]{2,1,0:T(8,128)}, f32[1,16,34,130]{3,2,1,0:T(8,128)S(1)}, f32[1,16,34,130]{3,2,1,0:T(8,128)S(1)}, f32[1,16,34,130]{3,2...) fusion(f32[14,18,34,130]{3,2,1,0:T(8,128)} %pad_maximum_fusion), kind=kLoop, calls=%fused_computation.159 | loop fusion | bytes 10749440 | tf_op jit(solution)/shard_map/slice | solution.py:46
  147.4 31.3 %fusion.17 = f32[8,16,32,128]{3,0,2,1:T(8,128)} fusion(f32[8,18,32,128]{3,0,2,1:T(8,128)} %copy-done.4, f32[8,18,1,128]{3,0,2,1:T(8,128)S(1)} %collective-permute-done.8, f32[8,18,1,128]{3,0,2,1:T(8,128)S(1)} %collective-permute-done.9, f32[8,18,34,129]{3,0,2,1:T(8,128)} %get-tuple-element.70, f32[8,18,34,129]{3,0,2,1:T(8,128)} %get-tuple-element.69, ...), kind=kLoop, calls=%fused_computation.36 | loop fusion | flops 31981568 | bytes 51789824 | tf_op jit(solution)/shard_map/sub | solution.py:66
  178.7 6.7 %fusion.100 = f32[8,8,1,1]{1,0,3,2:T(8,128)S(1)} fusion(f32[8,16,32,128]{3,0,2,1:T(8,128)} %fusion.17, f32[8,16,32,128]{3,2,1,0:T(8,128)S(1)} %copy-done), kind=kOutput, calls=%fused_computation.227 | convolution fusion | flops 50331648 | bytes 4194560 | tf_op jit(solution)/shard_map/dot_general | solution.py:73
  185.5 4.7 %convolution_bitcast_fusion.4 = f32[8,8]{1,0:T(8,128)S(1)} fusion(f32[8,16,32,128]{3,0,2,1:T(8,128)S(1)} %copy-done.2), kind=kOutput, calls=%fused_computation.142 | convolution fusion | flops 50331648 | bytes 2097408 | tf_op jit(solution)/shard_map/dot_general | solution.py:73
  190.2 15.4 %all-reduce.5 = (f32[8,8]{0,1:T(8,128)S(1)}, f32[8,8]{0,1:T(8,128)S(1)}, f32[8,8]{1,0:T(8,128)S(1)}, f32[8,8]{1,0:T(8,128)S(1)}) all-reduce(f32[8,8]{0,1:T(8,128)S(1)} %copy-done.26, f32[8,8]{0,1:T(8,128)S(1)} %bitcast.147, f32[8,8]{1,0:T(8,128)S(1)} %bitcast.148, ...), channel_id=1, replica_groups=mesh['gx'=4,'gy_0'=4,'gy_1'=2,'gz'=4] {'gx'}, use_global_device_ids=true, to_apply=%region_7.9 | all-reduce | flops 256 | bytes 2048 | tf_op jit(solution)/shard_map/psum | solution.py:19
  205.5 17.9 %all-reduce.3 = (f32[8,8]{0,1:T(8,128)S(1)}, f32[8,8]{0,1:T(8,128)S(1)}, f32[8,8]{1,0:T(8,128)S(1)}, f32[8,8]{1,0:T(8,128)S(1)}) all-reduce(f32[8,8]{0,1:T(8,128)S(1)} %get-tuple-element.26, f32[8,8]{0,1:T(8,128)S(1)} %get-tuple-element.27, ...), channel_id=1, replica_groups=mesh['gx'=4,'gy_0'=4,'gy_1'=2,'gz'=4] {'gy_0'}, use_global_device_ids=true, to_apply=%region_8.10 | all-reduce | flops 256 | bytes 2048 | tf_op jit(solution)/shard_map/psum | solution.py:19
  226.7 17.7 %all-reduce.1 = (f32[8,8]{0,1:T(8,128)S(1)}, f32[8,8]{0,1:T(8,128)S(1)}, f32[8,8]{1,0:T(8,128)S(1)}, f32[8,8]{1,0:T(8,128)S(1)}) all-reduce(f32[8,8]{0,1:T(8,128)S(1)} %get-tuple-element.32, f32[8,8]{0,1:T(8,128)S(1)} %get-tuple-element.33, ...), channel_id=1, replica_groups=mesh['gx'=4,'gy_0'=4,'gy_1'=2,'gz'=4] {'gz'}, use_global_device_ids=true, to_apply=%region_10.12 | all-reduce | flops 256 | bytes 2048 | tf_op jit(solution)/shard_map/psum | solution.py:19
  250.2 4.7 %convolution_subtract_fusion.1 = f32[8,16,32,128]{3,0,2,1:T(8,128)S(1)} fusion(f32[8,16,32,128]{3,0,2,1:T(8,128)} %fusion.17, f32[8,8]{1,0:T(8,128)S(1)} %fusion.90, f32[8,16,32,128]{3,2,1,0:T(8,128)S(1)} %copy-done), kind=kOutput, calls=%fused_computation.136 | convolution fusion | flops 50855936 | bytes 6291712 | tf_op jit(solution)/shard_map/ij,ixyz->jxyz/dot_general | solution.py:83
  261.8 4.2 %fusion.95 = f32[8,16,32,128]{3,0,2,1:T(8,128)} fusion(f32[8,8]{1,0:T(8,128)S(1)} %fusion.90, f32[8,16,32,128]{3,2,1,0:T(8,128)S(1)} %copy-done.1), kind=kOutput, calls=%fused_computation.213 | convolution fusion | flops 50331648 | bytes 4194560 | tf_op jit(solution)/shard_map/ij,ixyz->jxyz/dot_general | solution.py:83
  270.4 5.3 %convolution_bitcast_fusion.1 = f32[8,8]{1,0:T(8,128)} fusion(f32[8,16,32,128]{3,0,2,1:T(8,128)S(1)} %convolution_subtract_fusion.1), kind=kOutput, calls=%fused_computation.138 | convolution fusion | flops 50331648 | bytes 2097408 | tf_op jit(solution)/shard_map/dot_general | solution.py:73
  287.1 5.2 %collective-permute-start.17 = (f32[8,18,34,1]{2,0,3,1:T(8,128)}, f32[8,18,34,1]{2,0,3,1:T(8,128)}, u32[]{:S(2)}, u32[]{:S(2)}) collective-permute-start(f32[8,18,34,1]{2,0,3,1:T(8,128)} %copy.217), channel_id=1, source_target_pairs={{0,1},{1,2},{2,3},{4,5},{5,6},{6,7},{8,9},{9,10},{10,11},{12,13},{... | collective-permute-start | bytes 58760 | tf_op jit(solution)/shard_map/ppermute | solution.py:31
  301.6 7.9 %pad_maximum_fusion.3 = (f32[8,18,34,129]{3,0,2,1:T(8,128)}, f32[8,18,34,129]{3,0,2,1:T(8,128)}) fusion(f32[8,18,34,1]{3,0,2,1:T(8,128)} %copy.216, f32[8,18,1,128]{3,0,2,1:T(8,128)S(1)} %collective-permute-done.15, f32[8,1,32,128]{3,0,2,1:T(8,128)S(1)} %collective-permute-done.13, f32[8,16,32,128]{3,0,2,1:T(8,128)S(1)} %convolution_add_fusion.1, ...), kind=kLoop, calls=%fused_computation.4 | loop fusion | flops 6315840 | bytes 7598592 | tf_op jit(solution)/shard_map/concatenate | solution.py:29
  309.5 29.6 %fusion.30 = f32[8,16,32,128]{3,0,2,1:T(8,128)} fusion(f32[8,18,34,129]{3,0,2,1:T(8,128)} %get-tuple-element.66, f32[8,18,34,129]{3,0,2,1:T(8,128)} %get-tuple-element.65, f32[8,18,33,128]{3,0,2,1:T(8,128)} %get-tuple-element.74, f32[8,18,33,128]{3,0,2,1:T(8,128)} %get-tuple-element.73, f32[8,16,32,128]{3,0,2,1:T(8,128)S(1)} %convolution_add_fusion.1, ...), kind=kLoop, calls=%fused_computation.50 | loop fusion | flops 28835840 | bytes 61865984 | tf_op jit(solution)/shard_map/sub | solution.py:66
  339.1 6.2 %convolution_bitcast_fusion.2 = f32[8,8]{0,1:T(8,128)S(1)} fusion(f32[8,16,32,128]{3,0,2,1:T(8,128)S(1)} %convolution_add_fusion.1, f32[8,16,32,128]{3,0,2,1:T(8,128)} %fusion.30), kind=kOutput, calls=%fused_computation.139 | convolution fusion | flops 50331648 | bytes 4194560 | tf_op jit(solution)/shard_map/dot_general | solution.py:73
  345.3 9.7 %all-reduce.4 = (f32[8,8]{1,0:T(8,128)S(1)}, f32[8,8]{0,1:T(8,128)S(1)}) all-reduce(f32[8,8]{1,0:T(8,128)S(1)} %copy-done.25, f32[8,8]{0,1:T(8,128)S(1)} %convolution_bitcast_fusion.2), channel_id=1, replica_groups=mesh['gx'=4,'gy_0'=4,'gy_1'=2,'gz'=4] {'gx'}, use_global_device_ids=true, to_apply=%region_23.0 | all-reduce | flops 128 | bytes 1024 | tf_op jit(solution)/shard_map/psum | solution.py:19
  355.0 10.6 %all-reduce.2 = (f32[8,8]{1,0:T(8,128)S(1)}, f32[8,8]{0,1:T(8,128)S(1)}) all-reduce(f32[8,8]{1,0:T(8,128)S(1)} %get-tuple-element.24, f32[8,8]{0,1:T(8,128)S(1)} %get-tuple-element.25), channel_id=1, replica_groups=mesh['gx'=4,'gy_0'=4,'gy_1'=2,'gz'=4] {'gy_0'}, use_global_device_ids=true, to_apply=%region_24.0 | all-reduce | flops 128 | bytes 1024 | tf_op jit(solution)/shard_map/psum | solution.py:19
  368.1 8.0 %all-reduce = (f32[8,8]{1,0:T(8,128)S(1)}, f32[8,8]{0,1:T(8,128)S(1)}) all-reduce(f32[8,8]{1,0:T(8,128)S(1)} %get-tuple-element.30, f32[8,8]{0,1:T(8,128)S(1)} %get-tuple-element.31), channel_id=1, replica_groups=mesh['gx'=4,'gy_0'=4,'gy_1'=2,'gz'=4] {'gz'}, use_global_device_ids=true, to_apply=%region_26.29 | all-reduce | flops 128 | bytes 1024 | tf_op jit(solution)/shard_map/psum | solution.py:19
  (195 shorter events, 146.9 us)
Async XLA Ops:
  0.6 14.9 %copy-start = (f32[8,16,32,128]{3,2,1,0:T(8,128)S(1)}, f32[8,16,32,128]{3,2,1,0:T(8,128)}, u32[]{:S(2)}) copy-start(f32[8,16,32,128]{3,2,1,0:T(8,128)} %param.5) | copy-start | bytes 6291460
  4.0 10.8 %copy-start.7 = (f32[8,16,32,128]{3,0,2,1:T(8,128)}, f32[8,16,32,128]{3,0,2,1:T(8,128)S(1)}, u32[]{:S(2)}) copy-start(f32[8,16,32,128]{3,0,2,1:T(8,128)S(1)} %copy.170) | copy-start | bytes 6291460
  4.1 10.8 %collective-permute-start.6 = (f32[8,1,32,128]{3,0,2,1:T(8,128)S(1)}, f32[8,1,32,128]{3,0,2,1:T(8,128)S(1)}, u32[]{:S(2)}, u32[]{:S(2)}) collective-permute-start(f32[8,1,32,128]{3,0,2,1:T(8,128)S(1)} %get-tuple-element.82), channel_id=1, source_target_pairs={{0,32},{32,64},{64,96},{1,33},{33,65},{65,97},{2,34},{34,66},{66,9... | collective-permute-start | bytes 393224 | tf_op jit(solution)/shard_map/ppermute | solution.py:31
  8.8 35.8 %collective-permute-start = (f32[14,1,32,128]{3,2,1,0:T(8,128)S(1)}, f32[14,1,32,128]{3,2,1,0:T(8,128)S(1)}, u32[]{:S(2)}, u32[]{:S(2)}) collective-permute-start(f32[14,1,32,128]{3,2,1,0:T(8,128)S(1)} %get-tuple-element.64), channel_id=1, source_target_pairs={{0,32},{32,64},{64,96},{1,33},{33,65},{65,97},{2,34},{34,66},{66,9... | collective-permute-start | bytes 688136 | tf_op jit(solution)/shard_map/ppermute | solution.py:31
  12.3 34.9 %collective-permute-start.1 = (f32[14,1,32,128]{3,2,1,0:T(8,128)S(1)}, f32[14,1,32,128]{3,2,1,0:T(8,128)S(1)}, u32[]{:S(2)}, u32[]{:S(2)}) collective-permute-start(f32[14,1,32,128]{3,2,1,0:T(8,128)S(1)} %get-tuple-element.63), channel_id=1, source_target_pairs={{32,0},{64,32},{96,64},{33,1},{65,33},{97,65},{34,2},{66,34},{98,6... | collective-permute-start | bytes 688136 | tf_op jit(solution)/shard_map/ppermute | solution.py:33
  13.6 10.2 %collective-permute-start.7 = (f32[8,1,32,128]{3,0,2,1:T(8,128)S(1)}, f32[8,1,32,128]{3,0,2,1:T(8,128)S(1)}, u32[]{:S(2)}, u32[]{:S(2)}) collective-permute-start(f32[8,1,32,128]{3,0,2,1:T(8,128)S(1)} %get-tuple-element.81), channel_id=1, source_target_pairs={{32,0},{64,32},{96,64},{33,1},{65,33},{97,65},{34,2},{66,34},{98,6... | collective-permute-start | bytes 393224 | tf_op jit(solution)/shard_map/ppermute | solution.py:33
  15.6 10.8 %copy-start.6 = (f32[14,16,32,128]{3,2,1,0:T(8,128)S(1)}, f32[14,16,32,128]{3,2,1,0:T(8,128)}, u32[]{:S(2)}) copy-start(f32[14,16,32,128]{3,2,1,0:T(8,128)} %param.6) | copy-start | bytes 11010052
  23.8 3.7 collective-permute-start.8
  25.1 4.9 %collective-permute-start.9 = (f32[8,18,1,128]{3,0,2,1:T(8,128)S(1)}, f32[8,18,1,128]{3,0,2,1:T(8,128)S(1)}, u32[]{:S(2)}, u32[]{:S(2)}) collective-permute-start(f32[8,18,1,128]{3,0,2,1:T(8,128)S(1)} %get-tuple-element.77), channel_id=1, source_target_pairs={{4,0},{8,4},{12,8},{16,12},{20,16},{24,20},{28,24},{5,1},{9,5},{13... | collective-permute-start | bytes 221192 | tf_op jit(solution)/shard_map/ppermute | solution.py:33
  35.9 25.0 %collective-permute-start.10 = (f32[8,18,34,1]{2,0,3,1:T(8,128)S(1)}, f32[8,18,34,1]{2,0,3,1:T(8,128)S(1)}, u32[]{:S(2)}, u32[]{:S(2)}) collective-permute-start(f32[8,18,34,1]{2,0,3,1:T(8,128)S(1)} %copy.174), channel_id=1, source_target_pairs={{1,0},{2,1},{3,2},{5,4},{6,5},{7,6},{9,8},{10,9},{11,10},{13,12},{... | collective-permute-start | bytes 58760 | tf_op jit(solution)/shard_map/ppermute | solution.py:33
  40.0 23.6 %collective-permute-start.11 = (f32[8,18,34,1]{2,0,3,1:T(8,128)S(1)}, f32[8,18,34,1]{2,0,3,1:T(8,128)S(1)}, u32[]{:S(2)}, u32[]{:S(2)}) collective-permute-start(f32[8,18,34,1]{2,0,3,1:T(8,128)S(1)} %copy.176), channel_id=1, source_target_pairs={{0,1},{1,2},{2,3},{4,5},{5,6},{6,7},{8,9},{9,10},{10,11},{12,13},{... | collective-permute-start | bytes 58760 | tf_op jit(solution)/shard_map/ppermute | solution.py:31
  49.3 16.9 %collective-permute-start.2 = (f32[14,18,1,128]{3,0,2,1:T(8,128)S(1)}, f32[14,18,1,128]{3,0,2,1:T(8,128)S(1)}, u32[]{:S(2)}, u32[]{:S(2)}) collective-permute-start(f32[14,18,1,128]{3,0,2,1:T(8,128)S(1)} %copy.160), channel_id=1, source_target_pairs={{0,4},{4,8},{8,12},{12,16},{16,20},{20,24},{24,28},{1,5},{5,9},{9,... | collective-permute-start | bytes 387080 | tf_op jit(solution)/shard_map/ppermute | solution.py:31
  53.9 12.4 %collective-permute-start.3 = (f32[14,18,1,128]{3,0,2,1:T(8,128)S(1)}, f32[14,18,1,128]{3,0,2,1:T(8,128)S(1)}, u32[]{:S(2)}, u32[]{:S(2)}) collective-permute-start(f32[14,18,1,128]{3,0,2,1:T(8,128)S(1)} %copy.161), channel_id=1, source_target_pairs={{4,0},{8,4},{12,8},{16,12},{20,16},{24,20},{28,24},{5,1},{9,5},{13... | collective-permute-start | bytes 387080 | tf_op jit(solution)/shard_map/ppermute | solution.py:33
  78.8 17.5 %collective-permute-start.4 = (f32[14,18,34,1]{2,0,3,1:T(8,128)S(1)}, f32[14,18,34,1]{2,0,3,1:T(8,128)S(1)}, u32[]{:S(2)}, u32[]{:S(2)}) collective-permute-start(f32[14,18,34,1]{2,0,3,1:T(8,128)S(1)} %copy.164), channel_id=1, source_target_pairs={{0,1},{1,2},{2,3},{4,5},{5,6},{6,7},{8,9},{9,10},{10,11},{12,13},{... | collective-permute-start | bytes 102824 | tf_op jit(solution)/shard_map/ppermute | solution.py:31
  86.6 13.3 %collective-permute-start.5 = (f32[14,18,34,1]{2,0,3,1:T(8,128)S(1)}, f32[14,18,34,1]{2,0,3,1:T(8,128)S(1)}, u32[]{:S(2)}, u32[]{:S(2)}) collective-permute-start(f32[14,18,34,1]{2,0,3,1:T(8,128)S(1)} %copy.165), channel_id=1, source_target_pairs={{1,0},{2,1},{3,2},{5,4},{6,5},{7,6},{9,8},{10,9},{11,10},{13,12},{... | collective-permute-start | bytes 102824 | tf_op jit(solution)/shard_map/ppermute | solution.py:33
  147.4 31.3 %copy-start.12 = (f32[16,32,128]{2,1,0:T(8,128)}, f32[16,32,128]{2,1,0:T(8,128)S(1)}, u32[]{:S(2)}) copy-start(f32[16,32,128]{2,1,0:T(8,128)S(1)} %get-tuple-element.87) | copy-start | bytes 786436
  178.7 6.7 %copy-start.2 = (f32[8,16,32,128]{3,0,2,1:T(8,128)S(1)}, f32[8,16,32,128]{3,0,2,1:T(8,128)}, u32[]{:S(2)}) copy-start(f32[8,16,32,128]{3,0,2,1:T(8,128)} %fusion.17) | copy-start | bytes 6291460
  254.9 15.5 %copy-start.3 = (f32[8,16,32,128]{3,0,2,1:T(8,128)}, f32[8,16,32,128]{3,0,2,1:T(8,128)S(1)}, u32[]{:S(2)}) copy-start(f32[8,16,32,128]{3,0,2,1:T(8,128)S(1)} %convolution_subtract_fusion.1) | copy-start | bytes 6291460
  259.1 6.9 %collective-permute-start.12 = (f32[8,1,32,128]{3,0,2,1:T(8,128)S(1)}, f32[8,1,32,128]{3,0,2,1:T(8,128)S(1)}, u32[]{:S(2)}, u32[]{:S(2)}) collective-permute-start(f32[8,1,32,128]{3,0,2,1:T(8,128)S(1)} %get-tuple-element.79), channel_id=1, source_target_pairs={{0,32},{32,64},{64,96},{1,33},{33,65},{65,97},{2,34},{34,66},{66,9... | collective-permute-start | bytes 393224 | tf_op jit(solution)/shard_map/ppermute | solution.py:31
  260.5 6.9 %collective-permute-start.13 = (f32[8,1,32,128]{3,0,2,1:T(8,128)S(1)}, f32[8,1,32,128]{3,0,2,1:T(8,128)S(1)}, u32[]{:S(2)}, u32[]{:S(2)}) collective-permute-start(f32[8,1,32,128]{3,0,2,1:T(8,128)S(1)} %get-tuple-element.80), channel_id=1, source_target_pairs={{32,0},{64,32},{96,64},{33,1},{65,33},{97,65},{34,2},{66,34},{98,6... | collective-permute-start | bytes 393224 | tf_op jit(solution)/shard_map/ppermute | solution.py:33
  267.4 8.3 %collective-permute-start.14 = (f32[8,18,1,128]{3,0,2,1:T(8,128)S(1)}, f32[8,18,1,128]{3,0,2,1:T(8,128)S(1)}, u32[]{:S(2)}, u32[]{:S(2)}) collective-permute-start(f32[8,18,1,128]{3,0,2,1:T(8,128)S(1)} %get-tuple-element.75), channel_id=1, source_target_pairs={{0,4},{4,8},{8,12},{12,16},{16,20},{20,24},{24,28},{1,5},{5,9},{9,... | collective-permute-start | bytes 221192 | tf_op jit(solution)/shard_map/ppermute | solution.py:31
  268.7 7.0 %collective-permute-start.15 = (f32[8,18,1,128]{3,0,2,1:T(8,128)S(1)}, f32[8,18,1,128]{3,0,2,1:T(8,128)S(1)}, u32[]{:S(2)}, u32[]{:S(2)}) collective-permute-start(f32[8,18,1,128]{3,0,2,1:T(8,128)S(1)} %get-tuple-element.76), channel_id=1, source_target_pairs={{4,0},{8,4},{12,8},{16,12},{20,16},{24,20},{28,24},{5,1},{9,5},{13... | collective-permute-start | bytes 221192 | tf_op jit(solution)/shard_map/ppermute | solution.py:33
  282.4 12.3 %collective-permute-start.16 = (f32[8,18,34,1]{2,0,3,1:T(8,128)}, f32[8,18,34,1]{2,0,3,1:T(8,128)}, u32[]{:S(2)}, u32[]{:S(2)}) collective-permute-start(f32[8,18,34,1]{2,0,3,1:T(8,128)} %copy.215), channel_id=1, source_target_pairs={{1,0},{2,1},{3,2},{5,4},{6,5},{7,6},{9,8},{10,9},{11,10},{13,12},{... | collective-permute-start | bytes 58760 | tf_op jit(solution)/shard_map/ppermute | solution.py:33
  287.1 11.1 %collective-permute-start.17 = (f32[8,18,34,1]{2,0,3,1:T(8,128)}, f32[8,18,34,1]{2,0,3,1:T(8,128)}, u32[]{:S(2)}, u32[]{:S(2)}) collective-permute-start(f32[8,18,34,1]{2,0,3,1:T(8,128)} %copy.217), channel_id=1, source_target_pairs={{0,1},{1,2},{2,3},{4,5},{5,6},{6,7},{8,9},{9,10},{10,11},{12,13},{... | collective-permute-start | bytes 58760 | tf_op jit(solution)/shard_map/ppermute | solution.py:31
  (21 other events, 83.3 us)
where the time goes:
time: 396 us; the launch traced here: 389 us
  other arithmetic  107 us (27%)
  local copies, waits for them, and re-layouts  95.3 us (24%)
  blocking collectives  85 us (21%)
  matrix products  48.1 us (12%)
  starting transfers between devices  42 us (11%)
  waiting for transfers between devices  10.4 us (3%)
    psum x8, blocking collectives, over_axes(): x = lax.psum(x, axis)  85 us
    sub x2, other arithmetic, operate(): result = result - behind_w[None] * window(field, fmargin, depth, back)  60.9 us
    concatenate x7, other arithmetic, with_halo(): jnp.concatenate([lax.ppermute(tail, axis, [(i, (i + 1) % count) for i in...  34.9 us
    ppermute x9, starting transfers between devices, with_halo(): lax.ppermute(tail, axis, [(i, (i + 1) % count) for i in range(ends)])  29.2 us
    dot_general x5, matrix products, gram(): lax.dot_general(flat_l, flat_r, (((1,), (1,)), ((), ())), precision=lax.P...  28.4 us
    slice x35, local copies, waits for them, and re-layouts, window(): lax.slice_in_dim(result, begin, begin + inner + 2 * depth, axis=dim)  28.2 us
    dot_general x5, matrix products, combine(): jnp.einsum('ij,ixyz->jxyz', coef, field, precision=lax.Precision.HIGHEST)  17.8 us
    slice x9, local copies, waits for them, and re-layouts, with_halo(): head = lax.slice_in_dim(cells, 0, width, axis=dim)  17.3 us
  transfers between devices with their start and end apart: 18, of which 3 were waited for; matrix products, arithmetic and copies ran while one was open for 16% of the time, Pallas kernels for 0%

commit v1 on v0

v1 whole, which is shorter than its diff:
```python
import jax
import jax.numpy as jnp
from jax import lax
from jax.experimental import pallas as pl
from jax.experimental.pallas import tpu as pltpu
from jax.sharding import PartitionSpec as P

F32 = jnp.float32
X, Y, Z, F = 16, 32, 128, 8
FORWARD = [
    (a, b, c) for a in (-1, 0, 1) for b in (-1, 0, 1) for c in (-1, 0, 1) if (a, b, c) > (0, 0, 0)
]
OFF = {k + 1: o for k, o in enumerate(FORWARD)}
ZPLUS = [k for k in OFF if OFF[k][2] == 1]
ZMINUS = [k for k in OFF if OFF[k][2] == -1]
YPLUS = [k for k in OFF if OFF[k][1] == 1]
YMINUS = [k for k in OFF if OFF[k][1] == -1]
XPLUS = [k for k in OFF if OFF[k][0] == 1]
ZSHIFTED = ZPLUS + ZMINUS
WZ_AT = {k: i for i, k in enumerate(ZSHIFTED)}
GROUPS = ((0, 1), (1, -1), (1, 0), (1, 1))
SHIFT_AT = {0: 0, -1: 1, 1: 2}

VSPEC = pl.BlockSpec(memory_space=pltpu.VMEM)
HSPEC = pl.BlockSpec(memory_space=pl.ANY)
MIB = 1024 * 1024


def call(body, name, ins, outs, aliases=None, scratch=(), out_specs=None, limit=8):
    return pl.pallas_call(
        body,
        name=name,
        out_shape=[jax.ShapeDtypeStruct(s, F32) for s in outs],
        in_specs=[VSPEC] * len(ins),
        out_specs=out_specs or [VSPEC] * len(outs),
        input_output_aliases=aliases or {},
        scratch_shapes=list(scratch),
        compiler_params=pltpu.CompilerParams(vmem_limit_bytes=limit * MIB),
    )(*ins)


def lanes():
    return lax.broadcasted_iota(jnp.int32, (8, 128), 1)


def rows():
    return lax.broadcasted_iota(jnp.int32, (8, 128), 0)


def roll(v, shift):
    shift %= 128
    return pltpu.roll(v, shift, axis=1) if shift else v


def put_first(value, source, lane):
    return jnp.where(lanes() == 0, roll(source, -lane), roll(value, 1))


def put_last(value, source, lane):
    return jnp.where(lanes() == 127, roll(source, 127 - lane), roll(value, 127))


def spot(x, y):
    return (x % 4) * 32 + y


def pack_columns(field, high_ref, low_ref, base=0):
    def group(g, carry):
        high = jnp.zeros((8, 128), F32)
        low = jnp.zeros((8, 128), F32)
        for xx in range(4):
            for y in range(Y):
                v = field[4 * g + xx, y]
                at = spot(xx, y)
                here = lanes() == at
                high = jnp.where(here, roll(v, at - 127), high)
                low = jnp.where(here, roll(v, at), low)
        high_ref[base + g] = high
        low_ref[base + g] = low
        return carry

    lax.fori_loop(0, 4, group, 0)


def start_kernel(rhs, st, vi, zp, zm):
    def turn(x, carry):
        for yb in range(4):
            vi[x, pl.ds(8 * yb, 8)] = jnp.swapaxes(rhs[:, x, pl.ds(8 * yb, 8), :], 0, 1)
        return carry

    lax.fori_loop(0, X, turn, 0)
    pack_columns(vi, zp, zm)
    for ref, keys, edge in ((zp, ZPLUS, 127), (zm, ZMINUS, 0)):
        for j, k in enumerate(keys):
            out = jnp.zeros((8, 128), F32)
            for x in range(X):
                for yb in range(4):
                    at = 4 * x + yb
                    w = st[k, x, pl.ds(8 * yb, 8), :]
                    out = jnp.where(lanes() == at, roll(w, at - edge), out)
            ref[4 + j] = out


def shift_fields(vi, rl, rr, vm, vp):
    def group(g, carry):
        left = rl[g]
        right = rr[g]
        for xx in range(4):
            for y in range(Y):
                v = vi[4 * g + xx, y]
                at = spot(xx, y)
                vm[4 * g + xx, y] = put_first(v, left, at)
                vp[4 * g + xx, y] = put_last(v, right, at)
        return carry

    lax.fori_loop(0, 4, group, 0)


def edge_rows(vi, rl, rr, yp, ym):
    for x in range(X):
        yp[x] = vi[x, Y - 1]
        ym[x] = vi[x, 0]
    for g in range(4):
        yp[16 + g] = rl[g]
        yp[20 + g] = rr[g]
        ym[16 + g] = rl[g]
        ym[20 + g] = rr[g]


def behind_row(st, wz, k, x, y):
    if k in WZ_AT:
        return wz[WZ_AT[k], x, pl.ds(y, 1), :]
    return st[k, x, pl.ds(y, 1), :]


def second_kernel(vi, st, rl, rr, vm, vp, wz, sums, yp, ym):
    shift_fields(vi, rl, rr, vm, vp)
    for keys, source, put in ((ZPLUS, rl, put_first), (ZMINUS, rr, put_last)):
        for j, k in enumerate(keys):
            column = source[4 + j]
            for x in range(X):
                for yb in range(4):
                    w = st[k, x, pl.ds(8 * yb, 8), :]
                    wz[WZ_AT[k], x, pl.ds(8 * yb, 8), :] = put(w, column, 4 * x + yb)

    def behind(k, x, yb):
        if k in WZ_AT:
            return wz[WZ_AT[k], x, pl.ds(8 * yb, 8), :]
        return st[k, x, pl.ds(8 * yb, 8), :]

    def add_up(x, carry):
        for yb in range(4):
            total = st[0, x, pl.ds(8 * yb, 8), :]
            for k in OFF:
                total = total + st[k, x, pl.ds(8 * yb, 8), :]
            sums[4, x, pl.ds(8 * yb, 8), :] = total + behind(1, x, yb)
            for i, (a, b) in enumerate(GROUPS):
                keys = [k for k in OFF if OFF[k][:2] == (a, b)]
                sums[i, x, pl.ds(8 * yb, 8), :] = (
                    behind(keys[0], x, yb) + behind(keys[1], x, yb) + behind(keys[2], x, yb)
                )
        return carry

    lax.fori_loop(0, X, add_up, 0)
    edge_rows(vi, rl, rr, yp, ym)
    for ref, keys, y in ((yp, YPLUS, Y - 1), (ym, YMINUS, 0)):
        for j, k in enumerate(keys):
            for x in range(X):
                r = 16 * j + x
                ref[24 + r // 8, pl.ds(r % 8, 1), :] = behind_row(st, wz, k, x, y)


def second_again_kernel(vi, rl, rr, vm, vp, yp, ym):
    shift_fields(vi, rl, rr, vm, vp)
    edge_rows(vi, rl, rr, yp, ym)


def wide(row):
    return jnp.broadcast_to(row, (8, 128))


def plane(x, first, last, fields, st, wz, acc_ref, at, diag_of):
    cache = {}

    def v(s, dx, y):
        key = (s, dx, y)
        if key not in cache:
            cache[key] = fields[SHIFT_AT[s]][x + dx, y]
        return cache[key]

    coef = {}

    def ahead(k, y):
        if OFF[k][2] == 0:
            if (k, 0, y) not in coef:
                coef[k, 0, y] = wide(st[k, x, pl.ds(y, 1), :])
            return coef[k, 0, y]
        return wide(st[k, x, pl.ds(y, 1), :])

    def behind(k, a, y):
        if k not in WZ_AT:
            if (k, a, y) not in coef:
                coef[k, a, y] = wide(st[k, x - a, pl.ds(y, 1), :])
            return coef[k, a, y]
        return wide(wz[WZ_AT[k], x - a, pl.ds(y, 1), :])

    for y in range(Y):
        parts = [None, None]
        n = 0
        for k, (a, b, c) in OFF.items():
            if 0 <= y + b < Y and not (a == 1 and last):
                term = ahead(k, y) * v(c, a, y + b)
                parts[n % 2] = term if parts[n % 2] is None else parts[n % 2] + term
                n += 1
            if 0 <= y - b < Y and not (a == 1 and first):
                term = behind(k, a, y - b) * v(-c, -a, y - b)
                parts[n % 2] = term if parts[n % 2] is None else parts[n % 2] + term
                n += 1
        acc_ref[at, y] = wide(diag_of(x, y, first)) * v(0, 0, y) - (parts[0] + parts[1])


def interior(fields, st, wz, acc_ref, lo, hi, diag_of):
    begin, end = lo, hi
    if lo == 0:
        plane(0, True, False, fields, st, wz, acc_ref, 0, diag_of)
        begin = 1
    if hi == X:
        end = hi - 1

    def step(x, carry):
        plane(x, False, False, fields, st, wz, acc_ref, x - lo, diag_of)
        return carry

    lax.fori_loop(begin, end, step, 0)
    if hi == X:
        plane(X - 1, False, True, fields, st, wz, acc_ref, X - 1 - lo, diag_of)


def inner_kernel(lo, hi):
    def body(vi, vm, vp, st, wz, sums, acc, diag):
        def diag_of(x, y, first):
            total = sums[4, x, pl.ds(y, 1), :]
            if y > 0:
                total = total + sums[0, x, pl.ds(y - 1, 1), :]
            if not first:
                total = total + sums[2, x - 1, pl.ds(y, 1), :]
                if y > 0:
                    total = total + sums[3, x - 1, pl.ds(y - 1, 1), :]
                if y < Y - 1:
                    total = total + sums[1, x - 1, pl.ds(y + 1, 1), :]
            diag[x - lo, pl.ds(y, 1), :] = total
            return total

        interior((vi, vm, vp), st, wz, acc, lo, hi, diag_of)

    return body


def inner_again_kernel(lo, hi):
    def body(vi, vm, vp, st, wz, diag_lo, diag_hi, acc):
        diag = diag_lo if lo == 0 else diag_hi

        def diag_of(x, y, first):
            return diag[x - lo, pl.ds(y, 1), :]

        interior((vi, vm, vp), st, wz, acc, lo, hi, diag_of)

    return body


def ring_row(ref, keys, k, x):
    r = 16 * keys.index(k) + x
    return ref[24 + r // 8, pl.ds(r % 8, 1), :]


def third_kernel(with_diag):
    def body(*refs):
        if with_diag:
            vi, vm, vp, st, wz, rl, rr, qm, qp, sums, ring, xm, xp = refs
            qmw, qpw = qm, qp
        else:
            vi, vm, vp, st, wz, rl, rr, qm, qp, qmw, qpw, ring, xm, xp = refs
        for side, q, y in ((0, qm, Y - 1), (1, qp, 0)):
            for x in range(X):
                v = q[x]
                ring[side, 0, x] = v
                ring[side, 1, x] = put_first(v, q[16 + x // 4], spot(x, y))
                ring[side, 2, x] = put_last(v, q[20 + x // 4], spot(x, y))
        xm[0] = qm[0]
        for y in range(Y):
            xm[1 + y] = vi[0, y]
        xm[Y + 1] = qp[0]
        for i, tile in enumerate((rl[0], rr[0], qm[16], qm[20], qp[16], qp[20])):
            xm[Y + 2 + i] = tile
        last = X - 1
        for y in range(Y):
            total = None
            for k in XPLUS:
                _, b, c = OFF[k]
                s = SHIFT_AT[-c]
                if y - b < 0:
                    term = wide(ring_row(qmw, YPLUS, k, last)) * ring[0, s, last]
                elif y - b >= Y:
                    term = wide(ring_row(qpw, YMINUS, k, last)) * ring[1, s, last]
                else:
                    term = wide(behind_row(st, wz, k, last, y - b)) * (vi, vm, vp)[s][last, y - b]
                total = term if total is None else total + term
            xp[y] = total
            if with_diag:
                row = sums[2, last, pl.ds(y, 1), :]
                if y > 0:
                    row = row + sums[3, last, pl.ds(y - 1, 1), :]
                else:
                    for k in (11, 12, 13):
                        row = row + ring_row(qmw, YPLUS, k, last)
                if y < Y - 1:
                    row = row + sums[1, last, pl.ds(y + 1, 1), :]
                else:
                    for k in (5, 6, 7):
                        row = row + ring_row(qpw, YMINUS, k, last)
                xp[Y + y // 8, pl.ds(y % 8, 1), :] = row

    return body


def far_plane(tp):
    far = {}
    for y in range(-1, Y + 1):
        v = tp[y + 1]
        base, lane = (Y + 2, y) if 0 <= y < Y else ((Y + 4, Y - 1) if y < 0 else (Y + 6, 0))
        far[0, y] = v
        far[-1, y] = put_first(v, tp[base], lane)
        far[1, y] = put_last(v, tp[base + 1], lane)
    return far


def finish_edges(acc_of, acc_set, st, ring, qmw, qpw, tp, tm, extra):
    last = X - 1
    far = {}

    def far_at(s, y):
        if (s, y) not in far:
            v = tp[y + 1]
            base, lane = (Y + 2, y) if 0 <= y < Y else ((Y + 4, Y - 1) if y < 0 else (Y + 6, 0))
            if s == 0:
                far[s, y] = v
            elif s < 0:
                far[s, y] = put_first(v, tp[base], lane)
            else:
                far[s, y] = put_last(v, tp[base + 1], lane)
        return far[s, y]

    for x in range(X):
        for y in range(Y) if x in (0, last) else (0, Y - 1):
            total = None
            for k, (a, b, c) in OFF.items():
                terms = []
                if x + a == X:
                    terms.append(wide(st[k, x, pl.ds(y, 1), :]) * far_at(c, y + b))
                elif y + b < 0:
                    terms.append(wide(st[k, x, pl.ds(y, 1), :]) * ring[0, SHIFT_AT[c], x + a])
                elif y + b >= Y:
                    terms.append(wide(st[k, x, pl.ds(y, 1), :]) * ring[1, SHIFT_AT[c], x + a])
                if x - a >= 0:
                    if y - b < 0:
                        terms.append(
                            wide(ring_row(qmw, YPLUS, k, x - a)) * ring[0, SHIFT_AT[-c], x - a]
                        )
                    elif y - b >= Y:
                        terms.append(
                            wide(ring_row(qpw, YMINUS, k, x - a)) * ring[1, SHIFT_AT[-c], x - a]
                        )
                for term in terms:
                    total = term if total is None else total + term
            if x == 0:
                total = tm[y] if total is None else total + tm[y]
            value = acc_of(x, y) - total
            if extra is not None:
                fix = extra(x, y)
                if fix is not None:
                    value = value + fix
            acc_set(x, y, value)


HALF = X // 2


class Halves:
    def __init__(self, lo, hi):
        self.lo, self.hi = lo, hi

    def __getitem__(self, index):
        x, y = index
        return self.lo[x, y] if x < HALF else self.hi[x - HALF, y]


def join_kernel(with_diag):
    def body(*refs):
        if with_diag:
            acc_lo, acc_hi, dg_lo, dg_hi, vi, st, ring, qm, qp, tp, tm, out, dlo, dhi, zp, zm = refs

            def fix(x, y):
                row = None
                if y == 0:
                    for k in (2, 3, 4):
                        r = ring_row(qm, YPLUS, k, x)
                        row = r if row is None else row + r
                    if x > 0:
                        for k in (11, 12, 13):
                            row = row + ring_row(qm, YPLUS, k, x - 1)
                if y == Y - 1 and x > 0:
                    for k in (5, 6, 7):
                        r = ring_row(qp, YMINUS, k, x - 1)
                        row = r if row is None else row + r
                if x == 0:
                    r = tm[Y + y // 8, pl.ds(y % 8, 1), :]
                    row = r if row is None else row + r
                if row is None:
                    return None
                d = dlo if x < HALF else dhi
                d[x % HALF, pl.ds(y, 1), :] = d[x % HALF, pl.ds(y, 1), :] + row
                return wide(row) * vi[x, y]

            dlo[...] = dg_lo[...]
            dhi[...] = dg_hi[...]
        else:
            acc_lo, acc_hi, st, ring, qm, qp, tp, tm, out = refs
            fix = None

        def copy_lo(x, carry):
            out[x] = acc_lo[x]
            out[x + HALF] = acc_hi[x]
            return carry

        lax.fori_loop(0, HALF, copy_lo, 0)

        def acc_set(x, y, value):
            out[x, y] = value

        finish_edges(Halves(acc_lo, acc_hi).__getitem__ and (lambda x, y: Halves(acc_lo, acc_hi)[x, y]),
                     acc_set, st, ring, qm, qp, tp, tm, fix)
        if with_diag:
            pack_columns(out, zp, zm)

    return body


def turn_slow(v, s):
    return pltpu.roll(v, s, axis=0) if s else v


def lane_sum(v):
    return jnp.broadcast_to(jnp.sum(v, axis=1, keepdims=True), (8, 128))


def diagonals(pairs_of, count):
    zero = tuple(jnp.zeros((8, 128), F32) for _ in range(count))

    def step(i, carry):
        carry = list(carry)
        for j in range(4):
            for n, term in enumerate(pairs_of(i // 8, (i % 8) * 4 + j)):
                carry[n] = carry[n] + term
        return tuple(carry)

    return lax.fori_loop(0, X * Y // 4, step, zero)


def gram_early_kernel(vi, y1, out):
    def terms(x, y):
        u = vi[x, y]
        w = y1[x, y]
        result = []
        for s in range(5):
            ws = turn_slow(w, s)
            result += [u * turn_slow(u, s), u * ws, w * ws]
        return result

    sums = diagonals(terms, 15)
    tile = jnp.zeros((8, 128), F32)
    for s in range(5):
        for m in range(3):
            tile = jnp.where(lanes() == 8 * m + s, lane_sum(sums[3 * s + m]), tile)
    out[...] = tile


def gram_late_kernel(y1, y2, early, out):
    def terms(x, y):
        u = y1[x, y]
        w = y2[x, y]
        return [u * turn_slow(w, s) for s in range(5)]

    sums = diagonals(terms, 5)
    tile = early[...]
    for s in range(5):
        tile = jnp.where(lanes() == 24 + s, lane_sum(sums[s]), tile)
    out[...] = tile


def flat_kernel(v, out):
    def turn(x, carry):
        for yb in range(4):
            out[:, x, pl.ds(8 * yb, 8), :] = jnp.swapaxes(v[x, pl.ds(8 * yb, 8)], 0, 1)
        return carry

    lax.fori_loop(0, X, turn, 0)


def column(m, j):
    return lane_sum(jnp.where(lanes() == j, m, 0.0))


def across(m, i):
    return jnp.broadcast_to(m[i : i + 1, :], (8, 128))


def times(left, right):
    total = None
    for k in range(8):
        term = column(left, k) * across(right, k)
        total = term if total is None else total + term
    return total


def flip(m):
    out = jnp.zeros((8, 128), F32)
    for k in range(8):
        out = jnp.where(lanes() == k, lane_sum(jnp.where(lanes() == rows(), across(m, k), 0.0)), out)
    return out


def solve(matrix, right):
    both = jnp.where(lanes() < 8, matrix, pltpu.roll(right, 8, axis=1))
    for k in range(8):
        col = column(both, k)
        row = across(both, k) / across(col, k)
        both = jnp.where(rows() == k, row, both - col * row)
    moved = pltpu.roll(both, 120, axis=1)
    return jnp.where(lanes() < 8, moved, 0.0)


def moments(tile, m):
    total = jnp.zeros((8, 128), F32)
    for s in range(8):
        if s <= 4:
            col = column(tile, 8 * m + s)
        else:
            col = turn_slow(column(tile, 8 * m + 8 - s), s)
        hit = (lanes() < 8) & (((rows() - lanes()) & 7) == s)
        total = jnp.where(hit, col, total)
    return total


def last_kernel(tile_ref, r0, y1, y2, sol, res, coef, sbuf, rbuf, sems):
    tile = tile_ref[...]
    m0, m1, m2, m3 = (moments(tile, m) for m in range(4))
    eye = jnp.where((lanes() == rows()) & (lanes() < 8), 1.0, 0.0)
    alpha = solve(m1, m0)
    inverse = solve(m0, eye)
    alpha_t = flip(alpha)
    m2a = times(m2, alpha)
    first = times(m1, alpha)
    rr1 = m0 - first - flip(first) + times(alpha_t, m2a)
    big = eye + times(inverse, rr1)
    big_t = flip(big)
    pq = times(big_t, times(m1, big) - m2a) + times(alpha_t, times(m3, alpha) - times(m2, big))
    alpha2 = solve(pq, rr1)
    c1 = alpha + times(big, alpha2)
    c2 = times(alpha, alpha2)
    for j in range(8):
        coef[0, j] = column(c1, j)
        coef[1, j] = column(c2, j)

    chunk = 2
    copies = []

    def tile_out(x, yb):
        at = pl.ds(8 * yb, 8)
        a = [r0[i, x, at, :] for i in range(8)]
        b = [y1[i, x, at, :] for i in range(8)]
        c = [y2[i, x, at, :] for i in range(8)]
        for j in range(8):
            s0 = s1 = t0 = t1 = None
            for i in range(8):
                p = wide(coef[0, j, pl.ds(i, 1), :])
                q = wide(coef[1, j, pl.ds(i, 1), :])
                s0 = p * a[i] if s0 is None else s0 + p * a[i]
                s1 = q * b[i] if s1 is None else s1 + q * b[i]
                t0 = p * b[i] if t0 is None else t0 + p * b[i]
                t1 = q * c[i] if t1 is None else t1 + q * c[i]
            sbuf[j, x, at, :] = s0 - s1
            rbuf[j, x, at, :] = a[j] - (t0 - t1)

    def copy(n, src, dst, which):
        part = pl.ds(n * chunk, chunk)
        return pltpu.make_async_copy(src.at[:, part], dst.at[:, part], sems.at[which, n])

    def step(n, carry):
        for xx in range(chunk):
            def inner(yb, c):
                tile_out(n * chunk + xx, yb)
                return c
            lax.fori_loop(0, 4, inner, 0)
        copy(n, sbuf, sol, 0).start()
        copy(n, rbuf, res, 1).start()
        return carry

    lax.fori_loop(0, X // chunk, step, 0)
    for n in range(X // chunk):
        copy(n, sbuf, sol, 0).wait()
        copy(n, rbuf, res, 1).wait()


def shift(x, axis, step):
    n = lax.axis_size(axis)
    return lax.ppermute(x, axis, [(i, i + step) for i in range(n) if 0 <= i + step < n])


def everywhere(x):
    for axis in ("gy", "gx", "gz"):
        bit = 1
        while bit < lax.axis_size(axis):
            n = lax.axis_size(axis)
            x = x + lax.ppermute(x, axis, [(i, i ^ bit) for i in range(n)])
            bit *= 2
    return x


def shards(rhs, stencil):
    full = (X, Y, F, Z)
    half = (HALF, Y, F, Z)
    vi, zp, zm = call(start_kernel, "k_start", [rhs, stencil], [full, (9, 8, 128), (8, 8, 128)])
    rl = shift(zp, "gz", 1)
    rr = shift(zm, "gz", -1)
    vm, vp, wz, sums, yp, ym = call(
        second_kernel, "k_second", [vi, stencil, rl, rr],
        [full, full, (9, X, Y, Z), (5, X, Y, Z), (36, 8, 128), (30, 8, 128)],
    )
    qm = shift(yp, "gy", 1)
    qp = shift(ym, "gy", -1)
    dhalf = (HALF, Y, Z)
    acc_lo, dg_lo = call(inner_kernel(0, HALF), "k_inner_lo", [vi, vm, vp, stencil, wz, sums], [half, dhalf])
    ring, xm, xp = call(
        third_kernel(True), "k_third", [vi, vm, vp, stencil, wz, rl, rr, qm, qp, sums],
        [(2, 3, X, 8, 128), (Y + 8, 8, 128), (Y + 4, 8, 128)],
    )
    tp = shift(xm, "gx", -1)
    tm = shift(xp, "gx", 1)
    acc_hi, dg_hi = call(inner_kernel(HALF, X), "k_inner_hi", [vi, vm, vp, stencil, wz, sums], [half, dhalf])
    y1, dlo, dhi, zp, zm = call(
        join_kernel(True), "k_join",
        [acc_lo, acc_hi, dg_lo, dg_hi, vi, stencil, ring, qm, qp, tp, tm],
        [full, dhalf, dhalf, (4, 8, 128), (4, 8, 128)],
    )

    rl = shift(zp, "gz", 1)
    rr = shift(zm, "gz", -1)
    (early,) = call(gram_early_kernel, "k_gram", [vi, y1], [(8, 128)])
    vm, vp, yp, ym = call(
        second_again_kernel, "k_second2", [y1, rl, rr], [full, full, (24, 8, 128), (24, 8, 128)]
    )
    qmv = shift(yp, "gy", 1)
    qpv = shift(ym, "gy", -1)
    (acc_lo,) = call(inner_again_kernel(0, HALF), "k_inner2_lo", [y1, vm, vp, stencil, wz, dlo, dhi], [half])
    ring, xm, xp = call(
        third_kernel(False), "k_third2", [y1, vm, vp, stencil, wz, rl, rr, qmv, qpv, qm, qp],
        [(2, 3, X, 8, 128), (Y + 8, 8, 128), (Y, 8, 128)],
    )
    tp = shift(xm, "gx", -1)
    tm = shift(xp, "gx", 1)
    (acc_hi,) = call(inner_again_kernel(HALF, X), "k_inner2_hi", [y1, vm, vp, stencil, wz, dlo, dhi], [half])
    (y2,) = call(
        join_kernel(False), "k_join2", [acc_lo, acc_hi, stencil, ring, qm, qp, tp, tm], [full]
    )
    (tile,) = call(gram_late_kernel, "k_gram2", [y1, y2, early], [(8, 128)])
    compact = (F, X, Y, Z)
    (y1f,) = call(flat_kernel, "k_flat1", [y1], [compact])
    (y2f,) = call(flat_kernel, "k_flat2", [y2], [compact])
    tile = everywhere(tile)
    sol, res = call(
        last_kernel, "k_last", [tile, rhs, y1f, y2f], [compact, compact],
        out_specs=[HSPEC, HSPEC],
        scratch=[
            pltpu.VMEM((2, 8, 8, 128), F32),
            pltpu.VMEM(compact, F32),
            pltpu.VMEM(compact, F32),
            pltpu.SemaphoreType.DMA((2, X // 2)),
        ],
        limit=14,
    )
    return sol, res


def solution(mesh):
    placed = P(None, "gx", "gy", "gz")
    return jax.shard_map(
        shards, mesh=mesh, in_specs=(placed, placed), out_specs=(placed, placed), check_vma=False
    )
```

time: 396 us -> 115 us (0.29); the launches traced: 389 us -> 114 us
  other arithmetic: 107 us -> 0.02 us
  local copies, waits for them, and re-layouts: 95.3 us -> 3.63 us
  blocking collectives: 85 us -> 0 us
  matrix products: 48.1 us -> 0 us
  Pallas kernels: 0 us -> 35.5 us
  waiting for transfers between devices: 10.4 us -> 29.2 us
    psum x8 -> x0, blocking collectives: 85 us -> none  [over_axes(): x = lax.psum(x, axis)]
    slice x51 -> x0, local copies, waits for them, and re-layouts: 61.5 us -> none  [the longest x35 28.2 us: window(): lax.slice_in_dim(result, begin, begin + inner + 2 * depth, axis=dim)]
    sub x2 -> x0, other arithmetic: 60.9 us -> none  [operate(): result = result - behind_w[None] * window(field, fmargin, depth, back)]
    dot_general x14 -> x0, matrix products: 47 us -> none  [the longest x5 28.4 us: gram(): lax.dot_general(flat_l, flat_r, (((1,), (1,)), ((), ())), precision=lax.P...]
    pallas_call x0 -> x16, Pallas kernels: none -> 35.5 us  [call(): pl.pallas_call(body, name=name, out_shape=[jax.ShapeDtypeStruct(s, F32) f...]
    concatenate x7 -> x0, other arithmetic: 34.9 us -> none  [with_halo(): jnp.concatenate([lax.ppermute(tail, axis, [(i, (i + 1) % count) for i in...]
    ppermute x8 -> x0, local copies, waits for them, and re-layouts: 19.4 us -> none  [the longest x4 9.74 us: with_halo(): lax.ppermute(head, axis, [((i + 1) % count, i) for i in range(ends)])]
    ppermute x18 -> x19, waiting for transfers between devices: 10.4 us -> 29.2 us  [the longest x12 15.9 us: shift(): lax.ppermute(x, axis, [(i, i + step) for i in range(n) if 0 <= i + step <...]
  transfers between devices with their start and end apart: 18 -> 19, of which waited for: 3 -> 12; matrix products, arithmetic and copies ran while one was open for 16% -> 0% of each run, Pallas kernels for 0% -> 11%
where the time goes in v1:
time: 115 us; the launch traced here: 114 us
  starting transfers between devices  44.9 us (39%)
  Pallas kernels  35.5 us (31%)
  waiting for transfers between devices  29.2 us (25%)
  local copies, waits for them, and re-layouts  3.63 us (3%)
    pallas_call x16, Pallas kernels, call(): pl.pallas_call(body, name=name, out_shape=[jax.ShapeDtypeStruct(s, F32) f...  35.5 us
    ppermute x12, starting transfers between devices, shift(): lax.ppermute(x, axis, [(i, i + step) for i in range(n) if 0 <= i + step <...  29.3 us
    ppermute x12, waiting for transfers between devices, shift(): lax.ppermute(x, axis, [(i, i + step) for i in range(n) if 0 <= i + step <...  15.9 us
    ppermute x7, starting transfers between devices, everywhere(): x = x + lax.ppermute(x, axis, [(i, i ^ bit) for i in range(n)])  15.6 us
    ppermute x7, waiting for transfers between devices, everywhere(): x = x + lax.ppermute(x, axis, [(i, i ^ bit) for i in range(n)])  13.3 us
    unnamed x8, local copies, waits for them, and re-layouts  3.63 us
  transfers between devices with their start and end apart: 19, of which 12 were waited for; matrix products, arithmetic and copies ran while one was open for 0% of the time, Pallas kernels for 11%

profile of v1, /device:TPU:0, one launch (start us, length us, event | category | flops | bytes accessed | tf_op | source)
XLA Modules:
  0.0 114.1 jit_solution(15405617864810459674)
XLA Ops:
  0.6 2.0 %copy-done = f32[14,16,32,128]{3,2,1,0:T(8,128)S(1)} copy-done((f32[14,16,32,128]{3,2,1,0:T(8,128)S(1)}, f32[14,16,32,128]{3,2,1,0:T(8,128)}, u32[]{:S(2)}) %copy-start) | copy-done | bytes 3670040
  4.3 2.5 %k_start.1 = (f32[16,32,8,128]{3,2,1,0:T(8,128)S(1)}, f32[9,8,128]{2,1,0:T(8,128)S(1)}, f32[8,8,128]{2,1,0:T(8,128)S(1)}) custom-call(f32[8,16,32,128]{3,2,1,0:T(8,128)S(1)} %copy-done.2, f32[14,16,32,128]{3,2,1,0:T(8,128)S(1)} %copy-done), custom_call_target="tpu_custom_call" | custom-call | tf_op jit(solution)/shard_map/k_start/pallas_call | solution.py:30
  6.7 3.9 %collective-permute-start = (f32[9,8,128]{2,1,0:T(8,128)S(1)}, f32[9,8,128]{2,1,0:T(8,128)S(1)}, u32[]{:S(2)}, u32[]{:S(2)}) collective-permute-start(f32[9,8,128]{2,1,0:T(8,128)S(1)} %get-tuple-element.31), channel_id=1, source_target_pairs={{0,1},{1,2},{2,3},{4,5},{5,6},{6,7},{8,9},{9,10},{10,11},{12,13},{... | collective-permute-start | bytes 110600 | tf_op jit(solution)/shard_map/ppermute | solution.py:616
  12.0 4.5 %collective-permute-done.1.rr.refs_6_ = f32[8,8,128]{2,1,0:T(8,128)S(1)} collective-permute-done((f32[8,8,128]{2,1,0:T(8,128)S(1)}, f32[8,8,128]{2,1,0:T(8,128)S(1)}, u32[]{:S(2)}, u32[]{:S(2)}) %collective-permute-start.1) | collective-permute-done | bytes 32800 | tf_op jit(solution)/shard_map/ppermute | solution.py:616
  16.5 4.3 %k_second.1 = (f32[16,32,8,128]{3,2,1,0:T(8,128)S(1)}, f32[16,32,8,128]{3,2,1,0:T(8,128)S(1)}, f32[9,16,32,128]{3,2,1,0:T(8,128)S(1)}, f32[5,16,32,128]{3,2,1,0:...) custom-call(f32[16,32,8,128]{3,2,1,0:T(8,128)S(1)} %get-tuple-element.30.vi.refs_0_.refs_4_, ...), custom_call_target="tpu_custom_call" | custom-call | tf_op jit(solution)/shard_map/k_second/pallas_call | solution.py:30
  23.4 3.6 %collective-permute-done.3.refs_8_.refs_10_.refs_5_ = f32[30,8,128]{2,1,0:T(8,128)S(1)} collective-permute-done((f32[30,8,128]{2,1,0:T(8,128)S(1)}, f32[30,8,128]{2,1,0:T(8,128)S(1)}, u32[]{:S(2)}, u32[]{:S(2)}) %collective-permute-start.3) | collective-permute-done | bytes 122912 | tf_op jit(solution)/shard_map/ppermute | solution.py:616
  28.5 4.6 %collective-permute-start.5 = (f32[36,8,128]{2,1,0:T(8,128)S(1)}, f32[36,8,128]{2,1,0:T(8,128)S(1)}, u32[]{:S(2)}, u32[]{:S(2)}) collective-permute-start(f32[36,8,128]{2,1,0:T(8,128)S(1)} %get-tuple-element.45), channel_id=1, source_target_pairs={{0,32},{32,64},{64,96},{1,33},{33,65},{65,97},{2,34},{34,66},{66,9... | collective-permute-start | bytes 442376 | tf_op jit(solution)/shard_map/ppermute | solution.py:616
  33.1 2.2 %k_inner_lo.1 = (f32[8,32,8,128]{3,2,1,0:T(8,128)S(1)}, f32[8,32,128]{2,1,0:T(8,128)S(1)}) custom-call(f32[16,32,8,128]{3,2,1,0:T(8,128)S(1)} %get-tuple-element.30.vi.refs_0_.refs_4_, f32[16,32,8,128]{3,2,1,0:T(8,128)S(1)} %get-tuple-element.33.vm.refs_1_, f32[16,32,8,128]{3,2,1,0:T(8,128)S(1)} %get-tuple-element.34.vp.refs_2_, ...), custom_call_target="tpu_custom_call" | custom-call | tf_op jit(solution)/shard_map/k_inner_lo/pallas_call | solution.py:30
  35.2 2.2 %k_inner_hi.1 = (f32[8,32,8,128]{3,2,1,0:T(8,128)S(1)}, f32[8,32,128]{2,1,0:T(8,128)S(1)}) custom-call(f32[16,32,8,128]{3,2,1,0:T(8,128)S(1)} %get-tuple-element.30.vi.refs_0_.refs_4_, f32[16,32,8,128]{3,2,1,0:T(8,128)S(1)} %get-tuple-element.33.vm.refs_1_, f32[16,32,8,128]{3,2,1,0:T(8,128)S(1)} %get-tuple-element.34.vp.refs_2_, ...), custom_call_target="tpu_custom_call" | custom-call | tf_op jit(solution)/shard_map/k_inner_hi/pallas_call | solution.py:30
  39.3 3.8 %collective-permute-start.6 = (f32[4,8,128]{2,1,0:T(8,128)S(1)}, f32[4,8,128]{2,1,0:T(8,128)S(1)}, u32[]{:S(2)}, u32[]{:S(2)}) collective-permute-start(f32[4,8,128]{2,1,0:T(8,128)S(1)} %get-tuple-element.47), channel_id=1, source_target_pairs={{0,1},{1,2},{2,3},{4,5},{5,6},{6,7},{8,9},{9,10},{10,11},{12,13},{... | collective-permute-start | bytes 49160 | tf_op jit(solution)/shard_map/ppermute | solution.py:616
  44.6 4.2 %collective-permute-done.7.rr.refs_6_ = f32[4,8,128]{2,1,0:T(8,128)S(1)} collective-permute-done((f32[4,8,128]{2,1,0:T(8,128)S(1)}, f32[4,8,128]{2,1,0:T(8,128)S(1)}, u32[]{:S(2)}, u32[]{:S(2)}) %collective-permute-start.7) | collective-permute-done | bytes 16416 | tf_op jit(solution)/shard_map/ppermute | solution.py:616
  48.8 2.4 %k_second2.1 = (f32[16,32,8,128]{3,2,1,0:T(8,128)S(1)}, f32[16,32,8,128]{3,2,1,0:T(8,128)S(1)}, f32[24,8,128]{2,1,0:T(8,128)S(1)}, f32[24,8,128]{2,1,0:T(8,128)S(1)}) custom-call(f32[16,32,8,128]{3,2,1,0:T(8,128)S(1)} %get-tuple-element.46.vi.refs_0_.y1.v, f32[4,8,128]{2,1,0:T(8,128)S(1)} %collective-permute-done.6.rl.refs_5_, ...), custom_call_target="tpu_custom_call" | custom-call | tf_op jit(solution)/shard_map/k_second2/pallas_call | solution.py:30
  51.2 3.4 %collective-permute-start.8 = (f32[24,8,128]{2,1,0:T(8,128)S(1)}, f32[24,8,128]{2,1,0:T(8,128)S(1)}, u32[]{:S(2)}, u32[]{:S(2)}) collective-permute-start(f32[24,8,128]{2,1,0:T(8,128)S(1)} %get-tuple-element.53), channel_id=1, source_target_pairs={{0,4},{4,8},{8,12},{12,16},{16,20},{20,24},{24,28},{1,5},{5,9},{9,... | collective-permute-start | bytes 294920 | tf_op jit(solution)/shard_map/ppermute | solution.py:616
  55.9 3.3 %collective-permute-done.9.refs_8_ = f32[24,8,128]{2,1,0:T(8,128)S(1)} collective-permute-done((f32[24,8,128]{2,1,0:T(8,128)S(1)}, f32[24,8,128]{2,1,0:T(8,128)S(1)}, u32[]{:S(2)}, u32[]{:S(2)}) %collective-permute-start.9) | collective-permute-done | bytes 98336 | tf_op jit(solution)/shard_map/ppermute | solution.py:616
  60.8 4.6 %collective-permute-start.11 = (f32[32,8,128]{2,1,0:T(8,128)S(1)}, f32[32,8,128]{2,1,0:T(8,128)S(1)}, u32[]{:S(2)}, u32[]{:S(2)}) collective-permute-start(f32[32,8,128]{2,1,0:T(8,128)S(1)} %get-tuple-element.57), channel_id=1, source_target_pairs={{0,32},{32,64},{64,96},{1,33},{33,65},{65,97},{2,34},{34,66},{66,9... | collective-permute-start | bytes 393224 | tf_op jit(solution)/shard_map/ppermute | solution.py:616
  65.3 4.0 %k_gram.1.early = f32[8,128]{1,0:T(8,128)S(1)} custom-call(f32[16,32,8,128]{3,2,1,0:T(8,128)S(1)} %get-tuple-element.30.vi.refs_0_.refs_4_, f32[16,32,8,128]{3,2,1,0:T(8,128)S(1)} %get-tuple-element.46.vi.refs_0_.y1.v), custom_call_target="tpu_custom_call" | custom-call | tf_op jit(solution)/shard_map/k_gram/pallas_call | solution.py:30
  73.6 2.4 %k_gram2.1 = f32[8,128]{1,0:T(8,128)S(1)} custom-call(f32[16,32,8,128]{3,2,1,0:T(8,128)S(1)} %get-tuple-element.46.vi.refs_0_.y1.v, f32[16,32,8,128]{3,2,1,0:T(8,128)S(1)} %k_join2.1.y2.v, f32[8,128]{1,0:T(8,128)S(1)} %k_gram.1.early), custom_call_target="tpu_custom_call" | custom-call | tf_op jit(solution)/shard_map/k_gram2/pallas_call | solution.py:30
  76.0 2.7 %collective-permute-start.12 = (f32[8,128]{1,0:T(8,128)S(1)}, f32[8,128]{1,0:T(8,128)S(1)}, u32[]{:S(2)}, u32[]{:S(2)}) collective-permute-start(f32[8,128]{1,0:T(8,128)S(1)} %k_gram2.1), channel_id=1, source_target_pairs={{0,4},{4,0},{8,12},{12,8},{16,20},{20,16},{24,28},{28,24},{1,5},{5... | collective-permute-start | bytes 12296 | tf_op jit(solution)/shard_map/ppermute | solution.py:624
  83.2 2.6 %collective-permute-start.14 = (f32[8,128]{1,0:T(8,128)S(1)}, f32[8,128]{1,0:T(8,128)S(1)}, u32[]{:S(2)}, u32[]{:S(2)}) collective-permute-start(f32[8,128]{1,0:T(8,128)S(1)} %add.22), channel_id=1, source_target_pairs={{0,16},{4,20},{8,24},{12,28},{16,0},{20,4},{24,8},{28,12},{1,17},{... | collective-permute-start | bytes 12296 | tf_op jit(solution)/shard_map/ppermute | solution.py:624
  85.8 2.5 %collective-permute-done.14 = f32[8,128]{1,0:T(8,128)S(1)} collective-permute-done((f32[8,128]{1,0:T(8,128)S(1)}, f32[8,128]{1,0:T(8,128)S(1)}, u32[]{:S(2)}, u32[]{:S(2)}) %collective-permute-start.14) | collective-permute-done | bytes 4128 | tf_op jit(solution)/shard_map/ppermute | solution.py:624
  91.9 3.4 %collective-permute-start.16 = (f32[8,128]{1,0:T(8,128)S(1)}, f32[8,128]{1,0:T(8,128)S(1)}, u32[]{:S(2)}, u32[]{:S(2)}) collective-permute-start(f32[8,128]{1,0:T(8,128)S(1)} %add.24), channel_id=1, source_target_pairs={{0,64},{32,96},{64,0},{96,32},{1,65},{33,97},{65,1},{97,33},{2,66}... | collective-permute-start | bytes 12296 | tf_op jit(solution)/shard_map/ppermute | solution.py:624
  98.7 2.0 %collective-permute-done.17 = f32[8,128]{1,0:T(8,128)S(1)} collective-permute-done((f32[8,128]{1,0:T(8,128)S(1)}, f32[8,128]{1,0:T(8,128)S(1)}, u32[]{:S(2)}, u32[]{:S(2)}) %collective-permute-start.17) | collective-permute-done | bytes 4128 | tf_op jit(solution)/shard_map/ppermute | solution.py:624
  103.2 2.5 %collective-permute-done.18 = f32[8,128]{1,0:T(8,128)S(1)} collective-permute-done((f32[8,128]{1,0:T(8,128)S(1)}, f32[8,128]{1,0:T(8,128)S(1)}, u32[]{:S(2)}, u32[]{:S(2)}) %collective-permute-start.18) | collective-permute-done | bytes 4128 | tf_op jit(solution)/shard_map/ppermute | solution.py:624
  105.8 8.3 %k_last.1 = (f32[8,16,32,128]{3,2,1,0:T(8,128)}, f32[8,16,32,128]{3,2,1,0:T(8,128)}) custom-call(f32[8,128]{1,0:T(8,128)S(1)} %add.27.tile_ref, f32[8,16,32,128]{3,2,1,0:T(8,128)S(1)} %copy-done.3, f32[8,16,32,128]{3,2,1,0:T(8,128)S(1)} %k_flat1.1.y1, f32[8,16,32,128]{3,2,1,0:T(8,128)S(1)} %k_flat2.1.y2), custom_call_target="tpu_custom_call" | custom-call | tf_op jit(solution)/shard_map/k_last/pallas_call | solution.py:30
  (45 shorter events, 31.3 us)
Async XLA Ops:
  0.6 2.0 %copy-start = (f32[14,16,32,128]{3,2,1,0:T(8,128)S(1)}, f32[14,16,32,128]{3,2,1,0:T(8,128)}, u32[]{:S(2)}) copy-start(f32[14,16,32,128]{3,2,1,0:T(8,128)} %refs_2_.1) | copy-start | bytes 11010052
  2.7 1.6 %copy-start.2 = (f32[8,16,32,128]{3,2,1,0:T(8,128)S(1)}, f32[8,16,32,128]{3,2,1,0:T(8,128)}, u32[]{:S(2)}) copy-start(f32[8,16,32,128]{3,2,1,0:T(8,128)} %r0.1) | copy-start | bytes 6291460
  4.3 12.2 %copy-start.1 = (f32[14,16,32,128]{3,2,1,0:T(8,128)S(1)}, f32[14,16,32,128]{3,2,1,0:T(8,128)}, u32[]{:S(2)}) copy-start(f32[14,16,32,128]{3,2,1,0:T(8,128)} %refs_2_.1) | copy-start | bytes 11010052
  6.7 9.8 %collective-permute-start = (f32[9,8,128]{2,1,0:T(8,128)S(1)}, f32[9,8,128]{2,1,0:T(8,128)S(1)}, u32[]{:S(2)}, u32[]{:S(2)}) collective-permute-start(f32[9,8,128]{2,1,0:T(8,128)S(1)} %get-tuple-element.31), channel_id=1, source_target_pairs={{0,1},{1,2},{2,3},{4,5},{5,6},{6,7},{8,9},{9,10},{10,11},{12,13},{... | collective-permute-start | bytes 110600 | tf_op jit(solution)/shard_map/ppermute | solution.py:616
  10.7 5.8 %collective-permute-start.1 = (f32[8,8,128]{2,1,0:T(8,128)S(1)}, f32[8,8,128]{2,1,0:T(8,128)S(1)}, u32[]{:S(2)}, u32[]{:S(2)}) collective-permute-start(f32[8,8,128]{2,1,0:T(8,128)S(1)} %get-tuple-element.32), channel_id=1, source_target_pairs={{1,0},{2,1},{3,2},{5,4},{6,5},{7,6},{9,8},{10,9},{11,10},{13,12},{... | collective-permute-start | bytes 98312 | tf_op jit(solution)/shard_map/ppermute | solution.py:616
  20.8 6.3 %collective-permute-start.2 = (f32[36,8,128]{2,1,0:T(8,128)S(1)}, f32[36,8,128]{2,1,0:T(8,128)S(1)}, u32[]{:S(2)}, u32[]{:S(2)}) collective-permute-start(f32[36,8,128]{2,1,0:T(8,128)S(1)} %get-tuple-element.41), channel_id=1, source_target_pairs={{0,4},{4,8},{8,12},{12,16},{16,20},{20,24},{24,28},{1,5},{5,9},{9,... | collective-permute-start | bytes 442376 | tf_op jit(solution)/shard_map/ppermute | solution.py:616
  22.1 4.9 %collective-permute-start.3 = (f32[30,8,128]{2,1,0:T(8,128)S(1)}, f32[30,8,128]{2,1,0:T(8,128)S(1)}, u32[]{:S(2)}, u32[]{:S(2)}) collective-permute-start(f32[30,8,128]{2,1,0:T(8,128)S(1)} %get-tuple-element.42), channel_id=1, source_target_pairs={{4,0},{8,4},{12,8},{16,12},{20,16},{24,20},{28,24},{5,1},{9,5},{13... | collective-permute-start | bytes 368648 | tf_op jit(solution)/shard_map/ppermute | solution.py:616
  27.2 10.2 %collective-permute-start.4 = (f32[40,8,128]{2,1,0:T(8,128)S(1)}, f32[40,8,128]{2,1,0:T(8,128)S(1)}, u32[]{:S(2)}, u32[]{:S(2)}) collective-permute-start(f32[40,8,128]{2,1,0:T(8,128)S(1)} %get-tuple-element.44), channel_id=1, source_target_pairs={{32,0},{64,32},{96,64},{33,1},{65,33},{97,65},{34,2},{66,34},{98,6... | collective-permute-start | bytes 491528 | tf_op jit(solution)/shard_map/ppermute | solution.py:616
  28.5 8.9 %collective-permute-start.5 = (f32[36,8,128]{2,1,0:T(8,128)S(1)}, f32[36,8,128]{2,1,0:T(8,128)S(1)}, u32[]{:S(2)}, u32[]{:S(2)}) collective-permute-start(f32[36,8,128]{2,1,0:T(8,128)S(1)} %get-tuple-element.45), channel_id=1, source_target_pairs={{0,32},{32,64},{64,96},{1,33},{33,65},{65,97},{2,34},{34,66},{66,9... | collective-permute-start | bytes 442376 | tf_op jit(solution)/shard_map/ppermute | solution.py:616
  39.3 5.3 %collective-permute-start.6 = (f32[4,8,128]{2,1,0:T(8,128)S(1)}, f32[4,8,128]{2,1,0:T(8,128)S(1)}, u32[]{:S(2)}, u32[]{:S(2)}) collective-permute-start(f32[4,8,128]{2,1,0:T(8,128)S(1)} %get-tuple-element.47), channel_id=1, source_target_pairs={{0,1},{1,2},{2,3},{4,5},{5,6},{6,7},{8,9},{9,10},{10,11},{12,13},{... | collective-permute-start | bytes 49160 | tf_op jit(solution)/shard_map/ppermute | solution.py:616
  43.1 5.6 %collective-permute-start.7 = (f32[4,8,128]{2,1,0:T(8,128)S(1)}, f32[4,8,128]{2,1,0:T(8,128)S(1)}, u32[]{:S(2)}, u32[]{:S(2)}) collective-permute-start(f32[4,8,128]{2,1,0:T(8,128)S(1)} %get-tuple-element.48), channel_id=1, source_target_pairs={{1,0},{2,1},{3,2},{5,4},{6,5},{7,6},{9,8},{10,9},{11,10},{13,12},{... | collective-permute-start | bytes 49160 | tf_op jit(solution)/shard_map/ppermute | solution.py:616
  51.2 4.7 %collective-permute-start.8 = (f32[24,8,128]{2,1,0:T(8,128)S(1)}, f32[24,8,128]{2,1,0:T(8,128)S(1)}, u32[]{:S(2)}, u32[]{:S(2)}) collective-permute-start(f32[24,8,128]{2,1,0:T(8,128)S(1)} %get-tuple-element.53), channel_id=1, source_target_pairs={{0,4},{4,8},{8,12},{12,16},{16,20},{20,24},{24,28},{1,5},{5,9},{9,... | collective-permute-start | bytes 294920 | tf_op jit(solution)/shard_map/ppermute | solution.py:616
  54.6 4.7 %collective-permute-start.9 = (f32[24,8,128]{2,1,0:T(8,128)S(1)}, f32[24,8,128]{2,1,0:T(8,128)S(1)}, u32[]{:S(2)}, u32[]{:S(2)}) collective-permute-start(f32[24,8,128]{2,1,0:T(8,128)S(1)} %get-tuple-element.54), channel_id=1, source_target_pairs={{4,0},{8,4},{12,8},{16,12},{20,16},{24,20},{28,24},{5,1},{9,5},{13... | collective-permute-start | bytes 294920 | tf_op jit(solution)/shard_map/ppermute | solution.py:616
  59.5 13.7 %collective-permute-start.10 = (f32[40,8,128]{2,1,0:T(8,128)S(1)}, f32[40,8,128]{2,1,0:T(8,128)S(1)}, u32[]{:S(2)}, u32[]{:S(2)}) collective-permute-start(f32[40,8,128]{2,1,0:T(8,128)S(1)} %get-tuple-element.56), channel_id=1, source_target_pairs={{32,0},{64,32},{96,64},{33,1},{65,33},{97,65},{34,2},{66,34},{98,6... | collective-permute-start | bytes 491528 | tf_op jit(solution)/shard_map/ppermute | solution.py:616
  60.8 12.4 %collective-permute-start.11 = (f32[32,8,128]{2,1,0:T(8,128)S(1)}, f32[32,8,128]{2,1,0:T(8,128)S(1)}, u32[]{:S(2)}, u32[]{:S(2)}) collective-permute-start(f32[32,8,128]{2,1,0:T(8,128)S(1)} %get-tuple-element.57), channel_id=1, source_target_pairs={{0,32},{32,64},{64,96},{1,33},{33,65},{65,97},{2,34},{34,66},{66,9... | collective-permute-start | bytes 393224 | tf_op jit(solution)/shard_map/ppermute | solution.py:616
  76.0 3.6 %collective-permute-start.12 = (f32[8,128]{1,0:T(8,128)S(1)}, f32[8,128]{1,0:T(8,128)S(1)}, u32[]{:S(2)}, u32[]{:S(2)}) collective-permute-start(f32[8,128]{1,0:T(8,128)S(1)} %k_gram2.1), channel_id=1, source_target_pairs={{0,4},{4,0},{8,12},{12,8},{16,20},{20,16},{24,28},{28,24},{1,5},{5... | collective-permute-start | bytes 12296 | tf_op jit(solution)/shard_map/ppermute | solution.py:624
  79.6 3.6 %collective-permute-start.13 = (f32[8,128]{1,0:T(8,128)S(1)}, f32[8,128]{1,0:T(8,128)S(1)}, u32[]{:S(2)}, u32[]{:S(2)}) collective-permute-start(f32[8,128]{1,0:T(8,128)S(1)} %add.21), channel_id=1, source_target_pairs={{0,8},{4,12},{8,0},{12,4},{16,24},{20,28},{24,16},{28,20},{1,9},{5... | collective-permute-start | bytes 12296 | tf_op jit(solution)/shard_map/ppermute | solution.py:624
  83.2 5.1 %collective-permute-start.14 = (f32[8,128]{1,0:T(8,128)S(1)}, f32[8,128]{1,0:T(8,128)S(1)}, u32[]{:S(2)}, u32[]{:S(2)}) collective-permute-start(f32[8,128]{1,0:T(8,128)S(1)} %add.22), channel_id=1, source_target_pairs={{0,16},{4,20},{8,24},{12,28},{16,0},{20,4},{24,8},{28,12},{1,17},{... | collective-permute-start | bytes 12296 | tf_op jit(solution)/shard_map/ppermute | solution.py:624
  88.3 3.6 %collective-permute-start.15 = (f32[8,128]{1,0:T(8,128)S(1)}, f32[8,128]{1,0:T(8,128)S(1)}, u32[]{:S(2)}, u32[]{:S(2)}) collective-permute-start(f32[8,128]{1,0:T(8,128)S(1)} %add.23), channel_id=1, source_target_pairs={{0,32},{32,0},{64,96},{96,64},{1,33},{33,1},{65,97},{97,65},{2,34}... | collective-permute-start | bytes 12296 | tf_op jit(solution)/shard_map/ppermute | solution.py:624
  91.9 5.1 %collective-permute-start.16 = (f32[8,128]{1,0:T(8,128)S(1)}, f32[8,128]{1,0:T(8,128)S(1)}, u32[]{:S(2)}, u32[]{:S(2)}) collective-permute-start(f32[8,128]{1,0:T(8,128)S(1)} %add.24), channel_id=1, source_target_pairs={{0,64},{32,96},{64,0},{96,32},{1,65},{33,97},{65,1},{97,33},{2,66}... | collective-permute-start | bytes 12296 | tf_op jit(solution)/shard_map/ppermute | solution.py:624
  97.0 3.6 %collective-permute-start.17 = (f32[8,128]{1,0:T(8,128)S(1)}, f32[8,128]{1,0:T(8,128)S(1)}, u32[]{:S(2)}, u32[]{:S(2)}) collective-permute-start(f32[8,128]{1,0:T(8,128)S(1)} %add.25), channel_id=1, source_target_pairs={{0,1},{1,0},{2,3},{3,2},{4,5},{5,4},{6,7},{7,6},{8,9},{9,8},{10,11... | collective-permute-start | bytes 12296 | tf_op jit(solution)/shard_map/ppermute | solution.py:624
  100.6 5.1 %collective-permute-start.18 = (f32[8,128]{1,0:T(8,128)S(1)}, f32[8,128]{1,0:T(8,128)S(1)}, u32[]{:S(2)}, u32[]{:S(2)}) collective-permute-start(f32[8,128]{1,0:T(8,128)S(1)} %add.26), channel_id=1, source_target_pairs={{0,2},{1,3},{2,0},{3,1},{4,6},{5,7},{6,4},{7,5},{8,10},{9,11},{10,... | collective-permute-start | bytes 12296 | tf_op jit(solution)/shard_map/ppermute | solution.py:624
  102.8 3.0 %copy-start.3 = (f32[8,16,32,128]{3,2,1,0:T(8,128)S(1)}, f32[8,16,32,128]{3,2,1,0:T(8,128)}, u32[]{:S(2)}) copy-start(f32[8,16,32,128]{3,2,1,0:T(8,128)} %r0.1) | copy-start | bytes 6291460

commit v2 on v1

v2 whole, which is shorter than its diff:
```python
import jax
import jax.numpy as jnp
from jax import lax
from jax.experimental import pallas as pl
from jax.experimental.pallas import tpu as pltpu
from jax.sharding import PartitionSpec as P

F32 = jnp.float32
X, Y, Z, F = 16, 32, 128, 8
FORWARD = [
    (a, b, c) for a in (-1, 0, 1) for b in (-1, 0, 1) for c in (-1, 0, 1) if (a, b, c) > (0, 0, 0)
]
OFF = {k + 1: o for k, o in enumerate(FORWARD)}
ZPLUS = [k for k in OFF if OFF[k][2] == 1]
ZMINUS = [k for k in OFF if OFF[k][2] == -1]
YPLUS = [k for k in OFF if OFF[k][1] == 1]
YMINUS = [k for k in OFF if OFF[k][1] == -1]
XPLUS = [k for k in OFF if OFF[k][0] == 1]
ZSHIFTED = ZPLUS + ZMINUS
WZ_AT = {k: i for i, k in enumerate(ZSHIFTED)}
PAIRS = tuple(zip(ZPLUS, ZMINUS + [None]))
GROUPS = ((0, 1), (1, -1), (1, 0), (1, 1))
SHIFT_AT = {0: 0, -1: 1, 1: 2}

VSPEC = pl.BlockSpec(memory_space=pltpu.VMEM)
HSPEC = pl.BlockSpec(memory_space=pl.ANY)
MIB = 1024 * 1024


def call(body, name, ins, outs, after=(), aliases=None, scratch=(), in_specs=None, out_specs=None, limit=8):
    count = len(ins)

    def run(*refs):
        body(*refs[:count], *refs[count + len(after):])

    return pl.pallas_call(
        run,
        name=name,
        out_shape=[jax.ShapeDtypeStruct(s, F32) for s in outs],
        in_specs=(in_specs or [VSPEC] * count) + [HSPEC] * len(after),
        out_specs=out_specs or [VSPEC] * len(outs),
        input_output_aliases=aliases or {},
        scratch_shapes=list(scratch),
        compiler_params=pltpu.CompilerParams(vmem_limit_bytes=limit * MIB),
    )(*ins, *after)


def lanes():
    return lax.broadcasted_iota(jnp.int32, (8, 128), 1)


def rows():
    return lax.broadcasted_iota(jnp.int32, (8, 128), 0)


def roll(v, shift):
    shift %= 128
    return pltpu.roll(v, shift, axis=1) if shift else v


def spot(x, y):
    return (x % 4) * 32 + y


def with_ends(value, ends):
    before = roll(jnp.where(lanes() == 127, ends, value), 1)
    after = roll(jnp.where(lanes() == 0, ends, value), -1)
    return before, after


def clear_if(condition, *outs):
    @pl.when(condition)
    def _():
        for ref in outs:
            ref[...] = jnp.zeros(ref.shape, F32)


def at_first(axis):
    return lax.axis_index(axis) == 0


def at_last(axis):
    return lax.axis_index(axis) == lax.axis_size(axis) - 1


def pack_group(field, g, zp, zm):
    high = jnp.zeros((8, 128), F32)
    low = jnp.zeros((8, 128), F32)
    for xx in range(4):
        for y in range(Y):
            at = spot(xx, y)
            v = roll(field[4 * g + xx, y], at + 1)
            high = jnp.where(lanes() == at, v, high)
            low = jnp.where(lanes() == (at + 1) % 128, v, low)
    zp[g] = high
    zm[g] = low


def pack_columns(field, zp, zm):
    def group(g, carry):
        pack_group(field, g, zp, zm)
        return carry

    lax.fori_loop(0, 4, group, 0)


def start_kernel(rhs, stencil, rc, st, vi, zp, zm, sem_r, sem_s):
    def part(g):
        at = pl.ds(4 * g, 4)
        return pltpu.make_async_copy(rhs.at[:, at], rc.at[:, at], sem_r.at[g])

    def field(k):
        return pltpu.make_async_copy(stencil.at[k], st.at[k], sem_s.at[k])

    order = [k for pair in PAIRS for k in pair if k is not None]
    order += [k for k in range(14) if k not in order]
    for g in range(4):
        part(g).start()
    for k in order:
        field(k).start()

    def group(g, carry):
        part(g).wait()
        for xx in range(4):
            x = 4 * g + xx
            for yb in range(4):
                vi[x, pl.ds(8 * yb, 8)] = jnp.swapaxes(rc[:, x, pl.ds(8 * yb, 8), :], 0, 1)
        pack_group(vi, g, zp, zm)
        return carry

    lax.fori_loop(0, 4, group, 0)
    for k in order:
        field(k).wait()
    for j, (up, down) in enumerate(PAIRS):
        out = jnp.zeros((8, 128), F32)
        for x in range(X):
            for yb in range(4):
                at = 8 * x + 2 * yb
                w = st[up, x, pl.ds(8 * yb, 8), :]
                if down is not None:
                    w = jnp.where(lanes() == 0, st[down, x, pl.ds(8 * yb, 8), :], w)
                out = jnp.where((lanes() == at) | (lanes() == at + 1), roll(w, at + 1), out)
        zp[4 + j] = out
        zm[4 + j] = out
    clear_if(at_last("gz"), zp)
    clear_if(at_first("gz"), zm)


def even():
    return (lanes() & 1) == 0


def merged(rl, rr, g):
    left, right = rl[g], rr[g]
    return jnp.where(even(), left, right), jnp.where(even(), right, left)


def ends_of(pair, at):
    return roll(pair[at % 2], -(at + 1))


def shift_fields(vi, rl, rr, vm, vp):
    def group(g, carry):
        pair = merged(rl, rr, g)
        for xx in range(4):
            for part in range(0, Y, 16):
                ys = range(part, part + 16)
                ends = [ends_of(pair, spot(xx, y)) for y in ys]
                for y, end in zip(ys, ends):
                    before, after = with_ends(vi[4 * g + xx, y], end)
                    vm[4 * g + xx, y] = before
                    vp[4 * g + xx, y] = after
        return carry

    lax.fori_loop(0, 4, group, 0)


def shifted_couplings(st, ends, j, spots):
    up, down = PAIRS[j]
    tiles = [roll(ends[j], -(8 * x + 2 * yb + 1)) for x, yb in spots]
    result = []
    for tile, (x, yb) in zip(tiles, spots):
        w = st[up, x, pl.ds(8 * yb, 8), :]
        moved = {up: roll(jnp.where(lanes() == 127, tile, w), 1)}
        if down is not None:
            w = st[down, x, pl.ds(8 * yb, 8), :]
            moved[down] = roll(jnp.where(lanes() == 0, tile, w), -1)
        result.append(moved)
    return result


def edge_rows(vi, rl, rr, yp, ym):
    for x in range(X):
        yp[x] = vi[x, Y - 1]
        ym[x] = vi[x, 0]
    for g in range(4):
        for i, tile in enumerate(merged(rl, rr, g)):
            yp[16 + 2 * g + i] = tile
            ym[16 + 2 * g + i] = tile


def coupling_ends(rl, rr):
    return [jnp.where(even(), rl[4 + j], rr[4 + j]) for j in range(5)]


def edge_kernel(vi, st, rl, rr, yp, ym):
    edge_rows(vi, rl, rr, yp, ym)
    ends = coupling_ends(rl, rr)
    for ref, keys, y in ((yp, YPLUS, Y - 1), (ym, YMINUS, 0)):
        rows_of = {}
        for j, pair in enumerate(PAIRS):
            if pair[0] in keys or pair[1] in keys:
                moved = shifted_couplings(st, ends, j, [(x, y // 8) for x in range(X)])
                for x in range(X):
                    rows_of.update({(k, x): tile for k, tile in moved[x].items()})
        for i, k in enumerate(keys):
            for x in range(X):
                r = 16 * i + x
                if k in WZ_AT:
                    row = rows_of[k, x][y % 8 : y % 8 + 1, :]
                else:
                    row = st[k, x, pl.ds(y, 1), :]
                ref[24 + r // 8, pl.ds(r % 8, 1), :] = row
    clear_if(at_last("gy"), yp)
    clear_if(at_first("gy"), ym)


def edge_again_kernel(vi, rl, rr, yp, ym):
    edge_rows(vi, rl, rr, yp, ym)
    clear_if(at_last("gy"), yp)
    clear_if(at_first("gy"), ym)


def shift_kernel(vi, st, rl, rr, vm, vp, wz, sums):
    shift_fields(vi, rl, rr, vm, vp)
    ends = coupling_ends(rl, rr)
    for j in range(5):
        for x in range(0, X, 4):
            spots = [(x + i, yb) for i in range(4) for yb in range(4)]
            for (xx, yb), moved in zip(spots, shifted_couplings(st, ends, j, spots)):
                for k, tile in moved.items():
                    wz[WZ_AT[k], xx, pl.ds(8 * yb, 8), :] = tile

    def behind(k, x, yb):
        if k in WZ_AT:
            return wz[WZ_AT[k], x, pl.ds(8 * yb, 8), :]
        return st[k, x, pl.ds(8 * yb, 8), :]

    def add_up(x, carry):
        for yb in range(4):
            total = st[0, x, pl.ds(8 * yb, 8), :]
            for k in OFF:
                total = total + st[k, x, pl.ds(8 * yb, 8), :]
            sums[4, x, pl.ds(8 * yb, 8), :] = total + behind(1, x, yb)
            for i, (a, b) in enumerate(GROUPS):
                keys = [k for k in OFF if OFF[k][:2] == (a, b)]
                sums[i, x, pl.ds(8 * yb, 8), :] = (
                    behind(keys[0], x, yb) + behind(keys[1], x, yb) + behind(keys[2], x, yb)
                )
        return carry

    lax.fori_loop(0, X, add_up, 0)


def behind_row(st, wz, k, x, y):
    if k in WZ_AT:
        return wz[WZ_AT[k], x, pl.ds(y, 1), :]
    return st[k, x, pl.ds(y, 1), :]


def wide(row):
    return jnp.broadcast_to(row, (8, 128))


def plane(x, first, last, fields, st, wz, acc_ref, at, diag_of):
    cache = {}

    def v(s, dx, y):
        key = (s, dx, y)
        if key not in cache:
            cache[key] = fields[SHIFT_AT[s]][x + dx, y]
        return cache[key]

    coef = {}

    def ahead(k, y):
        if OFF[k][2] == 0:
            if (k, 0, y) not in coef:
                coef[k, 0, y] = wide(st[k, x, pl.ds(y, 1), :])
            return coef[k, 0, y]
        return wide(st[k, x, pl.ds(y, 1), :])

    def behind(k, a, y):
        if k not in WZ_AT:
            if (k, a, y) not in coef:
                coef[k, a, y] = wide(st[k, x - a, pl.ds(y, 1), :])
            return coef[k, a, y]
        return wide(wz[WZ_AT[k], x - a, pl.ds(y, 1), :])

    for y in range(Y):
        parts = [None, None]
        n = 0
        for k, (a, b, c) in OFF.items():
            if 0 <= y + b < Y and not (a == 1 and last):
                term = ahead(k, y) * v(c, a, y + b)
                parts[n % 2] = term if parts[n % 2] is None else parts[n % 2] + term
                n += 1
            if 0 <= y - b < Y and not (a == 1 and first):
                term = behind(k, a, y - b) * v(-c, -a, y - b)
                parts[n % 2] = term if parts[n % 2] is None else parts[n % 2] + term
                n += 1
        acc_ref[at, y] = wide(diag_of(x, y, first)) * v(0, 0, y) - (parts[0] + parts[1])


def interior(fields, st, wz, acc_ref, diag_of):
    plane(0, True, False, fields, st, wz, acc_ref, 0, diag_of)

    def step(x, carry):
        plane(x, False, False, fields, st, wz, acc_ref, x, diag_of)
        return carry

    lax.fori_loop(1, X - 1, step, 0)
    plane(X - 1, False, True, fields, st, wz, acc_ref, X - 1, diag_of)


def inner_kernel(vi, vm, vp, st, wz, sums, acc, diag):
    def diag_of(x, y, first):
        total = sums[4, x, pl.ds(y, 1), :]
        if y > 0:
            total = total + sums[0, x, pl.ds(y - 1, 1), :]
        if not first:
            total = total + sums[2, x - 1, pl.ds(y, 1), :]
            if y > 0:
                total = total + sums[3, x - 1, pl.ds(y - 1, 1), :]
            if y < Y - 1:
                total = total + sums[1, x - 1, pl.ds(y + 1, 1), :]
        diag[x, pl.ds(y, 1), :] = total
        return total

    interior((vi, vm, vp), st, wz, acc, diag_of)


def inner_again_kernel(vi, vm, vp, st, wz, diag, acc):
    interior((vi, vm, vp), st, wz, acc, lambda x, y, first: diag[x, pl.ds(y, 1), :])


def ring_row(ref, keys, k, x):
    r = 16 * keys.index(k) + x
    return ref[24 + r // 8, pl.ds(r % 8, 1), :]


def third_kernel(with_diag):
    def body(*refs):
        if with_diag:
            vi, vm, vp, st, wz, rl, rr, qm, qp, sums, ring, xm, xp = refs
            qmw, qpw = qm, qp
        else:
            vi, vm, vp, st, wz, rl, rr, qm, qp, qmw, qpw, ring, xm, xp = refs
        for side, q, y in ((0, qm, Y - 1), (1, qp, 0)):
            for x in range(X):
                g = 16 + 2 * (x // 4)
                before, after = with_ends(q[x], ends_of((q[g], q[g + 1]), spot(x, y)))
                ring[side, 0, x] = q[x]
                ring[side, 1, x] = before
                ring[side, 2, x] = after
        xm[0] = qm[0]
        for y in range(Y):
            xm[1 + y] = vi[0, y]
        xm[Y + 1] = qp[0]
        for i, tile in enumerate((*merged(rl, rr, 0), qm[16], qm[17], qp[16], qp[17])):
            xm[Y + 2 + i] = tile
        last = X - 1
        for y in range(Y):
            total = None
            for k in XPLUS:
                _, b, c = OFF[k]
                s = SHIFT_AT[-c]
                if y - b < 0:
                    term = wide(ring_row(qmw, YPLUS, k, last)) * ring[0, s, last]
                elif y - b >= Y:
                    term = wide(ring_row(qpw, YMINUS, k, last)) * ring[1, s, last]
                else:
                    term = wide(behind_row(st, wz, k, last, y - b)) * (vi, vm, vp)[s][last, y - b]
                total = term if total is None else total + term
            xp[y] = total
            if with_diag:
                row = sums[2, last, pl.ds(y, 1), :]
                if y > 0:
                    row = row + sums[3, last, pl.ds(y - 1, 1), :]
                else:
                    for k in (11, 12, 13):
                        row = row + ring_row(qmw, YPLUS, k, last)
                if y < Y - 1:
                    row = row + sums[1, last, pl.ds(y + 1, 1), :]
                else:
                    for k in (5, 6, 7):
                        row = row + ring_row(qpw, YMINUS, k, last)
                xp[Y + y // 8, pl.ds(y % 8, 1), :] = row
        clear_if(at_first("gx"), xm)
        clear_if(at_last("gx"), xp)

    return body


def finish_edges(acc, st, ring, qmw, qpw, tp, tm, extra):
    last = X - 1
    far = {}

    def far_at(s, y):
        if (0, y) not in far:
            base, at = (Y + 2, y) if 0 <= y < Y else ((Y + 4, Y - 1) if y < 0 else (Y + 6, 0))
            far[0, y] = tp[y + 1]
            far[-1, y], far[1, y] = with_ends(tp[y + 1], ends_of((tp[base], tp[base + 1]), at))
        return far[s, y]

    for x in range(X):
        for y in range(Y) if x in (0, last) else (0, Y - 1):
            total = None
            for k, (a, b, c) in OFF.items():
                terms = []
                if x + a == X:
                    terms.append(wide(st[k, x, pl.ds(y, 1), :]) * far_at(c, y + b))
                elif y + b < 0:
                    terms.append(wide(st[k, x, pl.ds(y, 1), :]) * ring[0, SHIFT_AT[c], x + a])
                elif y + b >= Y:
                    terms.append(wide(st[k, x, pl.ds(y, 1), :]) * ring[1, SHIFT_AT[c], x + a])
                if x - a >= 0:
                    if y - b < 0:
                        terms.append(
                            wide(ring_row(qmw, YPLUS, k, x - a)) * ring[0, SHIFT_AT[-c], x - a]
                        )
                    elif y - b >= Y:
                        terms.append(
                            wide(ring_row(qpw, YMINUS, k, x - a)) * ring[1, SHIFT_AT[-c], x - a]
                        )
                for term in terms:
                    total = term if total is None else total + term
            if x == 0:
                total = tm[y] if total is None else total + tm[y]
            value = acc[x, y] - total
            fix = extra(x, y) if extra is not None else None
            acc[x, y] = value if fix is None else value + fix


def join_kernel(acc_in, diag_in, vi, st, ring, qm, qp, tp, tm, acc, diag, zp, zm):
    def fix(x, y):
        row = None
        if y == 0:
            for k in (2, 3, 4):
                r = ring_row(qm, YPLUS, k, x)
                row = r if row is None else row + r
            if x > 0:
                for k in (11, 12, 13):
                    row = row + ring_row(qm, YPLUS, k, x - 1)
        if y == Y - 1 and x > 0:
            for k in (5, 6, 7):
                r = ring_row(qp, YMINUS, k, x - 1)
                row = r if row is None else row + r
        if x == 0:
            r = tm[Y + y // 8, pl.ds(y % 8, 1), :]
            row = r if row is None else row + r
        if row is None:
            return None
        diag[x, pl.ds(y, 1), :] = diag[x, pl.ds(y, 1), :] + row
        return wide(row) * vi[x, y]

    finish_edges(acc, st, ring, qm, qp, tp, tm, fix)
    pack_columns(acc, zp, zm)
    clear_if(at_last("gz"), zp)
    clear_if(at_first("gz"), zm)


def turn_flat(v, out, x):
    for yb in range(4):
        out[:, x, pl.ds(8 * yb, 8), :] = jnp.swapaxes(v[x, pl.ds(8 * yb, 8)], 0, 1)


def flat_kernel(v, out):
    def turn(x, carry):
        turn_flat(v, out, x)
        return carry

    lax.fori_loop(0, X, turn, 0)


PRODUCTS = [(i, j) for i in range(8) for j in range(i, 8)]


def gram(u, v):
    def step(n, carry):
        x, at = n // 4, pl.ds((n % 4) * 8, 8)
        a = [u[i, x, at, :] for i in range(8)]
        b = a if v is u else [v[i, x, at, :] for i in range(8)]
        return tuple(c + a[i] * b[j] for c, (i, j) in zip(carry, PRODUCTS))

    return lax.fori_loop(0, 4 * X, step, tuple(jnp.zeros((8, 128), F32) for _ in PRODUCTS))


def place(tile, sums, m):
    held = dict(zip(PRODUCTS, sums))
    held = {p: jnp.sum(s, axis=1, keepdims=True) for p, s in held.items()}
    for i in range(8):
        row = jnp.zeros((8, 128), F32)
        for j in range(8):
            row = jnp.where(lanes() == 8 * m + j, held[min(i, j), max(i, j)], row)
        row = jnp.broadcast_to(jnp.sum(row, axis=0, keepdims=True), (8, 128))
        mine = (rows() == i) & (lanes() >= 8 * m) & (lanes() < 8 * m + 8)
        tile = jnp.where(mine, row, tile)
    return tile


def gram_first_kernel(r0, out):
    out[...] = place(jnp.zeros((8, 128), F32), gram(r0, r0), 0)


def gram_second_kernel(r0, y1, early, flat, out):
    flat_kernel(y1, flat)
    tile = place(early[...], gram(r0, flat), 1)
    out[...] = place(tile, gram(flat, flat), 2)


def late_kernel(acc_in, st, ring, qm, qp, tp, tm, y1, early, acc, flat, out):
    finish_edges(acc, st, ring, qm, qp, tp, tm, None)
    flat_kernel(acc, flat)
    out[...] = place(early[...], gram(y1, flat), 3)


def differences_kernel(r0, y1, y2, d0, d1):
    def step(x, carry):
        for i in range(8):
            d0[i, x] = r0[i, x] - y1[i, x]
            d1[i, x] = y1[i, x] - y2[i, x]
        return carry

    lax.fori_loop(0, X, step, 0)


def entry(col, i):
    return jnp.broadcast_to(col[i : i + 1, :], (8, 128))


def times(left, right):
    result = []
    for j in range(8):
        total = None
        for k in range(8):
            term = left[k] * entry(right[j], k)
            total = term if total is None else total + term
        result.append(total)
    return result


def flip(m):
    result = []
    for j in range(8):
        out = entry(m[0], j)
        for i in range(1, 8):
            out = jnp.where(rows() == i, entry(m[i], j), out)
        result.append(out)
    return result


def plus(left, right):
    return [a + b for a, b in zip(left, right)]


def minus(left, right):
    return [a - b for a, b in zip(left, right)]


def solve(matrix, right):
    a = list(matrix)
    r = list(right)
    for k in range(8):
        inverse = 1.0 / entry(a[k], k)
        here = rows() == k
        for cols, js in ((a, range(k + 1, 8)), (r, range(8))):
            for j in js:
                f = entry(cols[j], k) * inverse
                cols[j] = jnp.where(here, f, cols[j] - a[k] * f)
    return r


def moments(tile, m):
    return [jnp.broadcast_to(tile[:, 8 * m + j : 8 * m + j + 1], (8, 128)) for j in range(8)]


def coefficients(tile):
    m0, m1, m2, m3 = (moments(tile, m) for m in range(4))
    eye = [jnp.where(rows() == j, 1.0, 0.0) for j in range(8)]
    alpha = solve(m1, m0)
    inverse = solve(m0, eye)
    alpha_t = flip(alpha)
    m2a = times(m2, alpha)
    first = times(m1, alpha)
    rr1 = plus(minus(minus(m0, first), flip(first)), times(alpha_t, m2a))
    big = plus(eye, times(inverse, rr1))
    pq = plus(
        times(flip(big), minus(times(m1, big), m2a)),
        times(alpha_t, minus(times(m3, alpha), times(m2, big))),
    )
    alpha2 = solve(pq, rr1)
    return plus(alpha, times(big, alpha2)), times(alpha, alpha2)


def last_kernel(tile_ref, r0, y1, d0, d1, sol, res, coef, sbuf, rbuf, sems):
    c1, c2 = coefficients(tile_ref[...])
    for j in range(8):
        coef[0, j] = c1[j]
        coef[1, j] = c1[j] - c2[j]
        coef[2, j] = c2[j]

    def tile_out(x, yb):
        at = pl.ds(8 * yb, 8)
        a = [d0[i, x, at, :] for i in range(8)]
        b = [y1[i, x, at, :] for i in range(8)]
        c = [d1[i, x, at, :] for i in range(8)]
        for j in range(8):
            sums = []
            for m, field in enumerate((a, b, c)):
                total = None
                for i in range(8):
                    term = wide(coef[m, j, pl.ds(i, 1), :]) * field[i]
                    total = term if total is None else total + term
                sums.append(total)
            sbuf[j, x, at, :] = sums[0] + sums[1]
            rbuf[j, x, at, :] = r0[j, x, at, :] - (sums[1] + sums[2])

    def copy(n, src, dst, which):
        part = pl.ds(n * 2, 2)
        return pltpu.make_async_copy(src.at[:, part], dst.at[:, part], sems.at[which, n])

    def step(n, carry):
        def inner(t, c):
            tile_out(n * 2 + t // 4, t % 4)
            return c

        lax.fori_loop(0, 8, inner, 0)
        copy(n, sbuf, sol, 0).start()
        copy(n, rbuf, res, 1).start()
        return carry

    lax.fori_loop(0, X // 2, step, 0)
    for n in range(X // 2):
        copy(n, sbuf, sol, 0).wait()
        copy(n, rbuf, res, 1).wait()


def shift(x, axis, step):
    n = lax.axis_size(axis)
    return lax.ppermute(x, axis, [(i, (i + step) % n) for i in range(n)])


def everywhere(x):
    for axis, bits in (("gy", (1, 2, 6)), ("gx", (1, 3)), ("gz", (1, 3))):
        n = lax.axis_size(axis)
        for bit in bits:
            x = x + lax.ppermute(x, axis, [(i, i ^ bit) for i in range(n)])
    return x


def shards(rhs, stencil):
    full = (X, Y, F, Z)
    compact = (F, X, Y, Z)
    tile = (8, 128)
    dma = pltpu.SemaphoreType.DMA
    rc, st, vi, zp, zm = call(
        start_kernel, "k_start", [rhs, stencil],
        [compact, (14, X, Y, Z), full, (9, *tile), (9, *tile)],
        in_specs=[HSPEC] * 2, scratch=[dma((4,)), dma((14,))],
    )
    rl = shift(zp, "gz", 1)
    rr = shift(zm, "gz", -1)
    (g0,) = call(gram_first_kernel, "k_gram0", [rc], [tile])
    yp, ym = call(edge_kernel, "k_edge", [vi, st, rl, rr], [(36, *tile), (30, *tile)], after=[g0])
    qm = shift(yp, "gy", 1)
    qp = shift(ym, "gy", -1)
    vm, vp, wz, sums = call(
        shift_kernel, "k_shift", [vi, st, rl, rr], [full, full, (9, X, Y, Z), (5, X, Y, Z)]
    )
    ring, xm, xp = call(
        third_kernel(True), "k_third", [vi, vm, vp, st, wz, rl, rr, qm, qp, sums],
        [(2, 3, X, *tile), (Y + 8, *tile), (Y + 4, *tile)],
    )
    tp = shift(xm, "gx", -1)
    tm = shift(xp, "gx", 1)
    acc, diag = call(inner_kernel, "k_inner", [vi, vm, vp, st, wz, sums], [full, (X, Y, Z)])
    y1, diag, zp, zm = call(
        join_kernel, "k_join", [acc, diag, vi, st, ring, qm, qp, tp, tm],
        [full, (X, Y, Z), (4, *tile), (4, *tile)], aliases={0: 0, 1: 1},
    )

    rl = shift(zp, "gz", 1)
    rr = shift(zm, "gz", -1)
    y1f, g2 = call(gram_second_kernel, "k_gram12", [rc, y1, g0], [compact, tile])
    yp, ym = call(
        edge_again_kernel, "k_edge2", [y1, rl, rr], [(24, *tile), (24, *tile)], after=[g2]
    )
    qmv = shift(yp, "gy", 1)
    qpv = shift(ym, "gy", -1)
    vm, vp = call(shift_fields, "k_shift2", [y1, rl, rr], [full, full])
    ring, xm, xp = call(
        third_kernel(False), "k_third2", [y1, vm, vp, st, wz, rl, rr, qmv, qpv, qm, qp],
        [(2, 3, X, *tile), (Y + 8, *tile), (Y, *tile)],
    )
    tp = shift(xm, "gx", -1)
    tm = shift(xp, "gx", 1)
    (acc,) = call(inner_again_kernel, "k_inner2", [y1, vm, vp, st, wz, diag], [full])
    _, y2f, moment = call(
        late_kernel, "k_late", [acc, st, ring, qm, qp, tp, tm, y1f, g2],
        [full, compact, tile], aliases={0: 0},
    )
    d0, d1 = call(differences_kernel, "k_diff", [rc, y1f, y2f], [compact, compact])
    moment = everywhere(moment)
    sol, res = call(
        last_kernel, "k_last", [moment, rc, y1f, d0, d1], [compact, compact],
        out_specs=[HSPEC, HSPEC],
        scratch=[
            pltpu.VMEM((3, 8, *tile), F32),
            pltpu.VMEM(compact, F32),
            pltpu.VMEM(compact, F32),
            dma((2, X // 2)),
        ],
        limit=14,
    )
    return sol, res


def solution(mesh):
    placed = P(None, "gx", "gy", "gz")
    return jax.shard_map(
        shards, mesh=mesh, in_specs=(placed, placed), out_specs=(placed, placed), check_vma=False
    )
```

time: 115 us -> 89.5 us (0.78)
  starting transfers between devices: 44.9 us -> 23.4 us
  waiting for transfers between devices: 29.2 us -> 25.2 us
    ppermute x12, waiting for transfers between devices: 15.9 us -> 3.66 us  [shift(): return lax.ppermute(x, axis, [(i, (i + step) % n) for i in range(n)])]
    ppermute x7, starting transfers between devices: 15.6 us -> 4.6 us  [everywhere(): x = x + lax.ppermute(x, axis, [(i, i ^ bit) for i in range(n)])]
    ppermute x12, starting transfers between devices: 29.3 us -> 18.9 us  [shift(): return lax.ppermute(x, axis, [(i, (i + step) % n) for i in range(n)])]
    ppermute x7, waiting for transfers between devices: 13.3 us -> 21.5 us  [everywhere(): x = x + lax.ppermute(x, axis, [(i, i ^ bit) for i in range(n)])]
    pallas_call x16 -> x15, Pallas kernels: 35.5 us -> 36.2 us  [call(): pl.pallas_call(run, name=name, out_shape=[jax.ShapeDtypeStruct(s, F32) fo...]
    unnamed x8 -> x4, local copies, waits for them, and re-layouts: 3.63 us -> 3.62 us
  transfers between devices with their start and end apart: 19 -> 19, of which waited for: 12 -> 10; matrix products, arithmetic and copies ran while one was open for 0% -> 0% of each run, Pallas kernels for 11% -> 26%
where the time goes in v2:
time: 89.5 us; the launch traced here: 89.3 us
  Pallas kernels  36.2 us (40%)
  waiting for transfers between devices  25.2 us (28%)
  starting transfers between devices  23.4 us (26%)
  local copies, waits for them, and re-layouts  3.62 us (4%)
    pallas_call x15, Pallas kernels, call(): pl.pallas_call(run, name=name, out_shape=[jax.ShapeDtypeStruct(s, F32) fo...  36.2 us
    ppermute x7, waiting for transfers between devices, everywhere(): x = x + lax.ppermute(x, axis, [(i, i ^ bit) for i in range(n)])  21.5 us
    ppermute x12, starting transfers between devices, shift(): return lax.ppermute(x, axis, [(i, (i + step) % n) for i in range(n)])  18.9 us
    ppermute x7, starting transfers between devices, everywhere(): x = x + lax.ppermute(x, axis, [(i, i ^ bit) for i in range(n)])  4.6 us
    ppermute x12, waiting for transfers between devices, shift(): return lax.ppermute(x, axis, [(i, (i + step) % n) for i in range(n)])  3.66 us
    unnamed x4, local copies, waits for them, and re-layouts  3.62 us
  transfers between devices with their start and end apart: 19, of which 10 were waited for; matrix products, arithmetic and copies ran while one was open for 0% of the time, Pallas kernels for 26%

profile of v2, /device:TPU:0, one launch (start us, length us, event | category | flops | bytes accessed | tf_op | source)
XLA Modules:
  0.0 89.3 jit_solution(3473903753184533034)
XLA Ops:
  0.6 2.0 %copy-done = f32[14,16,32,128]{3,2,1,0:T(8,128)S(1)} copy-done((f32[14,16,32,128]{3,2,1,0:T(8,128)S(1)}, f32[14,16,32,128]{3,2,1,0:T(8,128)}, u32[]{:S(2)}) %copy-start) | copy-done | bytes 3670040
  4.3 1.8 %k_start.1 = (f32[8,16,32,128]{3,2,1,0:T(8,128)S(1)}, f32[14,16,32,128]{3,2,1,0:T(8,128)S(1)}, f32[16,32,8,128]{3,2,1,0:T(8,128)S(1)}, f32[9,8,128]{2,1,0:T(8,128)S(1)}, f32[9,8,128]{2,1,0:T(8,128)S(1)}) custom-call(f32[8,16,32,128]{3,2,1,0:T(8,128)S(1)} %copy-done.1, f32[14,16,32,128]{3,2,1,0:T(8,128)S(1)} %copy-done), custom_call_target="tpu_custom_call" | custom-call | tf_op jit(solution)/shard_map/k_start/pallas_call | solution.py:36
  6.1 2.1 %collective-permute-start = (f32[9,8,128]{2,1,0:T(8,128)S(1)}, f32[9,8,128]{2,1,0:T(8,128)S(1)}, u32[]{:S(2)}, u32[]{:S(2)}) collective-permute-start(f32[9,8,128]{2,1,0:T(8,128)S(1)} %get-tuple-element.37), channel_id=1, source_target_pairs={{0,1},{1,2},{2,3},{3,0},{4,5},{5,6},{6,7},{7,4},{8,9},{9,10},{10,1... | collective-permute-start | bytes 110600 | tf_op jit(solution)/shard_map/ppermute | solution.py:651
  8.2 2.2 %collective-permute-start.1 = (f32[9,8,128]{2,1,0:T(8,128)S(1)}, f32[9,8,128]{2,1,0:T(8,128)S(1)}, u32[]{:S(2)}, u32[]{:S(2)}) collective-permute-start(f32[9,8,128]{2,1,0:T(8,128)S(1)} %get-tuple-element.38), channel_id=1, source_target_pairs={{0,3},{1,0},{2,1},{3,2},{4,7},{5,4},{6,5},{7,6},{8,11},{9,8},{10,9... | collective-permute-start | bytes 110600 | tf_op jit(solution)/shard_map/ppermute | solution.py:651
  10.4 1.8 %k_gram0.1.refs_4_.refs_2_ = f32[8,128]{1,0:T(8,128)S(1)} custom-call(f32[8,16,32,128]{3,2,1,0:T(8,128)S(1)} %get-tuple-element.45.refs_0_.refs_1_), custom_call_target="tpu_custom_call" | custom-call | tf_op jit(solution)/shard_map/k_gram0/pallas_call | solution.py:36
  12.7 2.9 %collective-permute-start.3 = (f32[30,8,128]{2,1,0:T(8,128)S(1)}, f32[30,8,128]{2,1,0:T(8,128)S(1)}, u32[]{:S(2)}, u32[]{:S(2)}) collective-permute-start(f32[30,8,128]{2,1,0:T(8,128)S(1)} %get-tuple-element.47), channel_id=1, source_target_pairs={{0,28},{4,0},{8,4},{12,8},{16,12},{20,16},{24,20},{28,24},{1,29},{... | collective-permute-start | bytes 368648 | tf_op jit(solution)/shard_map/ppermute | solution.py:651
  15.7 5.6 %k_shift.1 = (f32[16,32,8,128]{3,2,1,0:T(8,128)S(1)}, f32[16,32,8,128]{3,2,1,0:T(8,128)S(1)}, f32[9,16,32,128]{3,2,1,0:T(8,128)S(1)}, f32[5,16,32,128]{3,2,1,0:T(8,128)S(1)}) custom-call(f32[16,32,8,128]{3,2,1,0:T(8,128)S(1)} %get-tuple-element.35.refs_0_.refs_2_, f32[14,16,32,128]{3,2,1,0:T(8,128)S(1)} %get-tuple-element.36.refs_1_.refs_3_, ...), custom_call_target="tpu_custom_call" | custom-call | tf_op jit(solution)/shard_map/k_shift/pallas_call | solution.py:36
  21.5 3.1 %collective-permute-start.4 = (f32[40,8,128]{2,1,0:T(8,128)S(1)}, f32[40,8,128]{2,1,0:T(8,128)S(1)}, u32[]{:S(2)}, u32[]{:S(2)}) collective-permute-start(f32[40,8,128]{2,1,0:T(8,128)S(1)} %get-tuple-element.49), channel_id=1, source_target_pairs={{0,96},{32,0},{64,32},{96,64},{1,97},{33,1},{65,33},{97,65},{2,98}... | collective-permute-start | bytes 491528 | tf_op jit(solution)/shard_map/ppermute | solution.py:651
  24.6 4.4 %k_inner.1 = (f32[16,32,8,128]{3,2,1,0:T(8,128)S(1)}, f32[16,32,128]{2,1,0:T(8,128)S(1)}) custom-call(f32[16,32,8,128]{3,2,1,0:T(8,128)S(1)} %get-tuple-element.35.refs_0_.refs_2_, f32[16,32,8,128]{3,2,1,0:T(8,128)S(1)} %get-tuple-element.39.refs_1_, f32[16,32,8,128]{3,2,1,0:T(8,128)S(1)} %get-tuple-element.40.refs_2_, ...), custom_call_target="tpu_custom_call" | custom-call | tf_op jit(solution)/shard_map/k_inner/pallas_call | solution.py:36
  29.0 1.9 %collective-permute-done.5.refs_8_ = f32[36,8,128]{2,1,0:T(8,128)S(1)} collective-permute-done((f32[36,8,128]{2,1,0:T(8,128)S(1)}, f32[36,8,128]{2,1,0:T(8,128)S(1)}, u32[]{:S(2)}, u32[]{:S(2)}) %collective-permute-start.5) | collective-permute-done | bytes 147488 | tf_op jit(solution)/shard_map/ppermute | solution.py:651
  32.2 1.9 %collective-permute-start.6 = (f32[4,8,128]{2,1,0:T(8,128)S(1)}, f32[4,8,128]{2,1,0:T(8,128)S(1)}, u32[]{:S(2)}, u32[]{:S(2)}) collective-permute-start(f32[4,8,128]{2,1,0:T(8,128)S(1)} %get-tuple-element.52), channel_id=1, source_target_pairs={{0,1},{1,2},{2,3},{3,0},{4,5},{5,6},{6,7},{7,4},{8,9},{9,10},{10,1... | collective-permute-start | bytes 49160 | tf_op jit(solution)/shard_map/ppermute | solution.py:651
  35.6 4.1 %k_gram12.1 = (f32[8,16,32,128]{3,2,1,0:T(8,128)S(1)}, f32[8,128]{1,0:T(8,128)S(1)}) custom-call(f32[8,16,32,128]{3,2,1,0:T(8,128)S(1)} %get-tuple-element.45.refs_0_.refs_1_, f32[16,32,8,128]{3,2,1,0:T(8,128)S(1)} %get-tuple-element.51.refs_0_.refs_1_, f32[8,128]{1,0:T(8,128)S(1)} %k_gram0.1.refs_4_.refs_2_), custom_call_target="tpu_custom_call" | custom-call | tf_op jit(solution)/shard_map/k_gram12/pallas_call | solution.py:36
  39.8 2.9 %collective-permute-start.9 = (f32[24,8,128]{2,1,0:T(8,128)S(1)}, f32[24,8,128]{2,1,0:T(8,128)S(1)}, u32[]{:S(2)}, u32[]{:S(2)}) collective-permute-start(f32[24,8,128]{2,1,0:T(8,128)S(1)} %get-tuple-element.59), channel_id=1, source_target_pairs={{0,28},{4,0},{8,4},{12,8},{16,12},{20,16},{24,20},{28,24},{1,29},{... | collective-permute-start | bytes 294920 | tf_op jit(solution)/shard_map/ppermute | solution.py:651
  42.7 3.2 %k_shift2.1 = (f32[16,32,8,128]{3,2,1,0:T(8,128)S(1)}, f32[16,32,8,128]{3,2,1,0:T(8,128)S(1)}) custom-call(f32[16,32,8,128]{3,2,1,0:T(8,128)S(1)} %get-tuple-element.51.refs_0_.refs_1_, f32[4,8,128]{2,1,0:T(8,128)S(1)} %collective-permute-done.6.refs_1_.refs_5_, f32[4,8,128]{2,1,0:T(8,128)S(1)} %collective-permute-done.7.refs_2_.refs_6_), custom_call_target="tpu_custom_call" | custom-call | tf_op jit(solution)/shard_map/k_shift2/pallas_call | solution.py:36
  48.2 3.8 %k_inner2.1.refs_0_ = f32[16,32,8,128]{3,2,1,0:T(8,128)S(1)} custom-call(f32[16,32,8,128]{3,2,1,0:T(8,128)S(1)} %get-tuple-element.51.refs_0_.refs_1_, f32[16,32,8,128]{3,2,1,0:T(8,128)S(1)} %get-tuple-element.54.refs_1_, f32[16,32,8,128]{3,2,1,0:T(8,128)S(1)} %get-tuple-element.55.refs_2_, f32[14,16,32,128]{3,2,1,0:T(8,128)S(1)} %get-tuple-element.36.refs_1_.refs_3_, ...), custom_call_target="tpu_custom_call" | custom-call | tf_op jit(solution)/shard_map/k_inner2/pallas_call | solution.py:36
  53.7 2.6 %k_late.1 = (f32[16,32,8,128]{3,2,1,0:T(8,128)S(1)}, f32[8,16,32,128]{3,2,1,0:T(8,128)S(1)}, f32[8,128]{1,0:T(8,128)S(1)}) custom-call(f32[16,32,8,128]{3,2,1,0:T(8,128)S(1)} %k_inner2.1.refs_0_, f32[14,16,32,128]{3,2,1,0:T(8,128)S(1)} %get-tuple-element.36.refs_1_.refs_3_, ...), custom_call_target="tpu_custom_call", output_to_operand_aliasing={{0}: (0, {})} | custom-call | tf_op jit(solution)/shard_map/k_late/pallas_call | solution.py:36
  57.5 3.6 %collective-permute-done.13 = f32[8,128]{1,0:T(8,128)S(1)} collective-permute-done((f32[8,128]{1,0:T(8,128)S(1)}, f32[8,128]{1,0:T(8,128)S(1)}, u32[]{:S(2)}, u32[]{:S(2)}) %collective-permute-start.13) | collective-permute-done | bytes 4128 | tf_op jit(solution)/shard_map/ppermute | solution.py:658
  62.3 3.6 %collective-permute-done.14 = f32[8,128]{1,0:T(8,128)S(1)} collective-permute-done((f32[8,128]{1,0:T(8,128)S(1)}, f32[8,128]{1,0:T(8,128)S(1)}, u32[]{:S(2)}, u32[]{:S(2)}) %collective-permute-start.14) | collective-permute-done | bytes 4128 | tf_op jit(solution)/shard_map/ppermute | solution.py:658
  66.0 3.6 %collective-permute-done.15 = f32[8,128]{1,0:T(8,128)S(1)} collective-permute-done((f32[8,128]{1,0:T(8,128)S(1)}, f32[8,128]{1,0:T(8,128)S(1)}, u32[]{:S(2)}, u32[]{:S(2)}) %collective-permute-start.15) | collective-permute-done | bytes 4128 | tf_op jit(solution)/shard_map/ppermute | solution.py:658
  70.5 3.9 %collective-permute-done.16 = f32[8,128]{1,0:T(8,128)S(1)} collective-permute-done((f32[8,128]{1,0:T(8,128)S(1)}, f32[8,128]{1,0:T(8,128)S(1)}, u32[]{:S(2)}, u32[]{:S(2)}) %collective-permute-start.16) | collective-permute-done | bytes 4128 | tf_op jit(solution)/shard_map/ppermute | solution.py:658
  74.8 3.2 %collective-permute-done.17 = f32[8,128]{1,0:T(8,128)S(1)} collective-permute-done((f32[8,128]{1,0:T(8,128)S(1)}, f32[8,128]{1,0:T(8,128)S(1)}, u32[]{:S(2)}, u32[]{:S(2)}) %collective-permute-start.17) | collective-permute-done | bytes 4128 | tf_op jit(solution)/shard_map/ppermute | solution.py:658
  78.0 1.9 %collective-permute-start.18 = (f32[8,128]{1,0:T(8,128)S(1)}, f32[8,128]{1,0:T(8,128)S(1)}, u32[]{:S(2)}, u32[]{:S(2)}) collective-permute-start(f32[8,128]{1,0:T(8,128)S(1)} %add.26), channel_id=1, source_target_pairs={{0,3},{1,2},{2,1},{3,0},{4,7},{5,6},{6,5},{7,4},{8,11},{9,10},{10,... | collective-permute-start | bytes 12296 | tf_op jit(solution)/shard_map/ppermute | solution.py:658
  80.3 2.5 %collective-permute-done.18 = f32[8,128]{1,0:T(8,128)S(1)} collective-permute-done((f32[8,128]{1,0:T(8,128)S(1)}, f32[8,128]{1,0:T(8,128)S(1)}, u32[]{:S(2)}, u32[]{:S(2)}) %collective-permute-start.18) | collective-permute-done | bytes 4128 | tf_op jit(solution)/shard_map/ppermute | solution.py:658
  82.8 6.5 %k_last.1 = (f32[8,16,32,128]{3,2,1,0:T(8,128)}, f32[8,16,32,128]{3,2,1,0:T(8,128)}) custom-call(f32[8,128]{1,0:T(8,128)S(1)} %add.27.refs_0_, f32[8,16,32,128]{3,2,1,0:T(8,128)S(1)} %get-tuple-element.45.refs_0_.refs_1_, f32[8,16,32,128]{3,2,1,0:T(8,128)S(1)} %get-tuple-element.63.refs_7_.refs_1_.refs_2_, f32[8,16,32,128]{3,2,1,0:T(8,128)S(1)} %get-tuple-element.66.refs_3_, ...), custom_call_target="tpu_custom_call" | custom-call | tf_op jit(solution)/shard_map/k_last/pallas_call | solution.py:36
  (40 shorter events, 13.3 us)
Async XLA Ops:
  0.6 2.0 %copy-start = (f32[14,16,32,128]{3,2,1,0:T(8,128)S(1)}, f32[14,16,32,128]{3,2,1,0:T(8,128)}, u32[]{:S(2)}) copy-start(f32[14,16,32,128]{3,2,1,0:T(8,128)} %refs_1_.1) | copy-start | bytes 11010052
  2.7 1.6 %copy-start.1 = (f32[8,16,32,128]{3,2,1,0:T(8,128)S(1)}, f32[8,16,32,128]{3,2,1,0:T(8,128)}, u32[]{:S(2)}) copy-start(f32[8,16,32,128]{3,2,1,0:T(8,128)} %refs_0_.1) | copy-start | bytes 6291460
  6.1 6.2 %collective-permute-start = (f32[9,8,128]{2,1,0:T(8,128)S(1)}, f32[9,8,128]{2,1,0:T(8,128)S(1)}, u32[]{:S(2)}, u32[]{:S(2)}) collective-permute-start(f32[9,8,128]{2,1,0:T(8,128)S(1)} %get-tuple-element.37), channel_id=1, source_target_pairs={{0,1},{1,2},{2,3},{3,0},{4,5},{5,6},{6,7},{7,4},{8,9},{9,10},{10,1... | collective-permute-start | bytes 110600 | tf_op jit(solution)/shard_map/ppermute | solution.py:651
  8.2 4.1 %collective-permute-start.1 = (f32[9,8,128]{2,1,0:T(8,128)S(1)}, f32[9,8,128]{2,1,0:T(8,128)S(1)}, u32[]{:S(2)}, u32[]{:S(2)}) collective-permute-start(f32[9,8,128]{2,1,0:T(8,128)S(1)} %get-tuple-element.38), channel_id=1, source_target_pairs={{0,3},{1,0},{2,1},{3,2},{4,7},{5,4},{6,5},{7,6},{8,11},{9,8},{10,9... | collective-permute-start | bytes 110600 | tf_op jit(solution)/shard_map/ppermute | solution.py:651
  12.7 8.5 %collective-permute-start.2 = (f32[36,8,128]{2,1,0:T(8,128)S(1)}, f32[36,8,128]{2,1,0:T(8,128)S(1)}, u32[]{:S(2)}, u32[]{:S(2)}) collective-permute-start(f32[36,8,128]{2,1,0:T(8,128)S(1)} %get-tuple-element.46), channel_id=1, source_target_pairs={{0,4},{4,8},{8,12},{12,16},{16,20},{20,24},{24,28},{28,0},{1,5},{5... | collective-permute-start | bytes 442376 | tf_op jit(solution)/shard_map/ppermute | solution.py:651
  12.7 8.5 %collective-permute-start.3 = (f32[30,8,128]{2,1,0:T(8,128)S(1)}, f32[30,8,128]{2,1,0:T(8,128)S(1)}, u32[]{:S(2)}, u32[]{:S(2)}) collective-permute-start(f32[30,8,128]{2,1,0:T(8,128)S(1)} %get-tuple-element.47), channel_id=1, source_target_pairs={{0,28},{4,0},{8,4},{12,8},{16,12},{20,16},{24,20},{28,24},{1,29},{... | collective-permute-start | bytes 368648 | tf_op jit(solution)/shard_map/ppermute | solution.py:651
  21.5 9.4 %collective-permute-start.4 = (f32[40,8,128]{2,1,0:T(8,128)S(1)}, f32[40,8,128]{2,1,0:T(8,128)S(1)}, u32[]{:S(2)}, u32[]{:S(2)}) collective-permute-start(f32[40,8,128]{2,1,0:T(8,128)S(1)} %get-tuple-element.49), channel_id=1, source_target_pairs={{0,96},{32,0},{64,32},{96,64},{1,97},{33,1},{65,33},{97,65},{2,98}... | collective-permute-start | bytes 491528 | tf_op jit(solution)/shard_map/ppermute | solution.py:651
  24.6 6.4 %collective-permute-start.5 = (f32[36,8,128]{2,1,0:T(8,128)S(1)}, f32[36,8,128]{2,1,0:T(8,128)S(1)}, u32[]{:S(2)}, u32[]{:S(2)}) collective-permute-start(f32[36,8,128]{2,1,0:T(8,128)S(1)} %get-tuple-element.50), channel_id=1, source_target_pairs={{0,32},{32,64},{64,96},{96,0},{1,33},{33,65},{65,97},{97,1},{2,34}... | collective-permute-start | bytes 442376 | tf_op jit(solution)/shard_map/ppermute | solution.py:651
  32.2 7.5 %collective-permute-start.6 = (f32[4,8,128]{2,1,0:T(8,128)S(1)}, f32[4,8,128]{2,1,0:T(8,128)S(1)}, u32[]{:S(2)}, u32[]{:S(2)}) collective-permute-start(f32[4,8,128]{2,1,0:T(8,128)S(1)} %get-tuple-element.52), channel_id=1, source_target_pairs={{0,1},{1,2},{2,3},{3,0},{4,5},{5,6},{6,7},{7,4},{8,9},{9,10},{10,1... | collective-permute-start | bytes 49160 | tf_op jit(solution)/shard_map/ppermute | solution.py:651
  34.0 5.7 %collective-permute-start.7 = (f32[4,8,128]{2,1,0:T(8,128)S(1)}, f32[4,8,128]{2,1,0:T(8,128)S(1)}, u32[]{:S(2)}, u32[]{:S(2)}) collective-permute-start(f32[4,8,128]{2,1,0:T(8,128)S(1)} %get-tuple-element.53), channel_id=1, source_target_pairs={{0,3},{1,0},{2,1},{3,2},{4,7},{5,4},{6,5},{7,6},{8,11},{9,8},{10,9... | collective-permute-start | bytes 49160 | tf_op jit(solution)/shard_map/ppermute | solution.py:651
  39.8 6.1 %collective-permute-start.8 = (f32[24,8,128]{2,1,0:T(8,128)S(1)}, f32[24,8,128]{2,1,0:T(8,128)S(1)}, u32[]{:S(2)}, u32[]{:S(2)}) collective-permute-start(f32[24,8,128]{2,1,0:T(8,128)S(1)} %get-tuple-element.58), channel_id=1, source_target_pairs={{0,4},{4,8},{8,12},{12,16},{16,20},{20,24},{24,28},{28,0},{1,5},{5... | collective-permute-start | bytes 294920 | tf_op jit(solution)/shard_map/ppermute | solution.py:651
  39.8 6.1 %collective-permute-start.9 = (f32[24,8,128]{2,1,0:T(8,128)S(1)}, f32[24,8,128]{2,1,0:T(8,128)S(1)}, u32[]{:S(2)}, u32[]{:S(2)}) collective-permute-start(f32[24,8,128]{2,1,0:T(8,128)S(1)} %get-tuple-element.59), channel_id=1, source_target_pairs={{0,28},{4,0},{8,4},{12,8},{16,12},{20,16},{24,20},{28,24},{1,29},{... | collective-permute-start | bytes 294920 | tf_op jit(solution)/shard_map/ppermute | solution.py:651
  46.1 7.6 %collective-permute-start.10 = (f32[40,8,128]{2,1,0:T(8,128)S(1)}, f32[40,8,128]{2,1,0:T(8,128)S(1)}, u32[]{:S(2)}, u32[]{:S(2)}) collective-permute-start(f32[40,8,128]{2,1,0:T(8,128)S(1)} %get-tuple-element.61), channel_id=1, source_target_pairs={{0,96},{32,0},{64,32},{96,64},{1,97},{33,1},{65,33},{97,65},{2,98}... | collective-permute-start | bytes 491528 | tf_op jit(solution)/shard_map/ppermute | solution.py:651
  47.5 6.2 %collective-permute-start.11 = (f32[32,8,128]{2,1,0:T(8,128)S(1)}, f32[32,8,128]{2,1,0:T(8,128)S(1)}, u32[]{:S(2)}, u32[]{:S(2)}) collective-permute-start(f32[32,8,128]{2,1,0:T(8,128)S(1)} %get-tuple-element.62), channel_id=1, source_target_pairs={{0,32},{32,64},{64,96},{96,0},{1,33},{33,65},{65,97},{97,1},{2,34}... | collective-permute-start | bytes 393224 | tf_op jit(solution)/shard_map/ppermute | solution.py:651
  56.3 1.2 %collective-permute-start.12 = (f32[8,128]{1,0:T(8,128)S(1)}, f32[8,128]{1,0:T(8,128)S(1)}, u32[]{:S(2)}, u32[]{:S(2)}) collective-permute-start(f32[8,128]{1,0:T(8,128)S(1)} %get-tuple-element.64), channel_id=1, source_target_pairs={{0,4},{4,0},{8,12},{12,8},{16,20},{20,16},{24,28},{28,24},{1,5},{5... | collective-permute-start | bytes 12296 | tf_op jit(solution)/shard_map/ppermute | solution.py:658
  57.5 3.6 %collective-permute-start.13 = (f32[8,128]{1,0:T(8,128)S(1)}, f32[8,128]{1,0:T(8,128)S(1)}, u32[]{:S(2)}, u32[]{:S(2)}) collective-permute-start(f32[8,128]{1,0:T(8,128)S(1)} %add.21), channel_id=1, source_target_pairs={{0,8},{4,12},{8,0},{12,4},{16,24},{20,28},{24,16},{28,20},{1,9},{5... | collective-permute-start | bytes 12296 | tf_op jit(solution)/shard_map/ppermute | solution.py:658
  61.1 4.8 %collective-permute-start.14 = (f32[8,128]{1,0:T(8,128)S(1)}, f32[8,128]{1,0:T(8,128)S(1)}, u32[]{:S(2)}, u32[]{:S(2)}) collective-permute-start(f32[8,128]{1,0:T(8,128)S(1)} %add.22), channel_id=1, source_target_pairs={{0,24},{4,28},{8,16},{12,20},{16,8},{20,12},{24,0},{28,4},{1,25},{... | collective-permute-start | bytes 12296 | tf_op jit(solution)/shard_map/ppermute | solution.py:658
  66.0 3.6 %collective-permute-start.15 = (f32[8,128]{1,0:T(8,128)S(1)}, f32[8,128]{1,0:T(8,128)S(1)}, u32[]{:S(2)}, u32[]{:S(2)}) collective-permute-start(f32[8,128]{1,0:T(8,128)S(1)} %add.23), channel_id=1, source_target_pairs={{0,32},{32,0},{64,96},{96,64},{1,33},{33,1},{65,97},{97,65},{2,34}... | collective-permute-start | bytes 12296 | tf_op jit(solution)/shard_map/ppermute | solution.py:658
  69.6 4.8 %collective-permute-start.16 = (f32[8,128]{1,0:T(8,128)S(1)}, f32[8,128]{1,0:T(8,128)S(1)}, u32[]{:S(2)}, u32[]{:S(2)}) collective-permute-start(f32[8,128]{1,0:T(8,128)S(1)} %add.24), channel_id=1, source_target_pairs={{0,96},{32,64},{64,32},{96,0},{1,97},{33,65},{65,33},{97,1},{2,98}... | collective-permute-start | bytes 12296 | tf_op jit(solution)/shard_map/ppermute | solution.py:658
  74.4 3.6 %collective-permute-start.17 = (f32[8,128]{1,0:T(8,128)S(1)}, f32[8,128]{1,0:T(8,128)S(1)}, u32[]{:S(2)}, u32[]{:S(2)}) collective-permute-start(f32[8,128]{1,0:T(8,128)S(1)} %add.25), channel_id=1, source_target_pairs={{0,1},{1,0},{2,3},{3,2},{4,5},{5,4},{6,7},{7,6},{8,9},{9,8},{10,11... | collective-permute-start | bytes 12296 | tf_op jit(solution)/shard_map/ppermute | solution.py:658
  78.0 4.8 %collective-permute-start.18 = (f32[8,128]{1,0:T(8,128)S(1)}, f32[8,128]{1,0:T(8,128)S(1)}, u32[]{:S(2)}, u32[]{:S(2)}) collective-permute-start(f32[8,128]{1,0:T(8,128)S(1)} %add.26), channel_id=1, source_target_pairs={{0,3},{1,2},{2,1},{3,0},{4,7},{5,6},{6,5},{7,4},{8,11},{9,10},{10,... | collective-permute-start | bytes 12296 | tf_op jit(solution)/shard_map/ppermute | solution.py:658

commit v3 on v2

--- a/solution.py
+++ b/solution.py
@@ -24,7 +24,9 @@
 
 VSPEC = pl.BlockSpec(memory_space=pltpu.VMEM)
 HSPEC = pl.BlockSpec(memory_space=pl.ANY)
+FAR = pl.BlockSpec(memory_space=pltpu.HBM)
 MIB = 1024 * 1024
+START_LIMIT = 48
 
 
 def call(body, name, ins, outs, after=(), aliases=None, scratch=(), in_specs=None, out_specs=None, limit=8):
@@ -63,8 +65,8 @@
 
 
 def with_ends(value, ends):
-    before = roll(jnp.where(lanes() == 127, ends, value), 1)
-    after = roll(jnp.where(lanes() == 0, ends, value), -1)
+    before = jnp.where(lanes() == 0, ends, roll(value, 1))
+    after = jnp.where(lanes() == 127, ends, roll(value, -1))
     return before, after
 
 
@@ -104,16 +106,16 @@
     lax.fori_loop(0, 4, group, 0)
 
 
-def start_kernel(rhs, stencil, rc, st, vi, zp, zm, sem_r, sem_s):
+def start_kernel(rhs, stencil, rc, vi, zp, zm, st, sem_r, sem_s):
     def part(g):
         at = pl.ds(4 * g, 4)
         return pltpu.make_async_copy(rhs.at[:, at], rc.at[:, at], sem_r.at[g])
 
     def field(k):
-        return pltpu.make_async_copy(stencil.at[k], st.at[k], sem_s.at[k])
+        at = WZ_AT[k]
+        return pltpu.make_async_copy(stencil.at[k], st.at[at], sem_s.at[at])
 
     order = [k for pair in PAIRS for k in pair if k is not None]
-    order += [k for k in range(14) if k not in order]
     for g in range(4):
         part(g).start()
     for k in order:
@@ -136,9 +138,9 @@
         for x in range(X):
             for yb in range(4):
                 at = 8 * x + 2 * yb
-                w = st[up, x, pl.ds(8 * yb, 8), :]
+                w = st[WZ_AT[up], x, pl.ds(8 * yb, 8), :]
                 if down is not None:
-                    w = jnp.where(lanes() == 0, st[down, x, pl.ds(8 * yb, 8), :], w)
+                    w = jnp.where(lanes() == 0, st[WZ_AT[down], x, pl.ds(8 * yb, 8), :], w)
                 out = jnp.where((lanes() == at) | (lanes() == at + 1), roll(w, at + 1), out)
         zp[4 + j] = out
         zm[4 + j] = out
@@ -151,95 +153,78 @@
 
 
 def merged(rl, rr, g):
-    left, right = rl[g], rr[g]
+    left, right = roll(rl[g], 2), rr[g]
     return jnp.where(even(), left, right), jnp.where(even(), right, left)
 
 
 def ends_of(pair, at):
-    return roll(pair[at % 2], -(at + 1))
-
-
-def shift_fields(vi, rl, rr, vm, vp):
+    return roll(pair[at % 2], -(at + 2))
+
+
+def coupling_ends(rl, rr):
+    return [jnp.where(even(), roll(rl[4 + j], 2), rr[4 + j]) for j in range(5)]
+
+
+def coupling_end(ends, j, x, yb):
+    return roll(ends[j], -(8 * x + 2 * yb + 2))
+
+
+def roll_rows(vi, vm, vp, x):
+    for y in range(Y):
+        v = vi[x, y]
+        vm[x, y] = roll(v, 1)
+        vp[x, y] = roll(v, -1)
+
+
+def roll_fields(vi, vm, vp):
+    def step(n, carry):
+        for i in range(4):
+            roll_rows(vi, vm, vp, 4 * n + i)
+        return carry
+
+    lax.fori_loop(0, X // 4, step, 0)
+
+
+def roll_kernel(vi, st, vm, vp, wz):
+    def step(n, carry):
+        for i in range(4):
+            x = 4 * n + i
+            roll_rows(vi, vm, vp, x)
+            for k in ZSHIFTED:
+                for yb in range(4):
+                    at = pl.ds(8 * yb, 8)
+                    wz[WZ_AT[k], x, at, :] = roll(st[k, x, at, :], OFF[k][2])
+        return carry
+
+    lax.fori_loop(0, X // 4, step, 0)
+
+
+def put_ends(rl, rr, vm, vp):
+    first, last = lanes() == 0, lanes() == 127
+
     def group(g, carry):
         pair = merged(rl, rr, g)
         for xx in range(4):
-            for part in range(0, Y, 16):
-                ys = range(part, part + 16)
-                ends = [ends_of(pair, spot(xx, y)) for y in ys]
-                for y, end in zip(ys, ends):
-                    before, after = with_ends(vi[4 * g + xx, y], end)
-                    vm[4 * g + xx, y] = before
-                    vp[4 * g + xx, y] = after
+            for y in range(Y):
+                end = ends_of(pair, spot(xx, y))
+                pltpu.store(vm.at[4 * g + xx, y], end, mask=first)
+                pltpu.store(vp.at[4 * g + xx, y], end, mask=last)
         return carry
 
     lax.fori_loop(0, 4, group, 0)
 
 
-def shifted_couplings(st, ends, j, spots):
-    up, down = PAIRS[j]
-    tiles = [roll(ends[j], -(8 * x + 2 * yb + 1)) for x, yb in spots]
-    result = []
-    for tile, (x, yb) in zip(tiles, spots):
-        w = st[up, x, pl.ds(8 * yb, 8), :]
-        moved = {up: roll(jnp.where(lanes() == 127, tile, w), 1)}
-        if down is not None:
-            w = st[down, x, pl.ds(8 * yb, 8), :]
-            moved[down] = roll(jnp.where(lanes() == 0, tile, w), -1)
-        result.append(moved)
-    return result
-
-
-def edge_rows(vi, rl, rr, yp, ym):
-    for x in range(X):
-        yp[x] = vi[x, Y - 1]
-        ym[x] = vi[x, 0]
-    for g in range(4):
-        for i, tile in enumerate(merged(rl, rr, g)):
-            yp[16 + 2 * g + i] = tile
-            ym[16 + 2 * g + i] = tile
-
-
-def coupling_ends(rl, rr):
-    return [jnp.where(even(), rl[4 + j], rr[4 + j]) for j in range(5)]
-
-
-def edge_kernel(vi, st, rl, rr, yp, ym):
-    edge_rows(vi, rl, rr, yp, ym)
+def ends_kernel(vm_in, vp_in, wz_in, st, rl, rr, vm, vp, wz, sums):
+    put_ends(rl, rr, vm, vp)
     ends = coupling_ends(rl, rr)
-    for ref, keys, y in ((yp, YPLUS, Y - 1), (ym, YMINUS, 0)):
-        rows_of = {}
-        for j, pair in enumerate(PAIRS):
-            if pair[0] in keys or pair[1] in keys:
-                moved = shifted_couplings(st, ends, j, [(x, y // 8) for x in range(X)])
-                for x in range(X):
-                    rows_of.update({(k, x): tile for k, tile in moved[x].items()})
-        for i, k in enumerate(keys):
-            for x in range(X):
-                r = 16 * i + x
-                if k in WZ_AT:
-                    row = rows_of[k, x][y % 8 : y % 8 + 1, :]
-                else:
-                    row = st[k, x, pl.ds(y, 1), :]
-                ref[24 + r // 8, pl.ds(r % 8, 1), :] = row
-    clear_if(at_last("gy"), yp)
-    clear_if(at_first("gy"), ym)
-
-
-def edge_again_kernel(vi, rl, rr, yp, ym):
-    edge_rows(vi, rl, rr, yp, ym)
-    clear_if(at_last("gy"), yp)
-    clear_if(at_first("gy"), ym)
-
-
-def shift_kernel(vi, st, rl, rr, vm, vp, wz, sums):
-    shift_fields(vi, rl, rr, vm, vp)
-    ends = coupling_ends(rl, rr)
-    for j in range(5):
-        for x in range(0, X, 4):
-            spots = [(x + i, yb) for i in range(4) for yb in range(4)]
-            for (xx, yb), moved in zip(spots, shifted_couplings(st, ends, j, spots)):
-                for k, tile in moved.items():
-                    wz[WZ_AT[k], xx, pl.ds(8 * yb, 8), :] = tile
+    first, last = lanes() == 0, lanes() == 127
+    for j, pair in enumerate(PAIRS):
+        for x in range(X):
+            for yb in range(4):
+                end = coupling_end(ends, j, x, yb)
+                for k, mask in zip(pair, (first, last)):
+                    if k is not None:
+                        pltpu.store(wz.at[WZ_AT[k], x, pl.ds(8 * yb, 8), :], end, mask=mask)
 
     def behind(k, x, yb):
         if k in WZ_AT:
@@ -260,6 +245,50 @@
         return carry
 
     lax.fori_loop(0, X, add_up, 0)
+
+
+def ends_again_kernel(vm_in, vp_in, rl, rr, vm, vp):
+    put_ends(rl, rr, vm, vp)
+
+
+def edge_rows(vi, rl, rr, yp, ym):
+    for x in range(X):
+        yp[x] = vi[x, Y - 1]
+        ym[x] = vi[x, 0]
+    for g in range(4):
+        for i, tile in enumerate(merged(rl, rr, g)):
+            yp[16 + 2 * g + i] = tile
+            ym[16 + 2 * g + i] = tile
+
+
+def edge_kernel(vi, st, wz, rl, rr, yp, ym):
+    edge_rows(vi, rl, rr, yp, ym)
+    ends = coupling_ends(rl, rr)
+    for ref, keys, y in ((yp, YPLUS, Y - 1), (ym, YMINUS, 0)):
+        rows_of = {}
+        for j, pair in enumerate(PAIRS):
+            for x in range(X):
+                for k, edge in zip(pair, (0, 127)):
+                    if k in keys:
+                        end = coupling_end(ends, j, x, y // 8)
+                        w = wz[WZ_AT[k], x, pl.ds(8 * (y // 8), 8), :]
+                        rows_of[k, x] = jnp.where(lanes() == edge, end, w)
+        for i, k in enumerate(keys):
+            for x in range(X):
+                r = 16 * i + x
+                if k in WZ_AT:
+                    row = rows_of[k, x][y % 8 : y % 8 + 1, :]
+                else:
+                    row = st[k, x, pl.ds(y, 1), :]
+                ref[24 + r // 8, pl.ds(r % 8, 1), :] = row
+    clear_if(at_last("gy"), yp)
+    clear_if(at_first("gy"), ym)
+
+
+def edge_again_kernel(vi, rl, rr, yp, ym):
+    edge_rows(vi, rl, rr, yp, ym)
+    clear_if(at_last("gy"), yp)
+    clear_if(at_first("gy"), ym)
 
 
 def behind_row(st, wz, k, x, y):
@@ -435,8 +464,10 @@
                         )
                 for term in terms:
                     total = term if total is None else total + term
-            if x == 0:
+            if x == 0 and tm is not None:
                 total = tm[y] if total is None else total + tm[y]
+            if total is None:
+                continue
             value = acc[x, y] - total
             fix = extra(x, y) if extra is not None else None
             acc[x, y] = value if fix is None else value + fix
@@ -486,14 +517,18 @@
 PRODUCTS = [(i, j) for i in range(8) for j in range(i, 8)]
 
 
-def gram(u, v):
-    def step(n, carry):
-        x, at = n // 4, pl.ds((n % 4) * 8, 8)
-        a = [u[i, x, at, :] for i in range(8)]
-        b = a if v is u else [v[i, x, at, :] for i in range(8)]
-        return tuple(c + a[i] * b[j] for c, (i, j) in zip(carry, PRODUCTS))
-
-    return lax.fori_loop(0, 4 * X, step, tuple(jnp.zeros((8, 128), F32) for _ in PRODUCTS))
+def gram(u, v, planes=X, begin=None):
+    def step(x, carry):
+        for yb in range(4):
+            at = pl.ds(8 * yb, 8)
+            a = [u[i, x, at, :] for i in range(8)]
+            b = a if v is u else [v[i, x, at, :] for i in range(8)]
+            carry = tuple(c + a[i] * b[j] for c, (i, j) in zip(carry, PRODUCTS))
+        return carry
+
+    if begin is None:
+        begin = tuple(jnp.zeros((8, 128), F32) for _ in PRODUCTS)
+    return lax.fori_loop(0, planes, step, begin)
 
 
 def place(tile, sums, m):
@@ -519,13 +554,18 @@
     out[...] = place(tile, gram(flat, flat), 2)
 
 
-def late_kernel(acc_in, st, ring, qm, qp, tp, tm, y1, early, acc, flat, out):
-    finish_edges(acc, st, ring, qm, qp, tp, tm, None)
+def late_kernel(acc_in, st, ring, qm, qp, tp, xp, y1, early, acc, flat, out, far, sent):
+    finish_edges(acc, st, ring, qm, qp, tp, None, None)
+    for yb in range(4):
+        at = pl.ds(8 * yb, 8)
+        far[:, 0, at, :] = jnp.swapaxes(tp[pl.ds(8 * yb + 1, 8)], 0, 1)
+        sent[:, 0, at, :] = -jnp.swapaxes(xp[at], 0, 1)
     flat_kernel(acc, flat)
-    out[...] = place(early[...], gram(y1, flat), 3)
-
-
-def differences_kernel(r0, y1, y2, d0, d1):
+    sums = gram(far, sent, 1)
+    out[...] = place(early[...], gram(y1, flat, X, sums), 3)
+
+
+def differences_kernel(r0, y1, y2, tm, d0, d1):
     def step(x, carry):
         for i in range(8):
             d0[i, x] = r0[i, x] - y1[i, x]
@@ -533,6 +573,9 @@
         return carry
 
     lax.fori_loop(0, X, step, 0)
+    for yb in range(4):
+        at = pl.ds(8 * yb, 8)
+        d1[:, 0, at, :] = d1[:, 0, at, :] + jnp.swapaxes(tm[at], 0, 1)
 
 
 def entry(col, i):
@@ -627,21 +670,17 @@
             rbuf[j, x, at, :] = r0[j, x, at, :] - (sums[1] + sums[2])
 
     def copy(n, src, dst, which):
-        part = pl.ds(n * 2, 2)
-        return pltpu.make_async_copy(src.at[:, part], dst.at[:, part], sems.at[which, n])
+        return pltpu.make_async_copy(src.at[:, n], dst.at[:, n], sems.at[which, n])
 
     def step(n, carry):
-        def inner(t, c):
-            tile_out(n * 2 + t // 4, t % 4)
-            return c
-
-        lax.fori_loop(0, 8, inner, 0)
+        for yb in range(4):
+            tile_out(n, yb)
         copy(n, sbuf, sol, 0).start()
         copy(n, rbuf, res, 1).start()
         return carry
 
-    lax.fori_loop(0, X // 2, step, 0)
-    for n in range(X // 2):
+    lax.fori_loop(0, X, step, 0)
+    for n in range(X):
         copy(n, sbuf, sol, 0).wait()
         copy(n, rbuf, res, 1).wait()
 
@@ -664,23 +703,28 @@
     compact = (F, X, Y, Z)
     tile = (8, 128)
     dma = pltpu.SemaphoreType.DMA
-    rc, st, vi, zp, zm = call(
+    st = stencil
+    rc, vi, zp, zm = call(
         start_kernel, "k_start", [rhs, stencil],
-        [compact, (14, X, Y, Z), full, (9, *tile), (9, *tile)],
-        in_specs=[HSPEC] * 2, scratch=[dma((4,)), dma((14,))],
+        [compact, full, (9, *tile), (9, *tile)],
+        in_specs=[FAR] * 2,
+        scratch=[pltpu.VMEM((9, X, Y, Z), F32), dma((4,)), dma((9,))],
+        limit=START_LIMIT,
     )
     rl = shift(zp, "gz", 1)
     rr = shift(zm, "gz", -1)
-    (g0,) = call(gram_first_kernel, "k_gram0", [rc], [tile])
-    yp, ym = call(edge_kernel, "k_edge", [vi, st, rl, rr], [(36, *tile), (30, *tile)], after=[g0])
+    vm, vp, wz = call(roll_kernel, "k_roll", [vi, st], [full, full, (9, X, Y, Z)])
+    yp, ym = call(edge_kernel, "k_edge", [vi, st, wz, rl, rr], [(36, *tile), (30, *tile)])
     qm = shift(yp, "gy", 1)
     qp = shift(ym, "gy", -1)
     vm, vp, wz, sums = call(
-        shift_kernel, "k_shift", [vi, st, rl, rr], [full, full, (9, X, Y, Z), (5, X, Y, Z)]
-    )
+        ends_kernel, "k_ends", [vm, vp, wz, st, rl, rr],
+        [full, full, (9, X, Y, Z), (5, X, Y, Z)], aliases={0: 0, 1: 1, 2: 2}, after=[yp],
+    )
+    (g0,) = call(gram_first_kernel, "k_gram0", [rc], [tile], after=[yp])
     ring, xm, xp = call(
         third_kernel(True), "k_third", [vi, vm, vp, st, wz, rl, rr, qm, qp, sums],
-        [(2, 3, X, *tile), (Y + 8, *tile), (Y + 4, *tile)],
+        [(2, 3, X, *tile), (Y + 8, *tile), (Y + 4, *tile)], after=[g0],
     )
     tp = shift(xm, "gx", -1)
     tm = shift(xp, "gx", 1)
@@ -692,34 +736,39 @@
 
     rl = shift(zp, "gz", 1)
     rr = shift(zm, "gz", -1)
-    y1f, g2 = call(gram_second_kernel, "k_gram12", [rc, y1, g0], [compact, tile])
+    vm, vp = call(roll_fields, "k_roll2", [y1], [full, full])
     yp, ym = call(
-        edge_again_kernel, "k_edge2", [y1, rl, rr], [(24, *tile), (24, *tile)], after=[g2]
+        edge_again_kernel, "k_edge2", [y1, rl, rr], [(24, *tile), (24, *tile)], after=[vm]
     )
     qmv = shift(yp, "gy", 1)
     qpv = shift(ym, "gy", -1)
-    vm, vp = call(shift_fields, "k_shift2", [y1, rl, rr], [full, full])
+    vm, vp = call(
+        ends_again_kernel, "k_ends2", [vm, vp, rl, rr], [full, full],
+        aliases={0: 0, 1: 1}, after=[yp],
+    )
+    y1f, g2 = call(gram_second_kernel, "k_gram12", [rc, y1, g0], [compact, tile], after=[yp])
     ring, xm, xp = call(
         third_kernel(False), "k_third2", [y1, vm, vp, st, wz, rl, rr, qmv, qpv, qm, qp],
-        [(2, 3, X, *tile), (Y + 8, *tile), (Y, *tile)],
+        [(2, 3, X, *tile), (Y + 8, *tile), (Y, *tile)], after=[g2],
     )
     tp = shift(xm, "gx", -1)
     tm = shift(xp, "gx", 1)
     (acc,) = call(inner_again_kernel, "k_inner2", [y1, vm, vp, st, wz, diag], [full])
     _, y2f, moment = call(
-        late_kernel, "k_late", [acc, st, ring, qm, qp, tp, tm, y1f, g2],
+        late_kernel, "k_late", [acc, st, ring, qm, qp, tp, xp, y1f, g2],
         [full, compact, tile], aliases={0: 0},
-    )
-    d0, d1 = call(differences_kernel, "k_diff", [rc, y1f, y2f], [compact, compact])
+        scratch=[pltpu.VMEM((F, 1, Y, Z), F32), pltpu.VMEM((F, 1, Y, Z), F32)],
+    )
+    d0, d1 = call(differences_kernel, "k_diff", [rc, y1f, y2f, tm], [compact, compact])
     moment = everywhere(moment)
     sol, res = call(
         last_kernel, "k_last", [moment, rc, y1f, d0, d1], [compact, compact],
-        out_specs=[HSPEC, HSPEC],
+        out_specs=[FAR, FAR],
         scratch=[
             pltpu.VMEM((3, 8, *tile), F32),
             pltpu.VMEM(compact, F32),
             pltpu.VMEM(compact, F32),
-            dma((2, X // 2)),
+            dma((2, X)),
         ],
         limit=14,
     )

time: 89.5 us -> 79.2 us (0.88)
  waiting for transfers between devices: 25.2 us -> 19.3 us
  Pallas kernels: 36.2 us -> 30.7 us
  starting transfers between devices: 23.4 us -> 28.3 us
  local copies, waits for them, and re-layouts: 3.62 us -> 0.01 us
    pallas_call x15 -> x17, Pallas kernels: 36.2 us -> 30.7 us  [call(): pl.pallas_call(run, name=name, out_shape=[jax.ShapeDtypeStruct(s, F32) fo...]
    ppermute x7, waiting for transfers between devices: 21.5 us -> 16.5 us  [everywhere(): x = x + lax.ppermute(x, axis, [(i, i ^ bit) for i in range(n)])]
    ppermute x7, starting transfers between devices: 4.6 us -> 9.59 us  [everywhere(): x = x + lax.ppermute(x, axis, [(i, i ^ bit) for i in range(n)])]
    unnamed x4 -> x2, local copies, waits for them, and re-layouts: 3.62 us -> 0.01 us
    ppermute x12, waiting for transfers between devices: 3.66 us -> 2.75 us  [shift(): return lax.ppermute(x, axis, [(i, (i + step) % n) for i in range(n)])]
where the time goes in v3:
time: 79.2 us; the launch traced here: 79.1 us
  Pallas kernels  30.7 us (39%)
  starting transfers between devices  28.3 us (36%)
  waiting for transfers between devices  19.3 us (24%)
  between operations  0.83 us (1%)
    pallas_call x17, Pallas kernels, call(): pl.pallas_call(run, name=name, out_shape=[jax.ShapeDtypeStruct(s, F32) fo...  30.7 us
    ppermute x12, starting transfers between devices, shift(): return lax.ppermute(x, axis, [(i, (i + step) % n) for i in range(n)])  18.7 us
    ppermute x7, waiting for transfers between devices, everywhere(): x = x + lax.ppermute(x, axis, [(i, i ^ bit) for i in range(n)])  16.5 us
    ppermute x7, starting transfers between devices, everywhere(): x = x + lax.ppermute(x, axis, [(i, i ^ bit) for i in range(n)])  9.59 us
    ppermute x12, waiting for transfers between devices, shift(): return lax.ppermute(x, axis, [(i, (i + step) % n) for i in range(n)])  2.75 us
  transfers between devices with their start and end apart: 19, of which 10 were waited for; matrix products, arithmetic and copies ran while one was open for 0% of the time, Pallas kernels for 26%

profile of v3, /device:TPU:0, one launch (start us, length us, event | category | flops | bytes accessed | tf_op | source)
XLA Modules:
  0.0 79.1 jit_solution(16304078783849507965)
XLA Ops:
  0.6 3.0 %k_start.1 = (f32[8,16,32,128]{3,2,1,0:T(8,128)S(1)}, f32[16,32,8,128]{3,2,1,0:T(8,128)S(1)}, f32[9,8,128]{2,1,0:T(8,128)S(1)}, f32[9,8,128]{2,1,0:T(8,128)S(1)}) custom-call(f32[8,16,32,128]{3,2,1,0:T(8,128)} %refs_0_.1, f32[14,16,32,128]{3,2,1,0:T(8,128)} %refs_1_.7), custom_call_target="tpu_custom_call" | custom-call | tf_op jit(solution)/shard_map/k_start/pallas_call | solution.py:38
  3.7 2.1 %collective-permute-start = (f32[9,8,128]{2,1,0:T(8,128)S(1)}, f32[9,8,128]{2,1,0:T(8,128)S(1)}, u32[]{:S(2)}, u32[]{:S(2)}) collective-permute-start(f32[9,8,128]{2,1,0:T(8,128)S(1)} %get-tuple-element.43), channel_id=1, source_target_pairs={{0,1},{1,2},{2,3},{3,0},{4,5},{5,6},{6,7},{7,4},{8,9},{9,10},{10,1... | collective-permute-start | bytes 110600 | tf_op jit(solution)/shard_map/ppermute | solution.py:690
  5.8 2.2 %collective-permute-start.1 = (f32[9,8,128]{2,1,0:T(8,128)S(1)}, f32[9,8,128]{2,1,0:T(8,128)S(1)}, u32[]{:S(2)}, u32[]{:S(2)}) collective-permute-start(f32[9,8,128]{2,1,0:T(8,128)S(1)} %get-tuple-element.44), channel_id=1, source_target_pairs={{0,3},{1,0},{2,1},{3,2},{4,7},{5,4},{6,5},{7,6},{8,11},{9,8},{10,9... | collective-permute-start | bytes 110600 | tf_op jit(solution)/shard_map/ppermute | solution.py:690
  8.0 1.9 %k_roll.1 = (f32[16,32,8,128]{3,2,1,0:T(8,128)S(1)}, f32[16,32,8,128]{3,2,1,0:T(8,128)S(1)}, f32[9,16,32,128]{3,2,1,0:T(8,128)S(1)}) custom-call(f32[16,32,8,128]{3,2,1,0:T(8,128)S(1)} %get-tuple-element.39.refs_0_.refs_2_, f32[14,16,32,128]{3,2,1,0:T(8,128)S(1)} %copy-done), custom_call_target="tpu_custom_call" | custom-call | tf_op jit(solution)/shard_map/k_roll/pallas_call | solution.py:38
  10.2 2.9 %collective-permute-start.3 = (f32[30,8,128]{2,1,0:T(8,128)S(1)}, f32[30,8,128]{2,1,0:T(8,128)S(1)}, u32[]{:S(2)}, u32[]{:S(2)}) collective-permute-start(f32[30,8,128]{2,1,0:T(8,128)S(1)} %get-tuple-element.52), channel_id=1, source_target_pairs={{0,28},{4,0},{8,4},{12,8},{16,12},{20,16},{24,20},{28,24},{1,29},{... | collective-permute-start | bytes 368648 | tf_op jit(solution)/shard_map/ppermute | solution.py:690
  14.1 2.1 %k_ends.1 = (f32[16,32,8,128]{3,2,1,0:T(8,128)S(1)}, f32[16,32,8,128]{3,2,1,0:T(8,128)S(1)}, f32[9,16,32,128]{3,2,1,0:T(8,128)S(1)}, f32[5,16,32,128]{3,2,1,0:T(8,128)S(1)}) custom-call(f32[16,32,8,128]{3,2,1,0:T(8,128)S(1)} %get-tuple-element.40.refs_0_, ...), custom_call_target="tpu_custom_call", output_to_operand_aliasing={{0}: (0, {}), {1}: (1, {}), {2}: (2, {})} | custom-call | tf_op jit(solution)/shard_map/k_ends/pallas_call | solution.py:38
  16.4 3.1 %collective-permute-start.4 = (f32[40,8,128]{2,1,0:T(8,128)S(1)}, f32[40,8,128]{2,1,0:T(8,128)S(1)}, u32[]{:S(2)}, u32[]{:S(2)}) collective-permute-start(f32[40,8,128]{2,1,0:T(8,128)S(1)} %get-tuple-element.55), channel_id=1, source_target_pairs={{0,96},{32,0},{64,32},{96,64},{1,97},{33,1},{65,33},{97,65},{2,98}... | collective-permute-start | bytes 491528 | tf_op jit(solution)/shard_map/ppermute | solution.py:690
  19.5 4.7 %k_inner.1 = (f32[16,32,8,128]{3,2,1,0:T(8,128)S(1)}, f32[16,32,128]{2,1,0:T(8,128)S(1)}) custom-call(f32[16,32,8,128]{3,2,1,0:T(8,128)S(1)} %get-tuple-element.39.refs_0_.refs_2_, f32[16,32,8,128]{3,2,1,0:T(8,128)S(1)} %get-tuple-element.46.refs_1_, f32[16,32,8,128]{3,2,1,0:T(8,128)S(1)} %get-tuple-element.47.refs_2_, f32[14,16,32,128]{3,2,1,0:T(8,128)S(1)} %copy-done, ...), custom_call_target="tpu_custom_call" | custom-call | tf_op jit(solution)/shard_map/k_inner/pallas_call | solution.py:38
  24.2 1.9 %collective-permute-done.5.refs_8_ = f32[36,8,128]{2,1,0:T(8,128)S(1)} collective-permute-done((f32[36,8,128]{2,1,0:T(8,128)S(1)}, f32[36,8,128]{2,1,0:T(8,128)S(1)}, u32[]{:S(2)}, u32[]{:S(2)}) %collective-permute-start.5) | collective-permute-done | bytes 147488 | tf_op jit(solution)/shard_map/ppermute | solution.py:690
  27.3 1.8 %collective-permute-start.6 = (f32[4,8,128]{2,1,0:T(8,128)S(1)}, f32[4,8,128]{2,1,0:T(8,128)S(1)}, u32[]{:S(2)}, u32[]{:S(2)}) collective-permute-start(f32[4,8,128]{2,1,0:T(8,128)S(1)} %get-tuple-element.60), channel_id=1, source_target_pairs={{0,1},{1,2},{2,3},{3,0},{4,5},{5,6},{6,7},{7,4},{8,9},{9,10},{10,1... | collective-permute-start | bytes 49160 | tf_op jit(solution)/shard_map/ppermute | solution.py:690
  32.9 2.9 %collective-permute-start.9 = (f32[24,8,128]{2,1,0:T(8,128)S(1)}, f32[24,8,128]{2,1,0:T(8,128)S(1)}, u32[]{:S(2)}, u32[]{:S(2)}) collective-permute-start(f32[24,8,128]{2,1,0:T(8,128)S(1)} %get-tuple-element.66), channel_id=1, source_target_pairs={{0,28},{4,0},{8,4},{12,8},{16,12},{20,16},{24,20},{28,24},{1,29},{... | collective-permute-start | bytes 294920 | tf_op jit(solution)/shard_map/ppermute | solution.py:690
  35.9 2.2 %k_gram12.1 = (f32[8,16,32,128]{3,2,1,0:T(8,128)S(1)}, f32[8,128]{1,0:T(8,128)S(1)}) custom-call(f32[8,16,32,128]{3,2,1,0:T(8,128)S(1)} %get-tuple-element.53.refs_0_.refs_1_, f32[16,32,8,128]{3,2,1,0:T(8,128)S(1)} %get-tuple-element.57.refs_0_.refs_1_, f32[8,128]{1,0:T(8,128)S(1)} %k_gram0.1.refs_10_.refs_2_, ...), custom_call_target="tpu_custom_call" | custom-call | tf_op jit(solution)/shard_map/k_gram12/pallas_call | solution.py:38
  41.5 4.2 %k_inner2.1.refs_0_ = f32[16,32,8,128]{3,2,1,0:T(8,128)S(1)} custom-call(f32[16,32,8,128]{3,2,1,0:T(8,128)S(1)} %get-tuple-element.57.refs_0_.refs_1_, f32[16,32,8,128]{3,2,1,0:T(8,128)S(1)} %get-tuple-element.63.refs_1_, f32[16,32,8,128]{3,2,1,0:T(8,128)S(1)} %get-tuple-element.64.refs_2_, f32[14,16,32,128]{3,2,1,0:T(8,128)S(1)} %copy-done, ...), custom_call_target="tpu_custom_call" | custom-call | tf_op jit(solution)/shard_map/k_inner2/pallas_call | solution.py:38
  45.7 1.6 %k_late.1 = (f32[16,32,8,128]{3,2,1,0:T(8,128)S(1)}, f32[8,16,32,128]{3,2,1,0:T(8,128)S(1)}, f32[8,128]{1,0:T(8,128)S(1)}) custom-call(f32[16,32,8,128]{3,2,1,0:T(8,128)S(1)} %k_inner2.1.refs_0_, f32[14,16,32,128]{3,2,1,0:T(8,128)S(1)} %copy-done, f32[2,3,16,8,128]{4,3,2,1,0:T(8,128)S(1)} %get-tuple-element.68.refs_2_, ...), custom_call_target="tpu_custom_call", output_to_operand_aliasing={{0}: (0, {})} | custom-call | tf_op jit(solution)/shard_map/k_late/pallas_call | solution.py:38
  49.0 3.2 %collective-permute-done.12 = f32[8,128]{1,0:T(8,128)S(1)} collective-permute-done((f32[8,128]{1,0:T(8,128)S(1)}, f32[8,128]{1,0:T(8,128)S(1)}, u32[]{:S(2)}, u32[]{:S(2)}) %collective-permute-start.12) | collective-permute-done | bytes 4128 | tf_op jit(solution)/shard_map/ppermute | solution.py:697
  52.2 2.2 %collective-permute-start.13 = (f32[8,128]{1,0:T(8,128)S(1)}, f32[8,128]{1,0:T(8,128)S(1)}, u32[]{:S(2)}, u32[]{:S(2)}) collective-permute-start(f32[8,128]{1,0:T(8,128)S(1)} %add.22), channel_id=1, source_target_pairs={{0,24},{4,28},{8,16},{12,20},{16,8},{20,12},{24,0},{28,4},{1,25},{... | collective-permute-start | bytes 12296 | tf_op jit(solution)/shard_map/ppermute | solution.py:697
  54.4 2.7 %collective-permute-done.13 = f32[8,128]{1,0:T(8,128)S(1)} collective-permute-done((f32[8,128]{1,0:T(8,128)S(1)}, f32[8,128]{1,0:T(8,128)S(1)}, u32[]{:S(2)}, u32[]{:S(2)}) %collective-permute-start.13) | collective-permute-done | bytes 4128 | tf_op jit(solution)/shard_map/ppermute | solution.py:697
  57.0 3.6 %collective-permute-done.14 = f32[8,128]{1,0:T(8,128)S(1)} collective-permute-done((f32[8,128]{1,0:T(8,128)S(1)}, f32[8,128]{1,0:T(8,128)S(1)}, u32[]{:S(2)}, u32[]{:S(2)}) %collective-permute-start.14) | collective-permute-done | bytes 4128 | tf_op jit(solution)/shard_map/ppermute | solution.py:697
  60.6 2.6 %collective-permute-start.15 = (f32[8,128]{1,0:T(8,128)S(1)}, f32[8,128]{1,0:T(8,128)S(1)}, u32[]{:S(2)}, u32[]{:S(2)}) collective-permute-start(f32[8,128]{1,0:T(8,128)S(1)} %add.24), channel_id=1, source_target_pairs={{0,96},{32,64},{64,32},{96,0},{1,97},{33,65},{65,33},{97,1},{2,98}... | collective-permute-start | bytes 12296 | tf_op jit(solution)/shard_map/ppermute | solution.py:697
  63.2 2.3 %collective-permute-done.15 = f32[8,128]{1,0:T(8,128)S(1)} collective-permute-done((f32[8,128]{1,0:T(8,128)S(1)}, f32[8,128]{1,0:T(8,128)S(1)}, u32[]{:S(2)}, u32[]{:S(2)}) %collective-permute-start.15) | collective-permute-done | bytes 4128 | tf_op jit(solution)/shard_map/ppermute | solution.py:697
  65.5 1.6 %collective-permute-start.16 = (f32[8,128]{1,0:T(8,128)S(1)}, f32[8,128]{1,0:T(8,128)S(1)}, u32[]{:S(2)}, u32[]{:S(2)}) collective-permute-start(f32[8,128]{1,0:T(8,128)S(1)} %add.25), channel_id=1, source_target_pairs={{0,1},{1,0},{2,3},{3,2},{4,5},{5,4},{6,7},{7,6},{8,9},{9,8},{10,11... | collective-permute-start | bytes 12296 | tf_op jit(solution)/shard_map/ppermute | solution.py:697
  67.1 2.0 %collective-permute-done.16 = f32[8,128]{1,0:T(8,128)S(1)} collective-permute-done((f32[8,128]{1,0:T(8,128)S(1)}, f32[8,128]{1,0:T(8,128)S(1)}, u32[]{:S(2)}, u32[]{:S(2)}) %collective-permute-start.16) | collective-permute-done | bytes 4128 | tf_op jit(solution)/shard_map/ppermute | solution.py:697
  69.1 2.8 %collective-permute-start.17 = (f32[8,128]{1,0:T(8,128)S(1)}, f32[8,128]{1,0:T(8,128)S(1)}, u32[]{:S(2)}, u32[]{:S(2)}) collective-permute-start(f32[8,128]{1,0:T(8,128)S(1)} %add.26), channel_id=1, source_target_pairs={{0,3},{1,2},{2,1},{3,0},{4,7},{5,6},{6,5},{7,4},{8,11},{9,10},{10,... | collective-permute-start | bytes 12296 | tf_op jit(solution)/shard_map/ppermute | solution.py:697
  73.9 5.2 %k_last.1 = (f32[8,16,32,128]{3,2,1,0:T(8,128)}, f32[8,16,32,128]{3,2,1,0:T(8,128)}) custom-call(f32[8,128]{1,0:T(8,128)S(1)} %add.27.refs_0_, f32[8,16,32,128]{3,2,1,0:T(8,128)S(1)} %get-tuple-element.53.refs_0_.refs_1_, f32[8,16,32,128]{3,2,1,0:T(8,128)S(1)} %get-tuple-element.71.refs_7_.refs_1_.refs_2_, f32[8,16,32,128]{3,2,1,0:T(8,128)S(1)} %get-tuple-element.74.refs_3_, ...), custom_call_target="tpu_custom_call" | custom-call | tf_op jit(solution)/shard_map/k_last/pallas_call | solution.py:38
  (40 shorter events, 13.4 us)
Async XLA Ops:
  0.6 7.4 %copy-start = (f32[14,16,32,128]{3,2,1,0:T(8,128)S(1)}, f32[14,16,32,128]{3,2,1,0:T(8,128)}, u32[]{:S(2)}) copy-start(f32[14,16,32,128]{3,2,1,0:T(8,128)} %refs_1_.7) | copy-start | bytes 11010052
  3.7 6.3 %collective-permute-start = (f32[9,8,128]{2,1,0:T(8,128)S(1)}, f32[9,8,128]{2,1,0:T(8,128)S(1)}, u32[]{:S(2)}, u32[]{:S(2)}) collective-permute-start(f32[9,8,128]{2,1,0:T(8,128)S(1)} %get-tuple-element.43), channel_id=1, source_target_pairs={{0,1},{1,2},{2,3},{3,0},{4,5},{5,6},{6,7},{7,4},{8,9},{9,10},{10,1... | collective-permute-start | bytes 110600 | tf_op jit(solution)/shard_map/ppermute | solution.py:690
  5.8 4.2 %collective-permute-start.1 = (f32[9,8,128]{2,1,0:T(8,128)S(1)}, f32[9,8,128]{2,1,0:T(8,128)S(1)}, u32[]{:S(2)}, u32[]{:S(2)}) collective-permute-start(f32[9,8,128]{2,1,0:T(8,128)S(1)} %get-tuple-element.44), channel_id=1, source_target_pairs={{0,3},{1,0},{2,1},{3,2},{4,7},{5,4},{6,5},{7,6},{8,11},{9,8},{10,9... | collective-permute-start | bytes 110600 | tf_op jit(solution)/shard_map/ppermute | solution.py:690
  10.2 5.9 %collective-permute-start.2 = (f32[36,8,128]{2,1,0:T(8,128)S(1)}, f32[36,8,128]{2,1,0:T(8,128)S(1)}, u32[]{:S(2)}, u32[]{:S(2)}) collective-permute-start(f32[36,8,128]{2,1,0:T(8,128)S(1)} %get-tuple-element.45.refs_6_.refs_1_), channel_id=1, source_target_pairs={{0,4},{4,8},{8,12},{12,16},{16,20},{20,24},{24,28},{28,0},{1,5},{5... | collective-permute-start | bytes 442376 | tf_op jit(solution)/shard_map/ppermute | solution.py:690
  10.2 5.9 %collective-permute-start.3 = (f32[30,8,128]{2,1,0:T(8,128)S(1)}, f32[30,8,128]{2,1,0:T(8,128)S(1)}, u32[]{:S(2)}, u32[]{:S(2)}) collective-permute-start(f32[30,8,128]{2,1,0:T(8,128)S(1)} %get-tuple-element.52), channel_id=1, source_target_pairs={{0,28},{4,0},{8,4},{12,8},{16,12},{20,16},{24,20},{28,24},{1,29},{... | collective-permute-start | bytes 368648 | tf_op jit(solution)/shard_map/ppermute | solution.py:690
  16.4 9.7 %collective-permute-start.4 = (f32[40,8,128]{2,1,0:T(8,128)S(1)}, f32[40,8,128]{2,1,0:T(8,128)S(1)}, u32[]{:S(2)}, u32[]{:S(2)}) collective-permute-start(f32[40,8,128]{2,1,0:T(8,128)S(1)} %get-tuple-element.55), channel_id=1, source_target_pairs={{0,96},{32,0},{64,32},{96,64},{1,97},{33,1},{65,33},{97,65},{2,98}... | collective-permute-start | bytes 491528 | tf_op jit(solution)/shard_map/ppermute | solution.py:690
  19.5 6.6 %collective-permute-start.5 = (f32[36,8,128]{2,1,0:T(8,128)S(1)}, f32[36,8,128]{2,1,0:T(8,128)S(1)}, u32[]{:S(2)}, u32[]{:S(2)}) collective-permute-start(f32[36,8,128]{2,1,0:T(8,128)S(1)} %get-tuple-element.56), channel_id=1, source_target_pairs={{0,32},{32,64},{64,96},{96,0},{1,33},{33,65},{65,97},{97,1},{2,34}... | collective-permute-start | bytes 442376 | tf_op jit(solution)/shard_map/ppermute | solution.py:690
  27.3 5.0 %collective-permute-start.6 = (f32[4,8,128]{2,1,0:T(8,128)S(1)}, f32[4,8,128]{2,1,0:T(8,128)S(1)}, u32[]{:S(2)}, u32[]{:S(2)}) collective-permute-start(f32[4,8,128]{2,1,0:T(8,128)S(1)} %get-tuple-element.60), channel_id=1, source_target_pairs={{0,1},{1,2},{2,3},{3,0},{4,5},{5,6},{6,7},{7,4},{8,9},{9,10},{10,1... | collective-permute-start | bytes 49160 | tf_op jit(solution)/shard_map/ppermute | solution.py:690
  29.1 3.7 %collective-permute-start.7 = (f32[4,8,128]{2,1,0:T(8,128)S(1)}, f32[4,8,128]{2,1,0:T(8,128)S(1)}, u32[]{:S(2)}, u32[]{:S(2)}) collective-permute-start(f32[4,8,128]{2,1,0:T(8,128)S(1)} %get-tuple-element.61), channel_id=1, source_target_pairs={{0,3},{1,0},{2,1},{3,2},{4,7},{5,4},{6,5},{7,6},{8,11},{9,8},{10,9... | collective-permute-start | bytes 49160 | tf_op jit(solution)/shard_map/ppermute | solution.py:690
  32.9 6.3 %collective-permute-start.8 = (f32[24,8,128]{2,1,0:T(8,128)S(1)}, f32[24,8,128]{2,1,0:T(8,128)S(1)}, u32[]{:S(2)}, u32[]{:S(2)}) collective-permute-start(f32[24,8,128]{2,1,0:T(8,128)S(1)} %get-tuple-element.62.refs_4_.refs_3_), channel_id=1, source_target_pairs={{0,4},{4,8},{8,12},{12,16},{16,20},{20,24},{24,28},{28,0},{1,5},{5... | collective-permute-start | bytes 294920 | tf_op jit(solution)/shard_map/ppermute | solution.py:690
  32.9 6.3 %collective-permute-start.9 = (f32[24,8,128]{2,1,0:T(8,128)S(1)}, f32[24,8,128]{2,1,0:T(8,128)S(1)}, u32[]{:S(2)}, u32[]{:S(2)}) collective-permute-start(f32[24,8,128]{2,1,0:T(8,128)S(1)} %get-tuple-element.66), channel_id=1, source_target_pairs={{0,28},{4,0},{8,4},{12,8},{16,12},{20,16},{24,20},{28,24},{1,29},{... | collective-permute-start | bytes 294920 | tf_op jit(solution)/shard_map/ppermute | solution.py:690
  39.4 6.3 %collective-permute-start.10 = (f32[40,8,128]{2,1,0:T(8,128)S(1)}, f32[40,8,128]{2,1,0:T(8,128)S(1)}, u32[]{:S(2)}, u32[]{:S(2)}) collective-permute-start(f32[40,8,128]{2,1,0:T(8,128)S(1)} %get-tuple-element.69), channel_id=1, source_target_pairs={{0,96},{32,0},{64,32},{96,64},{1,97},{33,1},{65,33},{97,65},{2,98}... | collective-permute-start | bytes 491528 | tf_op jit(solution)/shard_map/ppermute | solution.py:690
  40.8 31.1 %collective-permute-start.18 = (f32[32,8,128]{2,1,0:T(8,128)S(1)}, f32[32,8,128]{2,1,0:T(8,128)S(1)}, u32[]{:S(2)}, u32[]{:S(2)}) collective-permute-start(f32[32,8,128]{2,1,0:T(8,128)S(1)} %get-tuple-element.70.refs_6_), channel_id=1, source_target_pairs={{0,32},{32,64},{64,96},{96,0},{1,33},{33,65},{65,97},{97,1},{2,34}... | collective-permute-start | bytes 393224 | tf_op jit(solution)/shard_map/ppermute | solution.py:690
  47.4 1.2 %collective-permute-start.11 = (f32[8,128]{1,0:T(8,128)S(1)}, f32[8,128]{1,0:T(8,128)S(1)}, u32[]{:S(2)}, u32[]{:S(2)}) collective-permute-start(f32[8,128]{1,0:T(8,128)S(1)} %get-tuple-element.72), channel_id=1, source_target_pairs={{0,4},{4,0},{8,12},{12,8},{16,20},{20,16},{24,28},{28,24},{1,5},{5... | collective-permute-start | bytes 12296 | tf_op jit(solution)/shard_map/ppermute | solution.py:697
  48.6 3.6 %collective-permute-start.12 = (f32[8,128]{1,0:T(8,128)S(1)}, f32[8,128]{1,0:T(8,128)S(1)}, u32[]{:S(2)}, u32[]{:S(2)}) collective-permute-start(f32[8,128]{1,0:T(8,128)S(1)} %add.21), channel_id=1, source_target_pairs={{0,8},{4,12},{8,0},{12,4},{16,24},{20,28},{24,16},{28,20},{1,9},{5... | collective-permute-start | bytes 12296 | tf_op jit(solution)/shard_map/ppermute | solution.py:697
  52.2 4.8 %collective-permute-start.13 = (f32[8,128]{1,0:T(8,128)S(1)}, f32[8,128]{1,0:T(8,128)S(1)}, u32[]{:S(2)}, u32[]{:S(2)}) collective-permute-start(f32[8,128]{1,0:T(8,128)S(1)} %add.22), channel_id=1, source_target_pairs={{0,24},{4,28},{8,16},{12,20},{16,8},{20,12},{24,0},{28,4},{1,25},{... | collective-permute-start | bytes 12296 | tf_op jit(solution)/shard_map/ppermute | solution.py:697
  57.0 3.6 %collective-permute-start.14 = (f32[8,128]{1,0:T(8,128)S(1)}, f32[8,128]{1,0:T(8,128)S(1)}, u32[]{:S(2)}, u32[]{:S(2)}) collective-permute-start(f32[8,128]{1,0:T(8,128)S(1)} %add.23), channel_id=1, source_target_pairs={{0,32},{32,0},{64,96},{96,64},{1,33},{33,1},{65,97},{97,65},{2,34}... | collective-permute-start | bytes 12296 | tf_op jit(solution)/shard_map/ppermute | solution.py:697
  60.6 4.8 %collective-permute-start.15 = (f32[8,128]{1,0:T(8,128)S(1)}, f32[8,128]{1,0:T(8,128)S(1)}, u32[]{:S(2)}, u32[]{:S(2)}) collective-permute-start(f32[8,128]{1,0:T(8,128)S(1)} %add.24), channel_id=1, source_target_pairs={{0,96},{32,64},{64,32},{96,0},{1,97},{33,65},{65,33},{97,1},{2,98}... | collective-permute-start | bytes 12296 | tf_op jit(solution)/shard_map/ppermute | solution.py:697
  65.5 3.6 %collective-permute-start.16 = (f32[8,128]{1,0:T(8,128)S(1)}, f32[8,128]{1,0:T(8,128)S(1)}, u32[]{:S(2)}, u32[]{:S(2)}) collective-permute-start(f32[8,128]{1,0:T(8,128)S(1)} %add.25), channel_id=1, source_target_pairs={{0,1},{1,0},{2,3},{3,2},{4,5},{5,4},{6,7},{7,6},{8,9},{9,8},{10,11... | collective-permute-start | bytes 12296 | tf_op jit(solution)/shard_map/ppermute | solution.py:697
  69.1 4.8 %collective-permute-start.17 = (f32[8,128]{1,0:T(8,128)S(1)}, f32[8,128]{1,0:T(8,128)S(1)}, u32[]{:S(2)}, u32[]{:S(2)}) collective-permute-start(f32[8,128]{1,0:T(8,128)S(1)} %add.26), channel_id=1, source_target_pairs={{0,3},{1,2},{2,1},{3,0},{4,7},{5,6},{6,5},{7,4},{8,11},{9,10},{10,... | collective-permute-start | bytes 12296 | tf_op jit(solution)/shard_map/ppermute | solution.py:697

commit v4 on v3

--- a/solution.py
+++ b/solution.py
@@ -369,7 +369,8 @@
     interior((vi, vm, vp), st, wz, acc, diag_of)
 
 
-def inner_again_kernel(vi, vm, vp, st, wz, diag, acc):
+def inner_again_kernel(vi, vm, vp, st, wz, diag, xp, acc, sent):
+    sent[...] = xp[...]
     interior((vi, vm, vp), st, wz, acc, lambda x, y, first: diag[x, pl.ds(y, 1), :])
 
 
@@ -690,12 +691,14 @@
     return lax.ppermute(x, axis, [(i, (i + step) % n) for i in range(n)])
 
 
-def everywhere(x):
-    for axis, bits in (("gy", (1, 2, 6)), ("gx", (1, 3)), ("gz", (1, 3))):
-        n = lax.axis_size(axis)
-        for bit in bits:
-            x = x + lax.ppermute(x, axis, [(i, i ^ bit) for i in range(n)])
-    return x
+def ring_sum(x, axis, stride):
+    left, right, across = (shift(x, axis, n * stride) for n in (1, -1, 2))
+    return (x + across) + (left + right)
+
+
+def other_core(x):
+    n = lax.axis_size("gy")
+    return lax.ppermute(x, "gy", [(i, i ^ 1) for i in range(n)])
 
 
 def shards(rhs, stencil):
@@ -721,10 +724,9 @@
         ends_kernel, "k_ends", [vm, vp, wz, st, rl, rr],
         [full, full, (9, X, Y, Z), (5, X, Y, Z)], aliases={0: 0, 1: 1, 2: 2}, after=[yp],
     )
-    (g0,) = call(gram_first_kernel, "k_gram0", [rc], [tile], after=[yp])
     ring, xm, xp = call(
         third_kernel(True), "k_third", [vi, vm, vp, st, wz, rl, rr, qm, qp, sums],
-        [(2, 3, X, *tile), (Y + 8, *tile), (Y + 4, *tile)], after=[g0],
+        [(2, 3, X, *tile), (Y + 8, *tile), (Y + 4, *tile)],
     )
     tp = shift(xm, "gx", -1)
     tm = shift(xp, "gx", 1)
@@ -737,8 +739,9 @@
     rl = shift(zp, "gz", 1)
     rr = shift(zm, "gz", -1)
     vm, vp = call(roll_fields, "k_roll2", [y1], [full, full])
+    (g0,) = call(gram_first_kernel, "k_gram0", [rc], [tile], after=[zp])
     yp, ym = call(
-        edge_again_kernel, "k_edge2", [y1, rl, rr], [(24, *tile), (24, *tile)], after=[vm]
+        edge_again_kernel, "k_edge2", [y1, rl, rr], [(24, *tile), (24, *tile)], after=[vm, g0]
     )
     qmv = shift(yp, "gy", 1)
     qpv = shift(ym, "gy", -1)
@@ -752,15 +755,18 @@
         [(2, 3, X, *tile), (Y + 8, *tile), (Y, *tile)], after=[g2],
     )
     tp = shift(xm, "gx", -1)
+    acc, xp = call(
+        inner_again_kernel, "k_inner2", [y1, vm, vp, st, wz, diag, xp], [full, (Y, *tile)]
+    )
     tm = shift(xp, "gx", 1)
-    (acc,) = call(inner_again_kernel, "k_inner2", [y1, vm, vp, st, wz, diag], [full])
     _, y2f, moment = call(
         late_kernel, "k_late", [acc, st, ring, qm, qp, tp, xp, y1f, g2],
         [full, compact, tile], aliases={0: 0},
         scratch=[pltpu.VMEM((F, 1, Y, Z), F32), pltpu.VMEM((F, 1, Y, Z), F32)],
     )
     d0, d1 = call(differences_kernel, "k_diff", [rc, y1f, y2f, tm], [compact, compact])
-    moment = everywhere(moment)
+    moment = ring_sum(ring_sum(moment, "gx", 1), "gz", 1)
+    moment = ring_sum(moment + other_core(moment), "gy", 2)
     sol, res = call(
         last_kernel, "k_last", [moment, rc, y1f, d0, d1], [compact, compact],
         out_specs=[FAR, FAR],

time: 79.2 us -> 74.4 us (0.939)
  waiting for transfers between devices: 19.3 us -> 9.43 us
  starting transfers between devices: 28.3 us -> 33 us
    ppermute x7 -> x1, waiting for transfers between devices: 16.5 us -> 1.15 us  [other_core(): return lax.ppermute(x, 'gy', [(i, i ^ 1) for i in range(n)])]
    ppermute x12 -> x21, starting transfers between devices: 18.7 us -> 33 us  [shift(): return lax.ppermute(x, axis, [(i, (i + step) % n) for i in range(n)])]
    ppermute x7 -> x1, starting transfers between devices: 9.59 us -> 0.09 us  [other_core(): return lax.ppermute(x, 'gy', [(i, i ^ 1) for i in range(n)])]
    ppermute x12 -> x21, waiting for transfers between devices: 2.75 us -> 8.28 us  [shift(): return lax.ppermute(x, axis, [(i, (i + step) % n) for i in range(n)])]
  transfers between devices with their start and end apart: 19 -> 22, of which waited for: 10 -> 9; matrix products, arithmetic and copies ran while one was open for 0% -> 0% of each run, Pallas kernels for 26% -> 25%
where the time goes in v4:
time: 74.4 us; the launch traced here: 74 us
  starting transfers between devices  33 us (44%)
  Pallas kernels  30.6 us (41%)
  waiting for transfers between devices  9.43 us (13%)
  between operations  0.84 us (1%)
    ppermute x21, starting transfers between devices, shift(): return lax.ppermute(x, axis, [(i, (i + step) % n) for i in range(n)])  33 us
    pallas_call x17, Pallas kernels, call(): pl.pallas_call(run, name=name, out_shape=[jax.ShapeDtypeStruct(s, F32) fo...  30.6 us
    ppermute x21, waiting for transfers between devices, shift(): return lax.ppermute(x, axis, [(i, (i + step) % n) for i in range(n)])  8.28 us
  transfers between devices with their start and end apart: 22, of which 9 were waited for; matrix products, arithmetic and copies ran while one was open for 0% of the time, Pallas kernels for 25%

profile of v4, /device:TPU:0, one launch (start us, length us, event | category | flops | bytes accessed | tf_op | source)
XLA Modules:
  0.0 74.0 jit_solution(17897929409333457805)
XLA Ops:
  0.6 3.0 %k_start.1 = (f32[8,16,32,128]{3,2,1,0:T(8,128)S(1)}, f32[16,32,8,128]{3,2,1,0:T(8,128)S(1)}, f32[9,8,128]{2,1,0:T(8,128)S(1)}, f32[9,8,128]{2,1,0:T(8,128)S(1)}) custom-call(f32[8,16,32,128]{3,2,1,0:T(8,128)} %refs_0_.1, f32[14,16,32,128]{3,2,1,0:T(8,128)} %refs_1_.7), custom_call_target="tpu_custom_call" | custom-call | tf_op jit(solution)/shard_map/k_start/pallas_call | solution.py:38
  3.7 2.1 %collective-permute-start = (f32[9,8,128]{2,1,0:T(8,128)S(1)}, f32[9,8,128]{2,1,0:T(8,128)S(1)}, u32[]{:S(2)}, u32[]{:S(2)}) collective-permute-start(f32[9,8,128]{2,1,0:T(8,128)S(1)} %get-tuple-element.45), channel_id=1, source_target_pairs={{0,1},{1,2},{2,3},{3,0},{4,5},{5,6},{6,7},{7,4},{8,9},{9,10},{10,1... | collective-permute-start | bytes 110600 | tf_op jit(solution)/shard_map/ppermute | solution.py:691
  5.8 2.2 %collective-permute-start.1 = (f32[9,8,128]{2,1,0:T(8,128)S(1)}, f32[9,8,128]{2,1,0:T(8,128)S(1)}, u32[]{:S(2)}, u32[]{:S(2)}) collective-permute-start(f32[9,8,128]{2,1,0:T(8,128)S(1)} %get-tuple-element.46), channel_id=1, source_target_pairs={{0,3},{1,0},{2,1},{3,2},{4,7},{5,4},{6,5},{7,6},{8,11},{9,8},{10,9... | collective-permute-start | bytes 110600 | tf_op jit(solution)/shard_map/ppermute | solution.py:691
  8.0 1.9 %k_roll.1 = (f32[16,32,8,128]{3,2,1,0:T(8,128)S(1)}, f32[16,32,8,128]{3,2,1,0:T(8,128)S(1)}, f32[9,16,32,128]{3,2,1,0:T(8,128)S(1)}) custom-call(f32[16,32,8,128]{3,2,1,0:T(8,128)S(1)} %get-tuple-element.41.refs_0_.refs_2_, f32[14,16,32,128]{3,2,1,0:T(8,128)S(1)} %copy-done), custom_call_target="tpu_custom_call" | custom-call | tf_op jit(solution)/shard_map/k_roll/pallas_call | solution.py:38
  10.2 2.9 %collective-permute-start.3 = (f32[30,8,128]{2,1,0:T(8,128)S(1)}, f32[30,8,128]{2,1,0:T(8,128)S(1)}, u32[]{:S(2)}, u32[]{:S(2)}) collective-permute-start(f32[30,8,128]{2,1,0:T(8,128)S(1)} %get-tuple-element.54), channel_id=1, source_target_pairs={{0,28},{4,0},{8,4},{12,8},{16,12},{20,16},{24,20},{28,24},{1,29},{... | collective-permute-start | bytes 368648 | tf_op jit(solution)/shard_map/ppermute | solution.py:691
  13.2 2.1 %k_ends.1 = (f32[16,32,8,128]{3,2,1,0:T(8,128)S(1)}, f32[16,32,8,128]{3,2,1,0:T(8,128)S(1)}, f32[9,16,32,128]{3,2,1,0:T(8,128)S(1)}, f32[5,16,32,128]{3,2,1,0:T(8,128)S(1)}) custom-call(f32[16,32,8,128]{3,2,1,0:T(8,128)S(1)} %get-tuple-element.42.refs_0_, ...), custom_call_target="tpu_custom_call", output_to_operand_aliasing={{0}: (0, {}), {1}: (1, {}), {2}: (2, {})} | custom-call | tf_op jit(solution)/shard_map/k_ends/pallas_call | solution.py:38
  16.2 3.1 %collective-permute-start.4 = (f32[40,8,128]{2,1,0:T(8,128)S(1)}, f32[40,8,128]{2,1,0:T(8,128)S(1)}, u32[]{:S(2)}, u32[]{:S(2)}) collective-permute-start(f32[40,8,128]{2,1,0:T(8,128)S(1)} %get-tuple-element.56), channel_id=1, source_target_pairs={{0,96},{32,0},{64,32},{96,64},{1,97},{33,1},{65,33},{97,65},{2,98}... | collective-permute-start | bytes 491528 | tf_op jit(solution)/shard_map/ppermute | solution.py:691
  19.3 4.6 %k_inner.1 = (f32[16,32,8,128]{3,2,1,0:T(8,128)S(1)}, f32[16,32,128]{2,1,0:T(8,128)S(1)}) custom-call(f32[16,32,8,128]{3,2,1,0:T(8,128)S(1)} %get-tuple-element.41.refs_0_.refs_2_, f32[16,32,8,128]{3,2,1,0:T(8,128)S(1)} %get-tuple-element.48.refs_1_, f32[16,32,8,128]{3,2,1,0:T(8,128)S(1)} %get-tuple-element.49.refs_2_, f32[14,16,32,128]{3,2,1,0:T(8,128)S(1)} %copy-done, ...), custom_call_target="tpu_custom_call" | custom-call | tf_op jit(solution)/shard_map/k_inner/pallas_call | solution.py:38
  23.9 2.2 %collective-permute-done.5.refs_8_ = f32[36,8,128]{2,1,0:T(8,128)S(1)} collective-permute-done((f32[36,8,128]{2,1,0:T(8,128)S(1)}, f32[36,8,128]{2,1,0:T(8,128)S(1)}, u32[]{:S(2)}, u32[]{:S(2)}) %collective-permute-start.5) | collective-permute-done | bytes 147488 | tf_op jit(solution)/shard_map/ppermute | solution.py:691
  27.3 1.8 %collective-permute-start.6 = (f32[4,8,128]{2,1,0:T(8,128)S(1)}, f32[4,8,128]{2,1,0:T(8,128)S(1)}, u32[]{:S(2)}, u32[]{:S(2)}) collective-permute-start(f32[4,8,128]{2,1,0:T(8,128)S(1)} %get-tuple-element.61.refs_1_), channel_id=1, source_target_pairs={{0,1},{1,2},{2,3},{3,0},{4,5},{5,6},{6,7},{7,4},{8,9},{9,10},{10,1... | collective-permute-start | bytes 49160 | tf_op jit(solution)/shard_map/ppermute | solution.py:691
  29.0 1.6 %collective-permute-start.7 = (f32[4,8,128]{2,1,0:T(8,128)S(1)}, f32[4,8,128]{2,1,0:T(8,128)S(1)}, u32[]{:S(2)}, u32[]{:S(2)}) collective-permute-start(f32[4,8,128]{2,1,0:T(8,128)S(1)} %get-tuple-element.62), channel_id=1, source_target_pairs={{0,3},{1,0},{2,1},{3,2},{4,7},{5,4},{6,5},{7,6},{8,11},{9,8},{10,9... | collective-permute-start | bytes 49160 | tf_op jit(solution)/shard_map/ppermute | solution.py:691
  31.5 1.3 %k_roll2.1 = (f32[16,32,8,128]{3,2,1,0:T(8,128)S(1)}, f32[16,32,8,128]{3,2,1,0:T(8,128)S(1)}) custom-call(f32[16,32,8,128]{3,2,1,0:T(8,128)S(1)} %get-tuple-element.58.refs_0_.refs_1_), custom_call_target="tpu_custom_call" | custom-call | tf_op jit(solution)/shard_map/k_roll2/pallas_call | solution.py:38
  33.0 2.9 %collective-permute-start.9 = (f32[24,8,128]{2,1,0:T(8,128)S(1)}, f32[24,8,128]{2,1,0:T(8,128)S(1)}, u32[]{:S(2)}, u32[]{:S(2)}) collective-permute-start(f32[24,8,128]{2,1,0:T(8,128)S(1)} %get-tuple-element.68), channel_id=1, source_target_pairs={{0,28},{4,0},{8,4},{12,8},{16,12},{20,16},{24,20},{28,24},{1,29},{... | collective-permute-start | bytes 294920 | tf_op jit(solution)/shard_map/ppermute | solution.py:691
  35.9 2.2 %k_gram12.1 = (f32[8,16,32,128]{3,2,1,0:T(8,128)S(1)}, f32[8,128]{1,0:T(8,128)S(1)}) custom-call(f32[8,16,32,128]{3,2,1,0:T(8,128)S(1)} %get-tuple-element.63.refs_0_.refs_1_, f32[16,32,8,128]{3,2,1,0:T(8,128)S(1)} %get-tuple-element.58.refs_0_.refs_1_, f32[8,128]{1,0:T(8,128)S(1)} %k_gram0.1.refs_4_.refs_2_, f32[24,8,128]{2,1,0:T(8,128)S(1)} %get-tuple-element.64.refs_4_.refs_3_), custom_call_target="tpu_custom_call" | custom-call | tf_op jit(solution)/shard_map/k_gram12/pallas_call | solution.py:38
  40.6 4.2 %k_inner2.1 = (f32[16,32,8,128]{3,2,1,0:T(8,128)S(1)}, f32[32,8,128]{2,1,0:T(8,128)S(1)}) custom-call(f32[16,32,8,128]{3,2,1,0:T(8,128)S(1)} %get-tuple-element.58.refs_0_.refs_1_, f32[16,32,8,128]{3,2,1,0:T(8,128)S(1)} %get-tuple-element.65.refs_1_, f32[16,32,8,128]{3,2,1,0:T(8,128)S(1)} %get-tuple-element.66.refs_2_, f32[14,16,32,128]{3,2,1,0:T(8,128)S(1)} %copy-done, ...), custom_call_target="tpu_custom_call" | custom-call | tf_op jit(solution)/shard_map/k_inner2/pallas_call | solution.py:38
  44.8 1.6 %k_late.1 = (f32[16,32,8,128]{3,2,1,0:T(8,128)S(1)}, f32[8,16,32,128]{3,2,1,0:T(8,128)S(1)}, f32[8,128]{1,0:T(8,128)S(1)}) custom-call(f32[16,32,8,128]{3,2,1,0:T(8,128)S(1)} %get-tuple-element.71.refs_0_, f32[14,16,32,128]{3,2,1,0:T(8,128)S(1)} %copy-done, f32[2,3,16,8,128]{4,3,2,1,0:T(8,128)S(1)} %get-tuple-element.72.refs_2_, ...), custom_call_target="tpu_custom_call", output_to_operand_aliasing={{0}: (0, {})} | custom-call | tf_op jit(solution)/shard_map/k_late/pallas_call | solution.py:38
  47.1 2.6 %collective-permute-start.12 = (f32[8,128]{1,0:T(8,128)S(1)}, f32[8,128]{1,0:T(8,128)S(1)}, u32[]{:S(2)}, u32[]{:S(2)}) collective-permute-start(f32[8,128]{1,0:T(8,128)S(1)} %get-tuple-element.76), channel_id=1, source_target_pairs={{0,32},{32,64},{64,96},{96,0},{1,33},{33,65},{65,97},{97,1},{2,34}... | collective-permute-start | bytes 12296 | tf_op jit(solution)/shard_map/ppermute | solution.py:691
  50.3 1.4 %collective-permute-done.11 = f32[8,128]{1,0:T(8,128)S(1)} collective-permute-done((f32[8,128]{1,0:T(8,128)S(1)}, f32[8,128]{1,0:T(8,128)S(1)}, u32[]{:S(2)}, u32[]{:S(2)}) %collective-permute-start.11) | collective-permute-done | bytes 4128 | tf_op jit(solution)/shard_map/ppermute | solution.py:691
  51.9 1.4 %collective-permute-done.13 = f32[8,128]{1,0:T(8,128)S(1)} collective-permute-done((f32[8,128]{1,0:T(8,128)S(1)}, f32[8,128]{1,0:T(8,128)S(1)}, u32[]{:S(2)}, u32[]{:S(2)}) %collective-permute-start.13) | collective-permute-done | bytes 4128 | tf_op jit(solution)/shard_map/ppermute | solution.py:691
  53.3 2.9 %collective-permute-start.14 = (f32[8,128]{1,0:T(8,128)S(1)}, f32[8,128]{1,0:T(8,128)S(1)}, u32[]{:S(2)}, u32[]{:S(2)}) collective-permute-start(f32[8,128]{1,0:T(8,128)S(1)} %add_add_fusion.2), channel_id=1, source_target_pairs={{0,2},{1,3},{2,0},{3,1},{4,6},{5,7},{6,4},{7,5},{8,10},{9,11},{10,... | collective-permute-start | bytes 12296 | tf_op jit(solution)/shard_map/ppermute | solution.py:691
  56.9 2.6 %collective-permute-start.16 = (f32[8,128]{1,0:T(8,128)S(1)}, f32[8,128]{1,0:T(8,128)S(1)}, u32[]{:S(2)}, u32[]{:S(2)}) collective-permute-start(f32[8,128]{1,0:T(8,128)S(1)} %add_add_fusion.2), channel_id=1, source_target_pairs={{0,3},{1,0},{2,1},{3,2},{4,7},{5,4},{6,5},{7,6},{8,11},{9,8},{10,9... | collective-permute-start | bytes 12296 | tf_op jit(solution)/shard_map/ppermute | solution.py:691
  62.3 1.7 %collective-permute-start.18 = (f32[8,128]{1,0:T(8,128)S(1)}, f32[8,128]{1,0:T(8,128)S(1)}, u32[]{:S(2)}, u32[]{:S(2)}) collective-permute-start(f32[8,128]{1,0:T(8,128)S(1)} %add.36), channel_id=1, source_target_pairs={{0,16},{4,20},{8,24},{12,28},{16,0},{20,4},{24,8},{28,12},{1,17},{... | collective-permute-start | bytes 12296 | tf_op jit(solution)/shard_map/ppermute | solution.py:691
  64.6 2.6 %collective-permute-start.20 = (f32[8,128]{1,0:T(8,128)S(1)}, f32[8,128]{1,0:T(8,128)S(1)}, u32[]{:S(2)}, u32[]{:S(2)}) collective-permute-start(f32[8,128]{1,0:T(8,128)S(1)} %add.36), channel_id=1, source_target_pairs={{0,24},{4,28},{8,0},{12,4},{16,8},{20,12},{24,16},{28,20},{1,25},{... | collective-permute-start | bytes 12296 | tf_op jit(solution)/shard_map/ppermute | solution.py:691
  68.7 5.2 %k_last.1 = (f32[8,16,32,128]{3,2,1,0:T(8,128)}, f32[8,16,32,128]{3,2,1,0:T(8,128)}) custom-call(f32[8,128]{1,0:T(8,128)S(1)} %add_add_fusion.refs_0_, f32[8,16,32,128]{3,2,1,0:T(8,128)S(1)} %get-tuple-element.63.refs_0_.refs_1_, f32[8,16,32,128]{3,2,1,0:T(8,128)S(1)} %get-tuple-element.75.refs_7_.refs_1_.refs_2_, ...), custom_call_target="tpu_custom_call" | custom-call | tf_op jit(solution)/shard_map/k_last/pallas_call | solution.py:38
  (43 shorter events, 13.0 us)
Async XLA Ops:
  0.6 7.4 %copy-start = (f32[14,16,32,128]{3,2,1,0:T(8,128)S(1)}, f32[14,16,32,128]{3,2,1,0:T(8,128)}, u32[]{:S(2)}) copy-start(f32[14,16,32,128]{3,2,1,0:T(8,128)} %refs_1_.7) | copy-start | bytes 11010052
  3.7 6.3 %collective-permute-start = (f32[9,8,128]{2,1,0:T(8,128)S(1)}, f32[9,8,128]{2,1,0:T(8,128)S(1)}, u32[]{:S(2)}, u32[]{:S(2)}) collective-permute-start(f32[9,8,128]{2,1,0:T(8,128)S(1)} %get-tuple-element.45), channel_id=1, source_target_pairs={{0,1},{1,2},{2,3},{3,0},{4,5},{5,6},{6,7},{7,4},{8,9},{9,10},{10,1... | collective-permute-start | bytes 110600 | tf_op jit(solution)/shard_map/ppermute | solution.py:691
  5.8 4.2 %collective-permute-start.1 = (f32[9,8,128]{2,1,0:T(8,128)S(1)}, f32[9,8,128]{2,1,0:T(8,128)S(1)}, u32[]{:S(2)}, u32[]{:S(2)}) collective-permute-start(f32[9,8,128]{2,1,0:T(8,128)S(1)} %get-tuple-element.46), channel_id=1, source_target_pairs={{0,3},{1,0},{2,1},{3,2},{4,7},{5,4},{6,5},{7,6},{8,11},{9,8},{10,9... | collective-permute-start | bytes 110600 | tf_op jit(solution)/shard_map/ppermute | solution.py:691
  10.2 5.8 %collective-permute-start.2 = (f32[36,8,128]{2,1,0:T(8,128)S(1)}, f32[36,8,128]{2,1,0:T(8,128)S(1)}, u32[]{:S(2)}, u32[]{:S(2)}) collective-permute-start(f32[36,8,128]{2,1,0:T(8,128)S(1)} %get-tuple-element.47.refs_6_), channel_id=1, source_target_pairs={{0,4},{4,8},{8,12},{12,16},{16,20},{20,24},{24,28},{28,0},{1,5},{5... | collective-permute-start | bytes 442376 | tf_op jit(solution)/shard_map/ppermute | solution.py:691
  10.2 5.4 %collective-permute-start.3 = (f32[30,8,128]{2,1,0:T(8,128)S(1)}, f32[30,8,128]{2,1,0:T(8,128)S(1)}, u32[]{:S(2)}, u32[]{:S(2)}) collective-permute-start(f32[30,8,128]{2,1,0:T(8,128)S(1)} %get-tuple-element.54), channel_id=1, source_target_pairs={{0,28},{4,0},{8,4},{12,8},{16,12},{20,16},{24,20},{28,24},{1,29},{... | collective-permute-start | bytes 368648 | tf_op jit(solution)/shard_map/ppermute | solution.py:691
  16.2 9.9 %collective-permute-start.4 = (f32[40,8,128]{2,1,0:T(8,128)S(1)}, f32[40,8,128]{2,1,0:T(8,128)S(1)}, u32[]{:S(2)}, u32[]{:S(2)}) collective-permute-start(f32[40,8,128]{2,1,0:T(8,128)S(1)} %get-tuple-element.56), channel_id=1, source_target_pairs={{0,96},{32,0},{64,32},{96,64},{1,97},{33,1},{65,33},{97,65},{2,98}... | collective-permute-start | bytes 491528 | tf_op jit(solution)/shard_map/ppermute | solution.py:691
  19.3 6.8 %collective-permute-start.5 = (f32[36,8,128]{2,1,0:T(8,128)S(1)}, f32[36,8,128]{2,1,0:T(8,128)S(1)}, u32[]{:S(2)}, u32[]{:S(2)}) collective-permute-start(f32[36,8,128]{2,1,0:T(8,128)S(1)} %get-tuple-element.57), channel_id=1, source_target_pairs={{0,32},{32,64},{64,96},{96,0},{1,33},{33,65},{65,97},{97,1},{2,34}... | collective-permute-start | bytes 442376 | tf_op jit(solution)/shard_map/ppermute | solution.py:691
  27.3 5.6 %collective-permute-start.6 = (f32[4,8,128]{2,1,0:T(8,128)S(1)}, f32[4,8,128]{2,1,0:T(8,128)S(1)}, u32[]{:S(2)}, u32[]{:S(2)}) collective-permute-start(f32[4,8,128]{2,1,0:T(8,128)S(1)} %get-tuple-element.61.refs_1_), channel_id=1, source_target_pairs={{0,1},{1,2},{2,3},{3,0},{4,5},{5,6},{6,7},{7,4},{8,9},{9,10},{10,1... | collective-permute-start | bytes 49160 | tf_op jit(solution)/shard_map/ppermute | solution.py:691
  29.0 3.8 %collective-permute-start.7 = (f32[4,8,128]{2,1,0:T(8,128)S(1)}, f32[4,8,128]{2,1,0:T(8,128)S(1)}, u32[]{:S(2)}, u32[]{:S(2)}) collective-permute-start(f32[4,8,128]{2,1,0:T(8,128)S(1)} %get-tuple-element.62), channel_id=1, source_target_pairs={{0,3},{1,0},{2,1},{3,2},{4,7},{5,4},{6,5},{7,6},{8,11},{9,8},{10,9... | collective-permute-start | bytes 49160 | tf_op jit(solution)/shard_map/ppermute | solution.py:691
  33.0 6.3 %collective-permute-start.8 = (f32[24,8,128]{2,1,0:T(8,128)S(1)}, f32[24,8,128]{2,1,0:T(8,128)S(1)}, u32[]{:S(2)}, u32[]{:S(2)}) collective-permute-start(f32[24,8,128]{2,1,0:T(8,128)S(1)} %get-tuple-element.64.refs_4_.refs_3_), channel_id=1, source_target_pairs={{0,4},{4,8},{8,12},{12,16},{16,20},{20,24},{24,28},{28,0},{1,5},{5... | collective-permute-start | bytes 294920 | tf_op jit(solution)/shard_map/ppermute | solution.py:691
  33.0 6.3 %collective-permute-start.9 = (f32[24,8,128]{2,1,0:T(8,128)S(1)}, f32[24,8,128]{2,1,0:T(8,128)S(1)}, u32[]{:S(2)}, u32[]{:S(2)}) collective-permute-start(f32[24,8,128]{2,1,0:T(8,128)S(1)} %get-tuple-element.68), channel_id=1, source_target_pairs={{0,28},{4,0},{8,4},{12,8},{16,12},{20,16},{24,20},{28,24},{1,29},{... | collective-permute-start | bytes 294920 | tf_op jit(solution)/shard_map/ppermute | solution.py:691
  39.5 5.4 %collective-permute-start.10 = (f32[40,8,128]{2,1,0:T(8,128)S(1)}, f32[40,8,128]{2,1,0:T(8,128)S(1)}, u32[]{:S(2)}, u32[]{:S(2)}) collective-permute-start(f32[40,8,128]{2,1,0:T(8,128)S(1)} %get-tuple-element.73), channel_id=1, source_target_pairs={{0,96},{32,0},{64,32},{96,64},{1,97},{33,1},{65,33},{97,65},{2,98}... | collective-permute-start | bytes 491528 | tf_op jit(solution)/shard_map/ppermute | solution.py:691
  46.5 5.2 %collective-permute-start.11 = (f32[8,128]{1,0:T(8,128)S(1)}, f32[8,128]{1,0:T(8,128)S(1)}, u32[]{:S(2)}, u32[]{:S(2)}) collective-permute-start(f32[8,128]{1,0:T(8,128)S(1)} %get-tuple-element.76), channel_id=1, source_target_pairs={{0,64},{32,96},{64,0},{96,32},{1,65},{33,97},{65,1},{97,33},{2,66}... | collective-permute-start | bytes 12296 | tf_op jit(solution)/shard_map/ppermute | solution.py:691
  47.1 4.8 %collective-permute-start.12 = (f32[8,128]{1,0:T(8,128)S(1)}, f32[8,128]{1,0:T(8,128)S(1)}, u32[]{:S(2)}, u32[]{:S(2)}) collective-permute-start(f32[8,128]{1,0:T(8,128)S(1)} %get-tuple-element.76), channel_id=1, source_target_pairs={{0,32},{32,64},{64,96},{96,0},{1,33},{33,65},{65,97},{97,1},{2,34}... | collective-permute-start | bytes 12296 | tf_op jit(solution)/shard_map/ppermute | solution.py:691
  49.7 3.6 %collective-permute-start.13 = (f32[8,128]{1,0:T(8,128)S(1)}, f32[8,128]{1,0:T(8,128)S(1)}, u32[]{:S(2)}, u32[]{:S(2)}) collective-permute-start(f32[8,128]{1,0:T(8,128)S(1)} %get-tuple-element.76), channel_id=1, source_target_pairs={{0,96},{32,0},{64,32},{96,64},{1,97},{33,1},{65,33},{97,65},{2,98}... | collective-permute-start | bytes 12296 | tf_op jit(solution)/shard_map/ppermute | solution.py:691
  53.3 6.4 %collective-permute-start.14 = (f32[8,128]{1,0:T(8,128)S(1)}, f32[8,128]{1,0:T(8,128)S(1)}, u32[]{:S(2)}, u32[]{:S(2)}) collective-permute-start(f32[8,128]{1,0:T(8,128)S(1)} %add_add_fusion.2), channel_id=1, source_target_pairs={{0,2},{1,3},{2,0},{3,1},{4,6},{5,7},{6,4},{7,5},{8,10},{9,11},{10,... | collective-permute-start | bytes 12296 | tf_op jit(solution)/shard_map/ppermute | solution.py:691
  56.2 4.8 %collective-permute-start.15 = (f32[8,128]{1,0:T(8,128)S(1)}, f32[8,128]{1,0:T(8,128)S(1)}, u32[]{:S(2)}, u32[]{:S(2)}) collective-permute-start(f32[8,128]{1,0:T(8,128)S(1)} %add_add_fusion.2), channel_id=1, source_target_pairs={{0,1},{1,2},{2,3},{3,0},{4,5},{5,6},{6,7},{7,4},{8,9},{9,10},{10,1... | collective-permute-start | bytes 12296 | tf_op jit(solution)/shard_map/ppermute | solution.py:691
  56.9 4.1 %collective-permute-start.16 = (f32[8,128]{1,0:T(8,128)S(1)}, f32[8,128]{1,0:T(8,128)S(1)}, u32[]{:S(2)}, u32[]{:S(2)}) collective-permute-start(f32[8,128]{1,0:T(8,128)S(1)} %add_add_fusion.2), channel_id=1, source_target_pairs={{0,3},{1,0},{2,1},{3,2},{4,7},{5,4},{6,5},{7,6},{8,11},{9,8},{10,9... | collective-permute-start | bytes 12296 | tf_op jit(solution)/shard_map/ppermute | solution.py:691
  59.4 7.7 %collective-permute-start.21 = (f32[32,8,128]{2,1,0:T(8,128)S(1)}, f32[32,8,128]{2,1,0:T(8,128)S(1)}, u32[]{:S(2)}, u32[]{:S(2)}) collective-permute-start(f32[32,8,128]{2,1,0:T(8,128)S(1)} %get-tuple-element.74.refs_6_), channel_id=1, source_target_pairs={{0,32},{32,64},{64,96},{96,0},{1,33},{33,65},{65,97},{97,1},{2,34}... | collective-permute-start | bytes 393224 | tf_op jit(solution)/shard_map/ppermute | solution.py:691
  61.0 1.2 %collective-permute-start.17 = (f32[8,128]{1,0:T(8,128)S(1)}, f32[8,128]{1,0:T(8,128)S(1)}, u32[]{:S(2)}, u32[]{:S(2)}) collective-permute-start(f32[8,128]{1,0:T(8,128)S(1)} %add_add_fusion.1), channel_id=1, source_target_pairs={{0,4},{4,0},{8,12},{12,8},{16,20},{20,16},{24,28},{28,24},{1,5},{5... | collective-permute-start | bytes 12296 | tf_op jit(solution)/shard_map/ppermute | solution.py:701
  62.3 5.4 %collective-permute-start.18 = (f32[8,128]{1,0:T(8,128)S(1)}, f32[8,128]{1,0:T(8,128)S(1)}, u32[]{:S(2)}, u32[]{:S(2)}) collective-permute-start(f32[8,128]{1,0:T(8,128)S(1)} %add.36), channel_id=1, source_target_pairs={{0,16},{4,20},{8,24},{12,28},{16,0},{20,4},{24,8},{28,12},{1,17},{... | collective-permute-start | bytes 12296 | tf_op jit(solution)/shard_map/ppermute | solution.py:691
  63.9 4.8 %collective-permute-start.19 = (f32[8,128]{1,0:T(8,128)S(1)}, f32[8,128]{1,0:T(8,128)S(1)}, u32[]{:S(2)}, u32[]{:S(2)}) collective-permute-start(f32[8,128]{1,0:T(8,128)S(1)} %add.36), channel_id=1, source_target_pairs={{0,8},{4,12},{8,16},{12,20},{16,24},{20,28},{24,0},{28,4},{1,9},{5... | collective-permute-start | bytes 12296 | tf_op jit(solution)/shard_map/ppermute | solution.py:691
  64.6 4.2 %collective-permute-start.20 = (f32[8,128]{1,0:T(8,128)S(1)}, f32[8,128]{1,0:T(8,128)S(1)}, u32[]{:S(2)}, u32[]{:S(2)}) collective-permute-start(f32[8,128]{1,0:T(8,128)S(1)} %add.36), channel_id=1, source_target_pairs={{0,24},{4,28},{8,0},{12,4},{16,8},{20,12},{24,16},{28,20},{1,25},{... | collective-permute-start | bytes 12296 | tf_op jit(solution)/shard_map/ppermute | solution.py:691

commit v5 on v4

--- a/solution.py
+++ b/solution.py
@@ -29,7 +29,7 @@
 START_LIMIT = 48
 
 
-def call(body, name, ins, outs, after=(), aliases=None, scratch=(), in_specs=None, out_specs=None, limit=8):
+def call(body, ins, outs, after=(), aliases=None, scratch=(), in_specs=None, out_specs=None, limit=8):
     count = len(ins)
 
     def run(*refs):
@@ -37,7 +37,6 @@
 
     return pl.pallas_call(
         run,
-        name=name,
         out_shape=[jax.ShapeDtypeStruct(s, F32) for s in outs],
         in_specs=(in_specs or [VSPEC] * count) + [HSPEC] * len(after),
         out_specs=out_specs or [VSPEC] * len(outs),
@@ -99,11 +98,8 @@
 
 
 def pack_columns(field, zp, zm):
-    def group(g, carry):
+    for g in range(4):
         pack_group(field, g, zp, zm)
-        return carry
-
-    lax.fori_loop(0, 4, group, 0)
 
 
 def start_kernel(rhs, stencil, rc, vi, zp, zm, st, sem_r, sem_s):
@@ -178,11 +174,11 @@
 
 def roll_fields(vi, vm, vp):
     def step(n, carry):
-        for i in range(4):
-            roll_rows(vi, vm, vp, 4 * n + i)
-        return carry
-
-    lax.fori_loop(0, X // 4, step, 0)
+        for i in range(8):
+            roll_rows(vi, vm, vp, 8 * n + i)
+        return carry
+
+    lax.fori_loop(0, X // 8, step, 0)
 
 
 def roll_kernel(vi, st, vm, vp, wz):
@@ -202,16 +198,17 @@
 def put_ends(rl, rr, vm, vp):
     first, last = lanes() == 0, lanes() == 127
 
-    def group(g, carry):
-        pair = merged(rl, rr, g)
-        for xx in range(4):
-            for y in range(Y):
-                end = ends_of(pair, spot(xx, y))
-                pltpu.store(vm.at[4 * g + xx, y], end, mask=first)
-                pltpu.store(vp.at[4 * g + xx, y], end, mask=last)
-        return carry
-
-    lax.fori_loop(0, 4, group, 0)
+    def groups(n, carry):
+        for g in (2 * n, 2 * n + 1):
+            pair = merged(rl, rr, g)
+            for xx in range(4):
+                for y in range(Y):
+                    end = ends_of(pair, spot(xx, y))
+                    pltpu.store(vm.at[4 * g + xx, y], end, mask=first)
+                    pltpu.store(vp.at[4 * g + xx, y], end, mask=last)
+        return carry
+
+    lax.fori_loop(0, 2, groups, 0)
 
 
 def ends_kernel(vm_in, vp_in, wz_in, st, rl, rr, vm, vp, wz, sums):
@@ -551,8 +548,11 @@
 
 def gram_second_kernel(r0, y1, early, flat, out):
     flat_kernel(y1, flat)
-    tile = place(early[...], gram(r0, flat), 1)
-    out[...] = place(tile, gram(flat, flat), 2)
+    out[...] = place(early[...], gram(r0, flat), 1)
+
+
+def gram_third_kernel(y1, early, out):
+    out[...] = place(early[...], gram(y1, y1), 2)
 
 
 def late_kernel(acc_in, st, ring, qm, qp, tp, xp, y1, early, acc, flat, out, far, sent):
@@ -708,7 +708,7 @@
     dma = pltpu.SemaphoreType.DMA
     st = stencil
     rc, vi, zp, zm = call(
-        start_kernel, "k_start", [rhs, stencil],
+        start_kernel, [rhs, stencil],
         [compact, full, (9, *tile), (9, *tile)],
         in_specs=[FAR] * 2,
         scratch=[pltpu.VMEM((9, X, Y, Z), F32), dma((4,)), dma((9,))],
@@ -716,59 +716,56 @@
     )
     rl = shift(zp, "gz", 1)
     rr = shift(zm, "gz", -1)
-    vm, vp, wz = call(roll_kernel, "k_roll", [vi, st], [full, full, (9, X, Y, Z)])
-    yp, ym = call(edge_kernel, "k_edge", [vi, st, wz, rl, rr], [(36, *tile), (30, *tile)])
+    vm, vp, wz = call(roll_kernel, [vi, st], [full, full, (9, X, Y, Z)])
+    yp, ym = call(edge_kernel, [vi, st, wz, rl, rr], [(36, *tile), (30, *tile)])
     qm = shift(yp, "gy", 1)
     qp = shift(ym, "gy", -1)
     vm, vp, wz, sums = call(
-        ends_kernel, "k_ends", [vm, vp, wz, st, rl, rr],
+        ends_kernel, [vm, vp, wz, st, rl, rr],
         [full, full, (9, X, Y, Z), (5, X, Y, Z)], aliases={0: 0, 1: 1, 2: 2}, after=[yp],
     )
+    (g0,) = call(gram_first_kernel, [rc], [tile], after=[yp])
     ring, xm, xp = call(
-        third_kernel(True), "k_third", [vi, vm, vp, st, wz, rl, rr, qm, qp, sums],
-        [(2, 3, X, *tile), (Y + 8, *tile), (Y + 4, *tile)],
+        third_kernel(True), [vi, vm, vp, st, wz, rl, rr, qm, qp, sums],
+        [(2, 3, X, *tile), (Y + 8, *tile), (Y + 4, *tile)], after=[g0],
     )
     tp = shift(xm, "gx", -1)
     tm = shift(xp, "gx", 1)
-    acc, diag = call(inner_kernel, "k_inner", [vi, vm, vp, st, wz, sums], [full, (X, Y, Z)])
+    acc, diag = call(inner_kernel, [vi, vm, vp, st, wz, sums], [full, (X, Y, Z)])
     y1, diag, zp, zm = call(
-        join_kernel, "k_join", [acc, diag, vi, st, ring, qm, qp, tp, tm],
+        join_kernel, [acc, diag, vi, st, ring, qm, qp, tp, tm],
         [full, (X, Y, Z), (4, *tile), (4, *tile)], aliases={0: 0, 1: 1},
     )
 
     rl = shift(zp, "gz", 1)
     rr = shift(zm, "gz", -1)
-    vm, vp = call(roll_fields, "k_roll2", [y1], [full, full])
-    (g0,) = call(gram_first_kernel, "k_gram0", [rc], [tile], after=[zp])
-    yp, ym = call(
-        edge_again_kernel, "k_edge2", [y1, rl, rr], [(24, *tile), (24, *tile)], after=[vm, g0]
-    )
+    vm, vp = call(roll_fields, [y1], [full, full])
+    y1f, g1 = call(gram_second_kernel, [rc, y1, g0], [compact, tile], after=[zp])
+    yp, ym = call(edge_again_kernel, [y1, rl, rr], [(24, *tile), (24, *tile)], after=[vm, g1])
     qmv = shift(yp, "gy", 1)
     qpv = shift(ym, "gy", -1)
     vm, vp = call(
-        ends_again_kernel, "k_ends2", [vm, vp, rl, rr], [full, full],
+        ends_again_kernel, [vm, vp, rl, rr], [full, full],
         aliases={0: 0, 1: 1}, after=[yp],
     )
-    y1f, g2 = call(gram_second_kernel, "k_gram12", [rc, y1, g0], [compact, tile], after=[yp])
+    (g2,) = call(gram_third_kernel, [y1f, g1], [tile], after=[yp])
     ring, xm, xp = call(
-        third_kernel(False), "k_third2", [y1, vm, vp, st, wz, rl, rr, qmv, qpv, qm, qp],
+        third_kernel(False), [y1, vm, vp, st, wz, rl, rr, qmv, qpv, qm, qp],
         [(2, 3, X, *tile), (Y + 8, *tile), (Y, *tile)], after=[g2],
     )
     tp = shift(xm, "gx", -1)
-    acc, xp = call(
-        inner_again_kernel, "k_inner2", [y1, vm, vp, st, wz, diag, xp], [full, (Y, *tile)]
-    )
+    acc, xp = call(inner_again_kernel, [y1, vm, vp, st, wz, diag, xp], [full, (Y, *tile)])
     tm = shift(xp, "gx", 1)
     _, y2f, moment = call(
-        late_kernel, "k_late", [acc, st, ring, qm, qp, tp, xp, y1f, g2],
+        late_kernel, [acc, st, ring, qm, qp, tp, xp, y1f, g2],
         [full, compact, tile], aliases={0: 0},
         scratch=[pltpu.VMEM((F, 1, Y, Z), F32), pltpu.VMEM((F, 1, Y, Z), F32)],
     )
-    d0, d1 = call(differences_kernel, "k_diff", [rc, y1f, y2f, tm], [compact, compact])
+    d0, d1 = call(differences_kernel, [rc, y1f, y2f, tm], [compact, compact])
     moment = ring_sum(ring_sum(moment, "gx", 1), "gz", 1)
     moment = ring_sum(moment + other_core(moment), "gy", 2)
     sol, res = call(
-        last_kernel, "k_last", [moment, rc, y1f, d0, d1], [compact, compact],
+        last_kernel, [moment, rc, y1f, d0, d1], [compact, compact],
         out_specs=[FAR, FAR],
         scratch=[
             pltpu.VMEM((3, 8, *tile), F32),

time: 74.4 us -> 74 us (level)
    pallas_call x17 -> x18, Pallas kernels: 30.6 us -> 30 us  [call(): pl.pallas_call(run, out_shape=[jax.ShapeDtypeStruct(s, F32) for s in outs...]
  transfers between devices with their start and end apart: 22 -> 22, of which waited for: 9 -> 8; matrix products, arithmetic and copies ran while one was open for 0% -> 0% of each run, Pallas kernels for 25% -> 25%
where the time goes in v5:
time: 74 us; the launch traced here: 73.5 us
  starting transfers between devices  33.7 us (46%)
  Pallas kernels  30 us (41%)
  waiting for transfers between devices  8.97 us (12%)
  between operations  0.84 us (1%)
    ppermute x21, starting transfers between devices, shift(): return lax.ppermute(x, axis, [(i, (i + step) % n) for i in range(n)])  33.6 us
    pallas_call x18, Pallas kernels, call(): pl.pallas_call(run, out_shape=[jax.ShapeDtypeStruct(s, F32) for s in outs...  30 us
    ppermute x21, waiting for transfers between devices, shift(): return lax.ppermute(x, axis, [(i, (i + step) % n) for i in range(n)])  7.82 us
  transfers between devices with their start and end apart: 22, of which 8 were waited for; matrix products, arithmetic and copies ran while one was open for 0% of the time, Pallas kernels for 25%

profile of v5, /device:TPU:0, one launch (start us, length us, event | category | flops | bytes accessed | tf_op | source)
XLA Modules:
  0.0 73.5 jit_solution(18277188187473364826)
XLA Ops:
  0.6 3.0 %shard_map.41 = (f32[8,16,32,128]{3,2,1,0:T(8,128)S(1)}, f32[16,32,8,128]{3,2,1,0:T(8,128)S(1)}, f32[9,8,128]{2,1,0:T(8,128)S(1)}, f32[9,8,128]{2,1,0:T(8,128)S(1)}) custom-call(f32[8,16,32,128]{3,2,1,0:T(8,128)} %refs_0_.1, f32[14,16,32,128]{3,2,1,0:T(8,128)} %refs_1_.7), custom_call_target="tpu_custom_call" | custom-call | tf_op jit(solution)/shard_map/pallas_call | solution.py:38
  3.7 2.1 %collective-permute-start = (f32[9,8,128]{2,1,0:T(8,128)S(1)}, f32[9,8,128]{2,1,0:T(8,128)S(1)}, u32[]{:S(2)}, u32[]{:S(2)}) collective-permute-start(f32[9,8,128]{2,1,0:T(8,128)S(1)} %get-tuple-element.45), channel_id=1, source_target_pairs={{0,1},{1,2},{2,3},{3,0},{4,5},{5,6},{6,7},{7,4},{8,9},{9,10},{10,1... | collective-permute-start | bytes 110600 | tf_op jit(solution)/shard_map/ppermute | solution.py:691
  5.8 2.2 %collective-permute-start.1 = (f32[9,8,128]{2,1,0:T(8,128)S(1)}, f32[9,8,128]{2,1,0:T(8,128)S(1)}, u32[]{:S(2)}, u32[]{:S(2)}) collective-permute-start(f32[9,8,128]{2,1,0:T(8,128)S(1)} %get-tuple-element.46), channel_id=1, source_target_pairs={{0,3},{1,0},{2,1},{3,2},{4,7},{5,4},{6,5},{7,6},{8,11},{9,8},{10,9... | collective-permute-start | bytes 110600 | tf_op jit(solution)/shard_map/ppermute | solution.py:691
  8.0 1.9 %shard_map.42 = (f32[16,32,8,128]{3,2,1,0:T(8,128)S(1)}, f32[16,32,8,128]{3,2,1,0:T(8,128)S(1)}, f32[9,16,32,128]{3,2,1,0:T(8,128)S(1)}) custom-call(f32[16,32,8,128]{3,2,1,0:T(8,128)S(1)} %get-tuple-element.41.refs_0_.refs_2_, f32[14,16,32,128]{3,2,1,0:T(8,128)S(1)} %copy-done), custom_call_target="tpu_custom_call" | custom-call | tf_op jit(solution)/shard_map/pallas_call | solution.py:38
  10.2 2.9 %collective-permute-start.3 = (f32[30,8,128]{2,1,0:T(8,128)S(1)}, f32[30,8,128]{2,1,0:T(8,128)S(1)}, u32[]{:S(2)}, u32[]{:S(2)}) collective-permute-start(f32[30,8,128]{2,1,0:T(8,128)S(1)} %get-tuple-element.54), channel_id=1, source_target_pairs={{0,28},{4,0},{8,4},{12,8},{16,12},{20,16},{24,20},{28,24},{1,29},{... | collective-permute-start | bytes 368648 | tf_op jit(solution)/shard_map/ppermute | solution.py:691
  14.1 1.9 %shard_map.44 = (f32[16,32,8,128]{3,2,1,0:T(8,128)S(1)}, f32[16,32,8,128]{3,2,1,0:T(8,128)S(1)}, f32[9,16,32,128]{3,2,1,0:T(8,128)S(1)}, f32[5,16,32,128]{3,2,1,0:T(8,128)S(1)}) custom-call(f32[16,32,8,128]{3,2,1,0:T(8,128)S(1)} %get-tuple-element.42.refs_0_, ...), custom_call_target="tpu_custom_call", output_to_operand_aliasing={{0}: (0, {}), {1}: (1, {}), {2}: (2, {})} | custom-call | tf_op jit(solution)/shard_map/pallas_call | solution.py:38
  16.2 3.1 %collective-permute-start.4 = (f32[40,8,128]{2,1,0:T(8,128)S(1)}, f32[40,8,128]{2,1,0:T(8,128)S(1)}, u32[]{:S(2)}, u32[]{:S(2)}) collective-permute-start(f32[40,8,128]{2,1,0:T(8,128)S(1)} %get-tuple-element.57), channel_id=1, source_target_pairs={{0,96},{32,0},{64,32},{96,64},{1,97},{33,1},{65,33},{97,65},{2,98}... | collective-permute-start | bytes 491528 | tf_op jit(solution)/shard_map/ppermute | solution.py:691
  19.3 4.7 %shard_map.45 = (f32[16,32,8,128]{3,2,1,0:T(8,128)S(1)}, f32[16,32,128]{2,1,0:T(8,128)S(1)}) custom-call(f32[16,32,8,128]{3,2,1,0:T(8,128)S(1)} %get-tuple-element.41.refs_0_.refs_2_, f32[16,32,8,128]{3,2,1,0:T(8,128)S(1)} %get-tuple-element.48.refs_1_, f32[16,32,8,128]{3,2,1,0:T(8,128)S(1)} %get-tuple-element.49.refs_2_, f32[14,16,32,128]{3,2,1,0:T(8,128)S(1)} %copy-done, ...), custom_call_target="tpu_custom_call" | custom-call | tf_op jit(solution)/shard_map/pallas_call | solution.py:38
  24.1 2.0 %collective-permute-done.5.refs_8_ = f32[36,8,128]{2,1,0:T(8,128)S(1)} collective-permute-done((f32[36,8,128]{2,1,0:T(8,128)S(1)}, f32[36,8,128]{2,1,0:T(8,128)S(1)}, u32[]{:S(2)}, u32[]{:S(2)}) %collective-permute-start.5) | collective-permute-done | bytes 147488 | tf_op jit(solution)/shard_map/ppermute | solution.py:691
  26.9 1.8 %collective-permute-start.6 = (f32[4,8,128]{2,1,0:T(8,128)S(1)}, f32[4,8,128]{2,1,0:T(8,128)S(1)}, u32[]{:S(2)}, u32[]{:S(2)}) collective-permute-start(f32[4,8,128]{2,1,0:T(8,128)S(1)} %get-tuple-element.62.refs_3_), channel_id=1, source_target_pairs={{0,1},{1,2},{2,3},{3,0},{4,5},{5,6},{6,7},{7,4},{8,9},{9,10},{10,1... | collective-permute-start | bytes 49160 | tf_op jit(solution)/shard_map/ppermute | solution.py:691
  28.7 1.6 %collective-permute-start.7 = (f32[4,8,128]{2,1,0:T(8,128)S(1)}, f32[4,8,128]{2,1,0:T(8,128)S(1)}, u32[]{:S(2)}, u32[]{:S(2)}) collective-permute-start(f32[4,8,128]{2,1,0:T(8,128)S(1)} %get-tuple-element.63), channel_id=1, source_target_pairs={{0,3},{1,0},{2,1},{3,2},{4,7},{5,4},{6,5},{7,6},{8,11},{9,8},{10,9... | collective-permute-start | bytes 49160 | tf_op jit(solution)/shard_map/ppermute | solution.py:691
  30.3 1.3 %shard_map.50 = (f32[8,16,32,128]{3,2,1,0:T(8,128)S(1)}, f32[8,128]{1,0:T(8,128)S(1)}) custom-call(f32[8,16,32,128]{3,2,1,0:T(8,128)S(1)} %get-tuple-element.55.refs_0_.refs_1_, f32[16,32,8,128]{3,2,1,0:T(8,128)S(1)} %get-tuple-element.59.refs_0_.refs_1_, f32[8,128]{1,0:T(8,128)S(1)} %shard_map.46.refs_10_.refs_2_, f32[4,8,128]{2,1,0:T(8,128)S(1)} %get-tuple-element.62.refs_3_), custom_call_target="tpu_custom_call" | custom-call | tf_op jit(solution)/shard_map/pallas_call | solution.py:38
  31.6 1.2 %shard_map.49 = (f32[16,32,8,128]{3,2,1,0:T(8,128)S(1)}, f32[16,32,8,128]{3,2,1,0:T(8,128)S(1)}) custom-call(f32[16,32,8,128]{3,2,1,0:T(8,128)S(1)} %get-tuple-element.59.refs_0_.refs_1_), custom_call_target="tpu_custom_call" | custom-call | tf_op jit(solution)/shard_map/pallas_call | solution.py:38
  33.0 2.9 %collective-permute-start.9 = (f32[24,8,128]{2,1,0:T(8,128)S(1)}, f32[24,8,128]{2,1,0:T(8,128)S(1)}, u32[]{:S(2)}, u32[]{:S(2)}) collective-permute-start(f32[24,8,128]{2,1,0:T(8,128)S(1)} %get-tuple-element.69), channel_id=1, source_target_pairs={{0,28},{4,0},{8,4},{12,8},{16,12},{20,16},{24,20},{28,24},{1,29},{... | collective-permute-start | bytes 294920 | tf_op jit(solution)/shard_map/ppermute | solution.py:691
  38.4 1.3 %collective-permute-start.10 = (f32[40,8,128]{2,1,0:T(8,128)S(1)}, f32[40,8,128]{2,1,0:T(8,128)S(1)}, u32[]{:S(2)}, u32[]{:S(2)}) collective-permute-start(f32[40,8,128]{2,1,0:T(8,128)S(1)} %get-tuple-element.74), channel_id=1, source_target_pairs={{0,96},{32,0},{64,32},{96,64},{1,97},{33,1},{65,33},{97,65},{2,98}... | collective-permute-start | bytes 491528 | tf_op jit(solution)/shard_map/ppermute | solution.py:691
  39.7 4.2 %shard_map.55 = (f32[16,32,8,128]{3,2,1,0:T(8,128)S(1)}, f32[32,8,128]{2,1,0:T(8,128)S(1)}) custom-call(f32[16,32,8,128]{3,2,1,0:T(8,128)S(1)} %get-tuple-element.59.refs_0_.refs_1_, f32[16,32,8,128]{3,2,1,0:T(8,128)S(1)} %get-tuple-element.66.refs_1_, f32[16,32,8,128]{3,2,1,0:T(8,128)S(1)} %get-tuple-element.67.refs_2_, f32[14,16,32,128]{3,2,1,0:T(8,128)S(1)} %copy-done, ...), custom_call_target="tpu_custom_call" | custom-call | tf_op jit(solution)/shard_map/pallas_call | solution.py:38
  44.8 1.6 %shard_map.56 = (f32[16,32,8,128]{3,2,1,0:T(8,128)S(1)}, f32[8,16,32,128]{3,2,1,0:T(8,128)S(1)}, f32[8,128]{1,0:T(8,128)S(1)}) custom-call(f32[16,32,8,128]{3,2,1,0:T(8,128)S(1)} %get-tuple-element.72.refs_0_, f32[14,16,32,128]{3,2,1,0:T(8,128)S(1)} %copy-done, f32[2,3,16,8,128]{4,3,2,1,0:T(8,128)S(1)} %get-tuple-element.73.refs_2_, ...), custom_call_target="tpu_custom_call", output_to_operand_aliasing={{0}: (0, {})} | custom-call | tf_op jit(solution)/shard_map/pallas_call | solution.py:38
  46.7 2.3 %collective-permute-start.12 = (f32[8,128]{1,0:T(8,128)S(1)}, f32[8,128]{1,0:T(8,128)S(1)}, u32[]{:S(2)}, u32[]{:S(2)}) collective-permute-start(f32[8,128]{1,0:T(8,128)S(1)} %get-tuple-element.76), channel_id=1, source_target_pairs={{0,32},{32,64},{64,96},{96,0},{1,33},{33,65},{65,97},{97,1},{2,34}... | collective-permute-start | bytes 12296 | tf_op jit(solution)/shard_map/ppermute | solution.py:691
  49.9 1.7 %collective-permute-done.11 = f32[8,128]{1,0:T(8,128)S(1)} collective-permute-done((f32[8,128]{1,0:T(8,128)S(1)}, f32[8,128]{1,0:T(8,128)S(1)}, u32[]{:S(2)}, u32[]{:S(2)}) %collective-permute-start.11) | collective-permute-done | bytes 4128 | tf_op jit(solution)/shard_map/ppermute | solution.py:691
  52.6 2.6 %collective-permute-start.14 = (f32[8,128]{1,0:T(8,128)S(1)}, f32[8,128]{1,0:T(8,128)S(1)}, u32[]{:S(2)}, u32[]{:S(2)}) collective-permute-start(f32[8,128]{1,0:T(8,128)S(1)} %add_add_fusion.2), channel_id=1, source_target_pairs={{0,2},{1,3},{2,0},{3,1},{4,6},{5,7},{6,4},{7,5},{8,10},{9,11},{10,... | collective-permute-start | bytes 12296 | tf_op jit(solution)/shard_map/ppermute | solution.py:691
  55.9 2.6 %collective-permute-start.16 = (f32[8,128]{1,0:T(8,128)S(1)}, f32[8,128]{1,0:T(8,128)S(1)}, u32[]{:S(2)}, u32[]{:S(2)}) collective-permute-start(f32[8,128]{1,0:T(8,128)S(1)} %add_add_fusion.2), channel_id=1, source_target_pairs={{0,3},{1,0},{2,1},{3,2},{4,7},{5,4},{6,5},{7,6},{8,11},{9,8},{10,9... | collective-permute-start | bytes 12296 | tf_op jit(solution)/shard_map/ppermute | solution.py:691
  61.3 2.2 %collective-permute-start.18 = (f32[8,128]{1,0:T(8,128)S(1)}, f32[8,128]{1,0:T(8,128)S(1)}, u32[]{:S(2)}, u32[]{:S(2)}) collective-permute-start(f32[8,128]{1,0:T(8,128)S(1)} %add.36), channel_id=1, source_target_pairs={{0,16},{4,20},{8,24},{12,28},{16,0},{20,4},{24,8},{28,12},{1,17},{... | collective-permute-start | bytes 12296 | tf_op jit(solution)/shard_map/ppermute | solution.py:691
  63.5 3.2 %collective-permute-start.20 = (f32[8,128]{1,0:T(8,128)S(1)}, f32[8,128]{1,0:T(8,128)S(1)}, u32[]{:S(2)}, u32[]{:S(2)}) collective-permute-start(f32[8,128]{1,0:T(8,128)S(1)} %add.36), channel_id=1, source_target_pairs={{0,24},{4,28},{8,0},{12,4},{16,8},{20,12},{24,16},{28,20},{1,25},{... | collective-permute-start | bytes 12296 | tf_op jit(solution)/shard_map/ppermute | solution.py:691
  68.3 5.2 %shard_map.58 = (f32[8,16,32,128]{3,2,1,0:T(8,128)}, f32[8,16,32,128]{3,2,1,0:T(8,128)}) custom-call(f32[8,128]{1,0:T(8,128)S(1)} %add_add_fusion.refs_0_, f32[8,16,32,128]{3,2,1,0:T(8,128)S(1)} %get-tuple-element.55.refs_0_.refs_1_, f32[8,16,32,128]{3,2,1,0:T(8,128)S(1)} %get-tuple-element.70.refs_0_.refs_7_.refs_1_.refs_2_, ...), custom_call_target="tpu_custom_call" | custom-call | tf_op jit(solution)/shard_map/pallas_call | solution.py:38
  (44 shorter events, 12.9 us)
Async XLA Ops:
  0.6 7.4 %copy-start = (f32[14,16,32,128]{3,2,1,0:T(8,128)S(1)}, f32[14,16,32,128]{3,2,1,0:T(8,128)}, u32[]{:S(2)}) copy-start(f32[14,16,32,128]{3,2,1,0:T(8,128)} %refs_1_.7) | copy-start | bytes 11010052
  3.7 6.3 %collective-permute-start = (f32[9,8,128]{2,1,0:T(8,128)S(1)}, f32[9,8,128]{2,1,0:T(8,128)S(1)}, u32[]{:S(2)}, u32[]{:S(2)}) collective-permute-start(f32[9,8,128]{2,1,0:T(8,128)S(1)} %get-tuple-element.45), channel_id=1, source_target_pairs={{0,1},{1,2},{2,3},{3,0},{4,5},{5,6},{6,7},{7,4},{8,9},{9,10},{10,1... | collective-permute-start | bytes 110600 | tf_op jit(solution)/shard_map/ppermute | solution.py:691
  5.8 4.2 %collective-permute-start.1 = (f32[9,8,128]{2,1,0:T(8,128)S(1)}, f32[9,8,128]{2,1,0:T(8,128)S(1)}, u32[]{:S(2)}, u32[]{:S(2)}) collective-permute-start(f32[9,8,128]{2,1,0:T(8,128)S(1)} %get-tuple-element.46), channel_id=1, source_target_pairs={{0,3},{1,0},{2,1},{3,2},{4,7},{5,4},{6,5},{7,6},{8,11},{9,8},{10,9... | collective-permute-start | bytes 110600 | tf_op jit(solution)/shard_map/ppermute | solution.py:691
  10.2 5.8 %collective-permute-start.2 = (f32[36,8,128]{2,1,0:T(8,128)S(1)}, f32[36,8,128]{2,1,0:T(8,128)S(1)}, u32[]{:S(2)}, u32[]{:S(2)}) collective-permute-start(f32[36,8,128]{2,1,0:T(8,128)S(1)} %get-tuple-element.47.refs_6_.refs_1_), channel_id=1, source_target_pairs={{0,4},{4,8},{8,12},{12,16},{16,20},{20,24},{24,28},{28,0},{1,5},{5... | collective-permute-start | bytes 442376 | tf_op jit(solution)/shard_map/ppermute | solution.py:691
  10.2 5.8 %collective-permute-start.3 = (f32[30,8,128]{2,1,0:T(8,128)S(1)}, f32[30,8,128]{2,1,0:T(8,128)S(1)}, u32[]{:S(2)}, u32[]{:S(2)}) collective-permute-start(f32[30,8,128]{2,1,0:T(8,128)S(1)} %get-tuple-element.54), channel_id=1, source_target_pairs={{0,28},{4,0},{8,4},{12,8},{16,12},{20,16},{24,20},{28,24},{1,29},{... | collective-permute-start | bytes 368648 | tf_op jit(solution)/shard_map/ppermute | solution.py:691
  16.2 9.9 %collective-permute-start.4 = (f32[40,8,128]{2,1,0:T(8,128)S(1)}, f32[40,8,128]{2,1,0:T(8,128)S(1)}, u32[]{:S(2)}, u32[]{:S(2)}) collective-permute-start(f32[40,8,128]{2,1,0:T(8,128)S(1)} %get-tuple-element.57), channel_id=1, source_target_pairs={{0,96},{32,0},{64,32},{96,64},{1,97},{33,1},{65,33},{97,65},{2,98}... | collective-permute-start | bytes 491528 | tf_op jit(solution)/shard_map/ppermute | solution.py:691
  19.3 6.8 %collective-permute-start.5 = (f32[36,8,128]{2,1,0:T(8,128)S(1)}, f32[36,8,128]{2,1,0:T(8,128)S(1)}, u32[]{:S(2)}, u32[]{:S(2)}) collective-permute-start(f32[36,8,128]{2,1,0:T(8,128)S(1)} %get-tuple-element.58), channel_id=1, source_target_pairs={{0,32},{32,64},{64,96},{96,0},{1,33},{33,65},{65,97},{97,1},{2,34}... | collective-permute-start | bytes 442376 | tf_op jit(solution)/shard_map/ppermute | solution.py:691
  26.9 5.9 %collective-permute-start.6 = (f32[4,8,128]{2,1,0:T(8,128)S(1)}, f32[4,8,128]{2,1,0:T(8,128)S(1)}, u32[]{:S(2)}, u32[]{:S(2)}) collective-permute-start(f32[4,8,128]{2,1,0:T(8,128)S(1)} %get-tuple-element.62.refs_3_), channel_id=1, source_target_pairs={{0,1},{1,2},{2,3},{3,0},{4,5},{5,6},{6,7},{7,4},{8,9},{9,10},{10,1... | collective-permute-start | bytes 49160 | tf_op jit(solution)/shard_map/ppermute | solution.py:691
  28.7 4.1 %collective-permute-start.7 = (f32[4,8,128]{2,1,0:T(8,128)S(1)}, f32[4,8,128]{2,1,0:T(8,128)S(1)}, u32[]{:S(2)}, u32[]{:S(2)}) collective-permute-start(f32[4,8,128]{2,1,0:T(8,128)S(1)} %get-tuple-element.63), channel_id=1, source_target_pairs={{0,3},{1,0},{2,1},{3,2},{4,7},{5,4},{6,5},{7,6},{8,11},{9,8},{10,9... | collective-permute-start | bytes 49160 | tf_op jit(solution)/shard_map/ppermute | solution.py:691
  32.9 5.3 %collective-permute-start.8 = (f32[24,8,128]{2,1,0:T(8,128)S(1)}, f32[24,8,128]{2,1,0:T(8,128)S(1)}, u32[]{:S(2)}, u32[]{:S(2)}) collective-permute-start(f32[24,8,128]{2,1,0:T(8,128)S(1)} %get-tuple-element.65.refs_4_.refs_2_), channel_id=1, source_target_pairs={{0,4},{4,8},{8,12},{12,16},{16,20},{20,24},{24,28},{28,0},{1,5},{5... | collective-permute-start | bytes 294920 | tf_op jit(solution)/shard_map/ppermute | solution.py:691
  33.0 5.2 %collective-permute-start.9 = (f32[24,8,128]{2,1,0:T(8,128)S(1)}, f32[24,8,128]{2,1,0:T(8,128)S(1)}, u32[]{:S(2)}, u32[]{:S(2)}) collective-permute-start(f32[24,8,128]{2,1,0:T(8,128)S(1)} %get-tuple-element.69), channel_id=1, source_target_pairs={{0,28},{4,0},{8,4},{12,8},{16,12},{20,16},{24,20},{28,24},{1,29},{... | collective-permute-start | bytes 294920 | tf_op jit(solution)/shard_map/ppermute | solution.py:691
  38.4 6.4 %collective-permute-start.10 = (f32[40,8,128]{2,1,0:T(8,128)S(1)}, f32[40,8,128]{2,1,0:T(8,128)S(1)}, u32[]{:S(2)}, u32[]{:S(2)}) collective-permute-start(f32[40,8,128]{2,1,0:T(8,128)S(1)} %get-tuple-element.74), channel_id=1, source_target_pairs={{0,96},{32,0},{64,32},{96,64},{1,97},{33,1},{65,33},{97,65},{2,98}... | collective-permute-start | bytes 491528 | tf_op jit(solution)/shard_map/ppermute | solution.py:691
  46.4 5.2 %collective-permute-start.11 = (f32[8,128]{1,0:T(8,128)S(1)}, f32[8,128]{1,0:T(8,128)S(1)}, u32[]{:S(2)}, u32[]{:S(2)}) collective-permute-start(f32[8,128]{1,0:T(8,128)S(1)} %get-tuple-element.76), channel_id=1, source_target_pairs={{0,64},{32,96},{64,0},{96,32},{1,65},{33,97},{65,1},{97,33},{2,66}... | collective-permute-start | bytes 12296 | tf_op jit(solution)/shard_map/ppermute | solution.py:691
  46.7 5.0 %collective-permute-start.12 = (f32[8,128]{1,0:T(8,128)S(1)}, f32[8,128]{1,0:T(8,128)S(1)}, u32[]{:S(2)}, u32[]{:S(2)}) collective-permute-start(f32[8,128]{1,0:T(8,128)S(1)} %get-tuple-element.76), channel_id=1, source_target_pairs={{0,32},{32,64},{64,96},{96,0},{1,33},{33,65},{65,97},{97,1},{2,34}... | collective-permute-start | bytes 12296 | tf_op jit(solution)/shard_map/ppermute | solution.py:691
  49.0 3.6 %collective-permute-start.13 = (f32[8,128]{1,0:T(8,128)S(1)}, f32[8,128]{1,0:T(8,128)S(1)}, u32[]{:S(2)}, u32[]{:S(2)}) collective-permute-start(f32[8,128]{1,0:T(8,128)S(1)} %get-tuple-element.76), channel_id=1, source_target_pairs={{0,96},{32,0},{64,32},{96,64},{1,97},{33,1},{65,33},{97,65},{2,98}... | collective-permute-start | bytes 12296 | tf_op jit(solution)/shard_map/ppermute | solution.py:691
  52.6 6.8 %collective-permute-start.14 = (f32[8,128]{1,0:T(8,128)S(1)}, f32[8,128]{1,0:T(8,128)S(1)}, u32[]{:S(2)}, u32[]{:S(2)}) collective-permute-start(f32[8,128]{1,0:T(8,128)S(1)} %add_add_fusion.2), channel_id=1, source_target_pairs={{0,2},{1,3},{2,0},{3,1},{4,6},{5,7},{6,4},{7,5},{8,10},{9,11},{10,... | collective-permute-start | bytes 12296 | tf_op jit(solution)/shard_map/ppermute | solution.py:691
  55.2 4.8 %collective-permute-start.15 = (f32[8,128]{1,0:T(8,128)S(1)}, f32[8,128]{1,0:T(8,128)S(1)}, u32[]{:S(2)}, u32[]{:S(2)}) collective-permute-start(f32[8,128]{1,0:T(8,128)S(1)} %add_add_fusion.2), channel_id=1, source_target_pairs={{0,1},{1,2},{2,3},{3,0},{4,5},{5,6},{6,7},{7,4},{8,9},{9,10},{10,1... | collective-permute-start | bytes 12296 | tf_op jit(solution)/shard_map/ppermute | solution.py:691
  55.9 4.1 %collective-permute-start.16 = (f32[8,128]{1,0:T(8,128)S(1)}, f32[8,128]{1,0:T(8,128)S(1)}, u32[]{:S(2)}, u32[]{:S(2)}) collective-permute-start(f32[8,128]{1,0:T(8,128)S(1)} %add_add_fusion.2), channel_id=1, source_target_pairs={{0,3},{1,0},{2,1},{3,2},{4,7},{5,4},{6,5},{7,6},{8,11},{9,8},{10,9... | collective-permute-start | bytes 12296 | tf_op jit(solution)/shard_map/ppermute | solution.py:691
  58.4 8.3 %collective-permute-start.21 = (f32[32,8,128]{2,1,0:T(8,128)S(1)}, f32[32,8,128]{2,1,0:T(8,128)S(1)}, u32[]{:S(2)}, u32[]{:S(2)}) collective-permute-start(f32[32,8,128]{2,1,0:T(8,128)S(1)} %get-tuple-element.75.refs_6_), channel_id=1, source_target_pairs={{0,32},{32,64},{64,96},{96,0},{1,33},{33,65},{65,97},{97,1},{2,34}... | collective-permute-start | bytes 393224 | tf_op jit(solution)/shard_map/ppermute | solution.py:691
  60.0 1.2 %collective-permute-start.17 = (f32[8,128]{1,0:T(8,128)S(1)}, f32[8,128]{1,0:T(8,128)S(1)}, u32[]{:S(2)}, u32[]{:S(2)}) collective-permute-start(f32[8,128]{1,0:T(8,128)S(1)} %add_add_fusion.1), channel_id=1, source_target_pairs={{0,4},{4,0},{8,12},{12,8},{16,20},{20,16},{24,28},{28,24},{1,5},{5... | collective-permute-start | bytes 12296 | tf_op jit(solution)/shard_map/ppermute | solution.py:701
  61.3 5.9 %collective-permute-start.18 = (f32[8,128]{1,0:T(8,128)S(1)}, f32[8,128]{1,0:T(8,128)S(1)}, u32[]{:S(2)}, u32[]{:S(2)}) collective-permute-start(f32[8,128]{1,0:T(8,128)S(1)} %add.36), channel_id=1, source_target_pairs={{0,16},{4,20},{8,24},{12,28},{16,0},{20,4},{24,8},{28,12},{1,17},{... | collective-permute-start | bytes 12296 | tf_op jit(solution)/shard_map/ppermute | solution.py:691
  63.5 4.8 %collective-permute-start.19 = (f32[8,128]{1,0:T(8,128)S(1)}, f32[8,128]{1,0:T(8,128)S(1)}, u32[]{:S(2)}, u32[]{:S(2)}) collective-permute-start(f32[8,128]{1,0:T(8,128)S(1)} %add.36), channel_id=1, source_target_pairs={{0,8},{4,12},{8,16},{12,20},{16,24},{20,28},{24,0},{28,4},{1,9},{5... | collective-permute-start | bytes 12296 | tf_op jit(solution)/shard_map/ppermute | solution.py:691
  63.5 4.8 %collective-permute-start.20 = (f32[8,128]{1,0:T(8,128)S(1)}, f32[8,128]{1,0:T(8,128)S(1)}, u32[]{:S(2)}, u32[]{:S(2)}) collective-permute-start(f32[8,128]{1,0:T(8,128)S(1)} %add.36), channel_id=1, source_target_pairs={{0,24},{4,28},{8,0},{12,4},{16,8},{20,12},{24,16},{28,20},{1,25},{... | collective-permute-start | bytes 12296 | tf_op jit(solution)/shard_map/ppermute | solution.py:691

commit v6 on v5

--- a/solution.py
+++ b/solution.py
@@ -505,20 +505,23 @@
 
 
 def flat_kernel(v, out):
-    def turn(x, carry):
-        turn_flat(v, out, x)
-        return carry
-
-    lax.fori_loop(0, X, turn, 0)
+    def turn(n, carry):
+        for i in range(4):
+            turn_flat(v, out, 4 * n + i)
+        return carry
+
+    lax.fori_loop(0, X // 4, turn, 0)
 
 
 PRODUCTS = [(i, j) for i in range(8) for j in range(i, 8)]
 
 
 def gram(u, v, planes=X, begin=None):
-    def step(x, carry):
-        for yb in range(4):
-            at = pl.ds(8 * yb, 8)
+    batch = 2 if planes % 2 == 0 else 1
+
+    def step(n, carry):
+        for t in range(4 * batch):
+            x, at = batch * n + t // 4, pl.ds(8 * (t % 4), 8)
             a = [u[i, x, at, :] for i in range(8)]
             b = a if v is u else [v[i, x, at, :] for i in range(8)]
             carry = tuple(c + a[i] * b[j] for c, (i, j) in zip(carry, PRODUCTS))
@@ -526,7 +529,7 @@
 
     if begin is None:
         begin = tuple(jnp.zeros((8, 128), F32) for _ in PRODUCTS)
-    return lax.fori_loop(0, planes, step, begin)
+    return lax.fori_loop(0, planes // batch, step, begin)
 
 
 def place(tile, sums, m):

time: 74 us -> 73.8 us (level)
  transfers between devices with their start and end apart: 22 -> 22, of which waited for: 8 -> 9; matrix products, arithmetic and copies ran while one was open for 0% -> 0% of each run, Pallas kernels for 25% -> 25%
where the time goes in v6:
time: 73.8 us; the launch traced here: 73.3 us
  starting transfers between devices  33.8 us (46%)
  Pallas kernels  29.5 us (40%)
  waiting for transfers between devices  9.14 us (12%)
  between operations  0.83 us (1%)
    ppermute x21, starting transfers between devices, shift(): return lax.ppermute(x, axis, [(i, (i + step) % n) for i in range(n)])  33.7 us
    pallas_call x18, Pallas kernels, call(): pl.pallas_call(run, out_shape=[jax.ShapeDtypeStruct(s, F32) for s in outs...  29.5 us
    ppermute x21, waiting for transfers between devices, shift(): return lax.ppermute(x, axis, [(i, (i + step) % n) for i in range(n)])  7.99 us
  transfers between devices with their start and end apart: 22, of which 9 were waited for; matrix products, arithmetic and copies ran while one was open for 0% of the time, Pallas kernels for 25%

profile of v6, /device:TPU:0, one launch (start us, length us, event | category | flops | bytes accessed | tf_op | source)
XLA Modules:
  0.0 73.3 jit_solution(18241576239654605183)
XLA Ops:
  0.6 3.0 %shard_map.41 = (f32[8,16,32,128]{3,2,1,0:T(8,128)S(1)}, f32[16,32,8,128]{3,2,1,0:T(8,128)S(1)}, f32[9,8,128]{2,1,0:T(8,128)S(1)}, f32[9,8,128]{2,1,0:T(8,128)S(1)}) custom-call(f32[8,16,32,128]{3,2,1,0:T(8,128)} %refs_0_.1, f32[14,16,32,128]{3,2,1,0:T(8,128)} %refs_1_.7), custom_call_target="tpu_custom_call" | custom-call | tf_op jit(solution)/shard_map/pallas_call | solution.py:38
  3.7 2.1 %collective-permute-start = (f32[9,8,128]{2,1,0:T(8,128)S(1)}, f32[9,8,128]{2,1,0:T(8,128)S(1)}, u32[]{:S(2)}, u32[]{:S(2)}) collective-permute-start(f32[9,8,128]{2,1,0:T(8,128)S(1)} %get-tuple-element.45), channel_id=1, source_target_pairs={{0,1},{1,2},{2,3},{3,0},{4,5},{5,6},{6,7},{7,4},{8,9},{9,10},{10,1... | collective-permute-start | bytes 110600 | tf_op jit(solution)/shard_map/ppermute | solution.py:694
  5.8 2.2 %collective-permute-start.1 = (f32[9,8,128]{2,1,0:T(8,128)S(1)}, f32[9,8,128]{2,1,0:T(8,128)S(1)}, u32[]{:S(2)}, u32[]{:S(2)}) collective-permute-start(f32[9,8,128]{2,1,0:T(8,128)S(1)} %get-tuple-element.46), channel_id=1, source_target_pairs={{0,3},{1,0},{2,1},{3,2},{4,7},{5,4},{6,5},{7,6},{8,11},{9,8},{10,9... | collective-permute-start | bytes 110600 | tf_op jit(solution)/shard_map/ppermute | solution.py:694
  8.0 1.9 %shard_map.42 = (f32[16,32,8,128]{3,2,1,0:T(8,128)S(1)}, f32[16,32,8,128]{3,2,1,0:T(8,128)S(1)}, f32[9,16,32,128]{3,2,1,0:T(8,128)S(1)}) custom-call(f32[16,32,8,128]{3,2,1,0:T(8,128)S(1)} %get-tuple-element.41.refs_0_.refs_2_, f32[14,16,32,128]{3,2,1,0:T(8,128)S(1)} %copy-done), custom_call_target="tpu_custom_call" | custom-call | tf_op jit(solution)/shard_map/pallas_call | solution.py:38
  10.2 2.9 %collective-permute-start.3 = (f32[30,8,128]{2,1,0:T(8,128)S(1)}, f32[30,8,128]{2,1,0:T(8,128)S(1)}, u32[]{:S(2)}, u32[]{:S(2)}) collective-permute-start(f32[30,8,128]{2,1,0:T(8,128)S(1)} %get-tuple-element.54), channel_id=1, source_target_pairs={{0,28},{4,0},{8,4},{12,8},{16,12},{20,16},{24,20},{28,24},{1,29},{... | collective-permute-start | bytes 368648 | tf_op jit(solution)/shard_map/ppermute | solution.py:694
  14.0 1.9 %shard_map.44 = (f32[16,32,8,128]{3,2,1,0:T(8,128)S(1)}, f32[16,32,8,128]{3,2,1,0:T(8,128)S(1)}, f32[9,16,32,128]{3,2,1,0:T(8,128)S(1)}, f32[5,16,32,128]{3,2,1,0:T(8,128)S(1)}) custom-call(f32[16,32,8,128]{3,2,1,0:T(8,128)S(1)} %get-tuple-element.42.refs_0_, ...), custom_call_target="tpu_custom_call", output_to_operand_aliasing={{0}: (0, {}), {1}: (1, {}), {2}: (2, {})} | custom-call | tf_op jit(solution)/shard_map/pallas_call | solution.py:38
  16.2 3.1 %collective-permute-start.4 = (f32[40,8,128]{2,1,0:T(8,128)S(1)}, f32[40,8,128]{2,1,0:T(8,128)S(1)}, u32[]{:S(2)}, u32[]{:S(2)}) collective-permute-start(f32[40,8,128]{2,1,0:T(8,128)S(1)} %get-tuple-element.57), channel_id=1, source_target_pairs={{0,96},{32,0},{64,32},{96,64},{1,97},{33,1},{65,33},{97,65},{2,98}... | collective-permute-start | bytes 491528 | tf_op jit(solution)/shard_map/ppermute | solution.py:694
  19.3 4.7 %shard_map.45 = (f32[16,32,8,128]{3,2,1,0:T(8,128)S(1)}, f32[16,32,128]{2,1,0:T(8,128)S(1)}) custom-call(f32[16,32,8,128]{3,2,1,0:T(8,128)S(1)} %get-tuple-element.41.refs_0_.refs_2_, f32[16,32,8,128]{3,2,1,0:T(8,128)S(1)} %get-tuple-element.48.refs_1_, f32[16,32,8,128]{3,2,1,0:T(8,128)S(1)} %get-tuple-element.49.refs_2_, f32[14,16,32,128]{3,2,1,0:T(8,128)S(1)} %copy-done, ...), custom_call_target="tpu_custom_call" | custom-call | tf_op jit(solution)/shard_map/pallas_call | solution.py:38
  24.1 2.1 %collective-permute-done.5.refs_8_ = f32[36,8,128]{2,1,0:T(8,128)S(1)} collective-permute-done((f32[36,8,128]{2,1,0:T(8,128)S(1)}, f32[36,8,128]{2,1,0:T(8,128)S(1)}, u32[]{:S(2)}, u32[]{:S(2)}) %collective-permute-start.5) | collective-permute-done | bytes 147488 | tf_op jit(solution)/shard_map/ppermute | solution.py:694
  26.9 1.8 %collective-permute-start.6 = (f32[4,8,128]{2,1,0:T(8,128)S(1)}, f32[4,8,128]{2,1,0:T(8,128)S(1)}, u32[]{:S(2)}, u32[]{:S(2)}) collective-permute-start(f32[4,8,128]{2,1,0:T(8,128)S(1)} %get-tuple-element.62.refs_3_), channel_id=1, source_target_pairs={{0,1},{1,2},{2,3},{3,0},{4,5},{5,6},{6,7},{7,4},{8,9},{9,10},{10,1... | collective-permute-start | bytes 49160 | tf_op jit(solution)/shard_map/ppermute | solution.py:694
  28.7 1.6 %collective-permute-start.7 = (f32[4,8,128]{2,1,0:T(8,128)S(1)}, f32[4,8,128]{2,1,0:T(8,128)S(1)}, u32[]{:S(2)}, u32[]{:S(2)}) collective-permute-start(f32[4,8,128]{2,1,0:T(8,128)S(1)} %get-tuple-element.63), channel_id=1, source_target_pairs={{0,3},{1,0},{2,1},{3,2},{4,7},{5,4},{6,5},{7,6},{8,11},{9,8},{10,9... | collective-permute-start | bytes 49160 | tf_op jit(solution)/shard_map/ppermute | solution.py:694
  31.4 1.2 %shard_map.49 = (f32[16,32,8,128]{3,2,1,0:T(8,128)S(1)}, f32[16,32,8,128]{3,2,1,0:T(8,128)S(1)}) custom-call(f32[16,32,8,128]{3,2,1,0:T(8,128)S(1)} %get-tuple-element.59.refs_0_.refs_1_), custom_call_target="tpu_custom_call" | custom-call | tf_op jit(solution)/shard_map/pallas_call | solution.py:38
  32.8 2.9 %collective-permute-start.9 = (f32[24,8,128]{2,1,0:T(8,128)S(1)}, f32[24,8,128]{2,1,0:T(8,128)S(1)}, u32[]{:S(2)}, u32[]{:S(2)}) collective-permute-start(f32[24,8,128]{2,1,0:T(8,128)S(1)} %get-tuple-element.69), channel_id=1, source_target_pairs={{0,28},{4,0},{8,4},{12,8},{16,12},{20,16},{24,20},{28,24},{1,29},{... | collective-permute-start | bytes 294920 | tf_op jit(solution)/shard_map/ppermute | solution.py:694
  38.2 1.2 %collective-permute-start.10 = (f32[40,8,128]{2,1,0:T(8,128)S(1)}, f32[40,8,128]{2,1,0:T(8,128)S(1)}, u32[]{:S(2)}, u32[]{:S(2)}) collective-permute-start(f32[40,8,128]{2,1,0:T(8,128)S(1)} %get-tuple-element.74), channel_id=1, source_target_pairs={{0,96},{32,0},{64,32},{96,64},{1,97},{33,1},{65,33},{97,65},{2,98}... | collective-permute-start | bytes 491528 | tf_op jit(solution)/shard_map/ppermute | solution.py:694
  39.5 4.2 %shard_map.55 = (f32[16,32,8,128]{3,2,1,0:T(8,128)S(1)}, f32[32,8,128]{2,1,0:T(8,128)S(1)}) custom-call(f32[16,32,8,128]{3,2,1,0:T(8,128)S(1)} %get-tuple-element.59.refs_0_.refs_1_, f32[16,32,8,128]{3,2,1,0:T(8,128)S(1)} %get-tuple-element.66.refs_1_, f32[16,32,8,128]{3,2,1,0:T(8,128)S(1)} %get-tuple-element.67.refs_2_, f32[14,16,32,128]{3,2,1,0:T(8,128)S(1)} %copy-done, ...), custom_call_target="tpu_custom_call" | custom-call | tf_op jit(solution)/shard_map/pallas_call | solution.py:38
  44.6 1.5 %shard_map.56 = (f32[16,32,8,128]{3,2,1,0:T(8,128)S(1)}, f32[8,16,32,128]{3,2,1,0:T(8,128)S(1)}, f32[8,128]{1,0:T(8,128)S(1)}) custom-call(f32[16,32,8,128]{3,2,1,0:T(8,128)S(1)} %get-tuple-element.72.refs_0_, f32[14,16,32,128]{3,2,1,0:T(8,128)S(1)} %copy-done, f32[2,3,16,8,128]{4,3,2,1,0:T(8,128)S(1)} %get-tuple-element.73.refs_2_, ...), custom_call_target="tpu_custom_call", output_to_operand_aliasing={{0}: (0, {})} | custom-call | tf_op jit(solution)/shard_map/pallas_call | solution.py:38
  46.3 2.3 %collective-permute-start.12 = (f32[8,128]{1,0:T(8,128)S(1)}, f32[8,128]{1,0:T(8,128)S(1)}, u32[]{:S(2)}, u32[]{:S(2)}) collective-permute-start(f32[8,128]{1,0:T(8,128)S(1)} %get-tuple-element.76), channel_id=1, source_target_pairs={{0,32},{32,64},{64,96},{96,0},{1,33},{33,65},{65,97},{97,1},{2,34}... | collective-permute-start | bytes 12296 | tf_op jit(solution)/shard_map/ppermute | solution.py:694
  49.5 1.7 %collective-permute-done.11 = f32[8,128]{1,0:T(8,128)S(1)} collective-permute-done((f32[8,128]{1,0:T(8,128)S(1)}, f32[8,128]{1,0:T(8,128)S(1)}, u32[]{:S(2)}, u32[]{:S(2)}) %collective-permute-start.11) | collective-permute-done | bytes 4128 | tf_op jit(solution)/shard_map/ppermute | solution.py:694
  52.3 2.7 %collective-permute-start.14 = (f32[8,128]{1,0:T(8,128)S(1)}, f32[8,128]{1,0:T(8,128)S(1)}, u32[]{:S(2)}, u32[]{:S(2)}) collective-permute-start(f32[8,128]{1,0:T(8,128)S(1)} %add_add_fusion.2), channel_id=1, source_target_pairs={{0,2},{1,3},{2,0},{3,1},{4,6},{5,7},{6,4},{7,5},{8,10},{9,11},{10,... | collective-permute-start | bytes 12296 | tf_op jit(solution)/shard_map/ppermute | solution.py:694
  55.7 2.6 %collective-permute-start.16 = (f32[8,128]{1,0:T(8,128)S(1)}, f32[8,128]{1,0:T(8,128)S(1)}, u32[]{:S(2)}, u32[]{:S(2)}) collective-permute-start(f32[8,128]{1,0:T(8,128)S(1)} %add_add_fusion.2), channel_id=1, source_target_pairs={{0,3},{1,0},{2,1},{3,2},{4,7},{5,4},{6,5},{7,6},{8,11},{9,8},{10,9... | collective-permute-start | bytes 12296 | tf_op jit(solution)/shard_map/ppermute | solution.py:694
  59.9 1.2 %collective-permute-done.17 = f32[8,128]{1,0:T(8,128)S(1)} collective-permute-done((f32[8,128]{1,0:T(8,128)S(1)}, f32[8,128]{1,0:T(8,128)S(1)}, u32[]{:S(2)}, u32[]{:S(2)}) %collective-permute-start.17) | collective-permute-done | bytes 4128 | tf_op jit(solution)/shard_map/ppermute | solution.py:704
  61.1 2.1 %collective-permute-start.18 = (f32[8,128]{1,0:T(8,128)S(1)}, f32[8,128]{1,0:T(8,128)S(1)}, u32[]{:S(2)}, u32[]{:S(2)}) collective-permute-start(f32[8,128]{1,0:T(8,128)S(1)} %add.36), channel_id=1, source_target_pairs={{0,16},{4,20},{8,24},{12,28},{16,0},{20,4},{24,8},{28,12},{1,17},{... | collective-permute-start | bytes 12296 | tf_op jit(solution)/shard_map/ppermute | solution.py:694
  63.2 3.2 %collective-permute-start.20 = (f32[8,128]{1,0:T(8,128)S(1)}, f32[8,128]{1,0:T(8,128)S(1)}, u32[]{:S(2)}, u32[]{:S(2)}) collective-permute-start(f32[8,128]{1,0:T(8,128)S(1)} %add.36), channel_id=1, source_target_pairs={{0,24},{4,28},{8,0},{12,4},{16,8},{20,12},{24,16},{28,20},{1,25},{... | collective-permute-start | bytes 12296 | tf_op jit(solution)/shard_map/ppermute | solution.py:694
  68.1 5.2 %shard_map.58 = (f32[8,16,32,128]{3,2,1,0:T(8,128)}, f32[8,16,32,128]{3,2,1,0:T(8,128)}) custom-call(f32[8,128]{1,0:T(8,128)S(1)} %add_add_fusion.refs_0_, f32[8,16,32,128]{3,2,1,0:T(8,128)S(1)} %get-tuple-element.55.refs_0_.refs_1_, f32[8,16,32,128]{3,2,1,0:T(8,128)S(1)} %get-tuple-element.70.refs_0_.refs_7_.refs_1_.refs_2_, ...), custom_call_target="tpu_custom_call" | custom-call | tf_op jit(solution)/shard_map/pallas_call | solution.py:38
  (44 shorter events, 12.9 us)
Async XLA Ops:
  0.6 7.4 %copy-start = (f32[14,16,32,128]{3,2,1,0:T(8,128)S(1)}, f32[14,16,32,128]{3,2,1,0:T(8,128)}, u32[]{:S(2)}) copy-start(f32[14,16,32,128]{3,2,1,0:T(8,128)} %refs_1_.7) | copy-start | bytes 11010052
  3.7 6.3 %collective-permute-start = (f32[9,8,128]{2,1,0:T(8,128)S(1)}, f32[9,8,128]{2,1,0:T(8,128)S(1)}, u32[]{:S(2)}, u32[]{:S(2)}) collective-permute-start(f32[9,8,128]{2,1,0:T(8,128)S(1)} %get-tuple-element.45), channel_id=1, source_target_pairs={{0,1},{1,2},{2,3},{3,0},{4,5},{5,6},{6,7},{7,4},{8,9},{9,10},{10,1... | collective-permute-start | bytes 110600 | tf_op jit(solution)/shard_map/ppermute | solution.py:694
  5.8 4.2 %collective-permute-start.1 = (f32[9,8,128]{2,1,0:T(8,128)S(1)}, f32[9,8,128]{2,1,0:T(8,128)S(1)}, u32[]{:S(2)}, u32[]{:S(2)}) collective-permute-start(f32[9,8,128]{2,1,0:T(8,128)S(1)} %get-tuple-element.46), channel_id=1, source_target_pairs={{0,3},{1,0},{2,1},{3,2},{4,7},{5,4},{6,5},{7,6},{8,11},{9,8},{10,9... | collective-permute-start | bytes 110600 | tf_op jit(solution)/shard_map/ppermute | solution.py:694
  10.2 5.8 %collective-permute-start.2 = (f32[36,8,128]{2,1,0:T(8,128)S(1)}, f32[36,8,128]{2,1,0:T(8,128)S(1)}, u32[]{:S(2)}, u32[]{:S(2)}) collective-permute-start(f32[36,8,128]{2,1,0:T(8,128)S(1)} %get-tuple-element.47.refs_6_.refs_1_), channel_id=1, source_target_pairs={{0,4},{4,8},{8,12},{12,16},{16,20},{20,24},{24,28},{28,0},{1,5},{5... | collective-permute-start | bytes 442376 | tf_op jit(solution)/shard_map/ppermute | solution.py:694
  10.2 5.7 %collective-permute-start.3 = (f32[30,8,128]{2,1,0:T(8,128)S(1)}, f32[30,8,128]{2,1,0:T(8,128)S(1)}, u32[]{:S(2)}, u32[]{:S(2)}) collective-permute-start(f32[30,8,128]{2,1,0:T(8,128)S(1)} %get-tuple-element.54), channel_id=1, source_target_pairs={{0,28},{4,0},{8,4},{12,8},{16,12},{20,16},{24,20},{28,24},{1,29},{... | collective-permute-start | bytes 368648 | tf_op jit(solution)/shard_map/ppermute | solution.py:694
  16.2 9.9 %collective-permute-start.4 = (f32[40,8,128]{2,1,0:T(8,128)S(1)}, f32[40,8,128]{2,1,0:T(8,128)S(1)}, u32[]{:S(2)}, u32[]{:S(2)}) collective-permute-start(f32[40,8,128]{2,1,0:T(8,128)S(1)} %get-tuple-element.57), channel_id=1, source_target_pairs={{0,96},{32,0},{64,32},{96,64},{1,97},{33,1},{65,33},{97,65},{2,98}... | collective-permute-start | bytes 491528 | tf_op jit(solution)/shard_map/ppermute | solution.py:694
  19.3 6.8 %collective-permute-start.5 = (f32[36,8,128]{2,1,0:T(8,128)S(1)}, f32[36,8,128]{2,1,0:T(8,128)S(1)}, u32[]{:S(2)}, u32[]{:S(2)}) collective-permute-start(f32[36,8,128]{2,1,0:T(8,128)S(1)} %get-tuple-element.58), channel_id=1, source_target_pairs={{0,32},{32,64},{64,96},{96,0},{1,33},{33,65},{65,97},{97,1},{2,34}... | collective-permute-start | bytes 442376 | tf_op jit(solution)/shard_map/ppermute | solution.py:694
  26.9 5.7 %collective-permute-start.6 = (f32[4,8,128]{2,1,0:T(8,128)S(1)}, f32[4,8,128]{2,1,0:T(8,128)S(1)}, u32[]{:S(2)}, u32[]{:S(2)}) collective-permute-start(f32[4,8,128]{2,1,0:T(8,128)S(1)} %get-tuple-element.62.refs_3_), channel_id=1, source_target_pairs={{0,1},{1,2},{2,3},{3,0},{4,5},{5,6},{6,7},{7,4},{8,9},{9,10},{10,1... | collective-permute-start | bytes 49160 | tf_op jit(solution)/shard_map/ppermute | solution.py:694
  28.7 4.0 %collective-permute-start.7 = (f32[4,8,128]{2,1,0:T(8,128)S(1)}, f32[4,8,128]{2,1,0:T(8,128)S(1)}, u32[]{:S(2)}, u32[]{:S(2)}) collective-permute-start(f32[4,8,128]{2,1,0:T(8,128)S(1)} %get-tuple-element.63), channel_id=1, source_target_pairs={{0,3},{1,0},{2,1},{3,2},{4,7},{5,4},{6,5},{7,6},{8,11},{9,8},{10,9... | collective-permute-start | bytes 49160 | tf_op jit(solution)/shard_map/ppermute | solution.py:694
  32.8 5.3 %collective-permute-start.8 = (f32[24,8,128]{2,1,0:T(8,128)S(1)}, f32[24,8,128]{2,1,0:T(8,128)S(1)}, u32[]{:S(2)}, u32[]{:S(2)}) collective-permute-start(f32[24,8,128]{2,1,0:T(8,128)S(1)} %get-tuple-element.65.refs_4_.refs_2_), channel_id=1, source_target_pairs={{0,4},{4,8},{8,12},{12,16},{16,20},{20,24},{24,28},{28,0},{1,5},{5... | collective-permute-start | bytes 294920 | tf_op jit(solution)/shard_map/ppermute | solution.py:694
  32.8 5.2 %collective-permute-start.9 = (f32[24,8,128]{2,1,0:T(8,128)S(1)}, f32[24,8,128]{2,1,0:T(8,128)S(1)}, u32[]{:S(2)}, u32[]{:S(2)}) collective-permute-start(f32[24,8,128]{2,1,0:T(8,128)S(1)} %get-tuple-element.69), channel_id=1, source_target_pairs={{0,28},{4,0},{8,4},{12,8},{16,12},{20,16},{24,20},{28,24},{1,29},{... | collective-permute-start | bytes 294920 | tf_op jit(solution)/shard_map/ppermute | solution.py:694
  38.2 6.3 %collective-permute-start.10 = (f32[40,8,128]{2,1,0:T(8,128)S(1)}, f32[40,8,128]{2,1,0:T(8,128)S(1)}, u32[]{:S(2)}, u32[]{:S(2)}) collective-permute-start(f32[40,8,128]{2,1,0:T(8,128)S(1)} %get-tuple-element.74), channel_id=1, source_target_pairs={{0,96},{32,0},{64,32},{96,64},{1,97},{33,1},{65,33},{97,65},{2,98}... | collective-permute-start | bytes 491528 | tf_op jit(solution)/shard_map/ppermute | solution.py:694
  46.0 5.2 %collective-permute-start.11 = (f32[8,128]{1,0:T(8,128)S(1)}, f32[8,128]{1,0:T(8,128)S(1)}, u32[]{:S(2)}, u32[]{:S(2)}) collective-permute-start(f32[8,128]{1,0:T(8,128)S(1)} %get-tuple-element.76), channel_id=1, source_target_pairs={{0,64},{32,96},{64,0},{96,32},{1,65},{33,97},{65,1},{97,33},{2,66}... | collective-permute-start | bytes 12296 | tf_op jit(solution)/shard_map/ppermute | solution.py:694
  46.3 4.9 %collective-permute-start.12 = (f32[8,128]{1,0:T(8,128)S(1)}, f32[8,128]{1,0:T(8,128)S(1)}, u32[]{:S(2)}, u32[]{:S(2)}) collective-permute-start(f32[8,128]{1,0:T(8,128)S(1)} %get-tuple-element.76), channel_id=1, source_target_pairs={{0,32},{32,64},{64,96},{96,0},{1,33},{33,65},{65,97},{97,1},{2,34}... | collective-permute-start | bytes 12296 | tf_op jit(solution)/shard_map/ppermute | solution.py:694
  48.7 3.6 %collective-permute-start.13 = (f32[8,128]{1,0:T(8,128)S(1)}, f32[8,128]{1,0:T(8,128)S(1)}, u32[]{:S(2)}, u32[]{:S(2)}) collective-permute-start(f32[8,128]{1,0:T(8,128)S(1)} %get-tuple-element.76), channel_id=1, source_target_pairs={{0,96},{32,0},{64,32},{96,64},{1,97},{33,1},{65,33},{97,65},{2,98}... | collective-permute-start | bytes 12296 | tf_op jit(solution)/shard_map/ppermute | solution.py:694
  52.3 6.9 %collective-permute-start.14 = (f32[8,128]{1,0:T(8,128)S(1)}, f32[8,128]{1,0:T(8,128)S(1)}, u32[]{:S(2)}, u32[]{:S(2)}) collective-permute-start(f32[8,128]{1,0:T(8,128)S(1)} %add_add_fusion.2), channel_id=1, source_target_pairs={{0,2},{1,3},{2,0},{3,1},{4,6},{5,7},{6,4},{7,5},{8,10},{9,11},{10,... | collective-permute-start | bytes 12296 | tf_op jit(solution)/shard_map/ppermute | solution.py:694
  55.0 4.8 %collective-permute-start.15 = (f32[8,128]{1,0:T(8,128)S(1)}, f32[8,128]{1,0:T(8,128)S(1)}, u32[]{:S(2)}, u32[]{:S(2)}) collective-permute-start(f32[8,128]{1,0:T(8,128)S(1)} %add_add_fusion.2), channel_id=1, source_target_pairs={{0,1},{1,2},{2,3},{3,0},{4,5},{5,6},{6,7},{7,4},{8,9},{9,10},{10,1... | collective-permute-start | bytes 12296 | tf_op jit(solution)/shard_map/ppermute | solution.py:694
  55.7 4.1 %collective-permute-start.16 = (f32[8,128]{1,0:T(8,128)S(1)}, f32[8,128]{1,0:T(8,128)S(1)}, u32[]{:S(2)}, u32[]{:S(2)}) collective-permute-start(f32[8,128]{1,0:T(8,128)S(1)} %add_add_fusion.2), channel_id=1, source_target_pairs={{0,3},{1,0},{2,1},{3,2},{4,7},{5,4},{6,5},{7,6},{8,11},{9,8},{10,9... | collective-permute-start | bytes 12296 | tf_op jit(solution)/shard_map/ppermute | solution.py:694
  58.2 8.2 %collective-permute-start.21 = (f32[32,8,128]{2,1,0:T(8,128)S(1)}, f32[32,8,128]{2,1,0:T(8,128)S(1)}, u32[]{:S(2)}, u32[]{:S(2)}) collective-permute-start(f32[32,8,128]{2,1,0:T(8,128)S(1)} %get-tuple-element.75.refs_6_), channel_id=1, source_target_pairs={{0,32},{32,64},{64,96},{96,0},{1,33},{33,65},{65,97},{97,1},{2,34}... | collective-permute-start | bytes 393224 | tf_op jit(solution)/shard_map/ppermute | solution.py:694
  59.8 1.2 %collective-permute-start.17 = (f32[8,128]{1,0:T(8,128)S(1)}, f32[8,128]{1,0:T(8,128)S(1)}, u32[]{:S(2)}, u32[]{:S(2)}) collective-permute-start(f32[8,128]{1,0:T(8,128)S(1)} %add_add_fusion.1), channel_id=1, source_target_pairs={{0,4},{4,0},{8,12},{12,8},{16,20},{20,16},{24,28},{28,24},{1,5},{5... | collective-permute-start | bytes 12296 | tf_op jit(solution)/shard_map/ppermute | solution.py:704
  61.1 5.8 %collective-permute-start.18 = (f32[8,128]{1,0:T(8,128)S(1)}, f32[8,128]{1,0:T(8,128)S(1)}, u32[]{:S(2)}, u32[]{:S(2)}) collective-permute-start(f32[8,128]{1,0:T(8,128)S(1)} %add.36), channel_id=1, source_target_pairs={{0,16},{4,20},{8,24},{12,28},{16,0},{20,4},{24,8},{28,12},{1,17},{... | collective-permute-start | bytes 12296 | tf_op jit(solution)/shard_map/ppermute | solution.py:694
  63.2 4.8 %collective-permute-start.19 = (f32[8,128]{1,0:T(8,128)S(1)}, f32[8,128]{1,0:T(8,128)S(1)}, u32[]{:S(2)}, u32[]{:S(2)}) collective-permute-start(f32[8,128]{1,0:T(8,128)S(1)} %add.36), channel_id=1, source_target_pairs={{0,8},{4,12},{8,16},{12,20},{16,24},{20,28},{24,0},{28,4},{1,9},{5... | collective-permute-start | bytes 12296 | tf_op jit(solution)/shard_map/ppermute | solution.py:694
  63.2 4.8 %collective-permute-start.20 = (f32[8,128]{1,0:T(8,128)S(1)}, f32[8,128]{1,0:T(8,128)S(1)}, u32[]{:S(2)}, u32[]{:S(2)}) collective-permute-start(f32[8,128]{1,0:T(8,128)S(1)} %add.36), channel_id=1, source_target_pairs={{0,24},{4,28},{8,0},{12,4},{16,8},{20,12},{24,16},{28,20},{1,25},{... | collective-permute-start | bytes 12296 | tf_op jit(solution)/shard_map/ppermute | solution.py:694
